TPU v7x, 32 devices: a whole 2x2x4 slice. The times are simulated.
32 devices in a mesh: slab: 8 (over z, y), sub: 4 (over x, core).
Axes of the slice: x: 2, y: 2, z: 4, core: 2. Of those that a mesh axis runs over, the one named last changes fastest.
Arguments:
- orbitals: bfloat16 [32, 16, 110592], P(('slab', 'sub')), may hold values from -0.25 to 0.25
- occupations: int32 [32, 16], P(('slab', 'sub')), may hold values from 0 to 2, as said below
- patch_sign: int32 [32], P(('slab', 'sub')), may hold values from -1 to 1, as said below
- corners: int32 [32, 3], replicated, may hold values from 0 to 255, as said below
- core_span: int32 [32, 6], P(('slab', 'sub')), may hold values from 8 to 32, as said below
- outer_density: float32 [32, 256, 256], P('slab', 'sub'), may hold values from 0 to 0.3, as said below
Outputs:
- box_potential: float32 [32, 110592], P(('slab', 'sub'))
- potential: float32 [32, 256, 256], P('slab', 'sub')
Inputs may be any that keep to these rules, and one draw needn't show every extreme that they name: Each fragment's occupations sum to 16. patch_sign[f] is -1 raised to the number of dimensions along which fragment f's core is 16 cells long. corners[f, 0] lies in [4 * (f // 4), that + 4), the planes of the slab index that holds fragment f; corners[f, 1] lies in [0, 256) and corners[f, 2] in [0, 256). `core_span`: each core lies inside its box and is 16 or 32 cells long along each dimension; fragments 8 j to 8 j + 7 are the eight kinds of core that start at one common grid cell, a corner of the fragment division; along the second and third dimensions these corners lie at different points of one lattice of spacing 16. `outer_density`: nonnegative; zero exactly on the cells where the fragments given here have signed coverage one.
All inputs are finite; a program needn't handle non-finite values.
Results may differ from a plain program's by a relative error of at most 0.0003.
Values sent between devices are 32-bit elements; how exact they have to be, the bound alone decides.
No kernel may reach another device: no remote copies, remote signals or barrier semaphores. Data moves between devices by JAX's collectives and lax.ppermute only.
A program may use at most 64 MiB of HBM per device.

v0:
```python
import math

import jax
import jax.numpy as jnp
import numpy as np
from jax import lax
from jax.experimental import pallas as pl
from jax.experimental.pallas import tpu as pltpu
from jax.sharding import PartitionSpec as P

BOX = 48
CORE = 32
PLANE = BOX * BOX
GROUPS = 6
WIDE = PLANE // GROUPS
PACK = CORE * CORE
LANES = 128
PIECE = PACK + LANES
KINDS = 8

spacing = 0.35
floor_density = 0.001

AXES = ("slab", "sub")


def exchange_correlation(density):
    clipped = jnp.maximum(density, floor_density)
    radius = jnp.cbrt(3.0 / (4.0 * math.pi * clipped))
    exchange = -jnp.cbrt(3.0 * clipped / math.pi)
    correlation = -0.44 / (radius + 7.8) - 0.44 * radius / (3.0 * (radius + 7.8) ** 2)
    return exchange + correlation


def split_table(table):
    high = table.astype(np.float32).astype(jnp.bfloat16)
    low = (table - high.astype(np.float64)).astype(np.float32).astype(jnp.bfloat16)
    return np.stack([high, low])


def hartley(count, repeat=1):
    index = np.arange(count)
    angle = 2.0 * np.pi / count * (np.outer(index, index) % count)
    return split_table(np.kron(np.cos(angle) + np.sin(angle), np.eye(repeat)))


def parts(values):
    high = values.astype(jnp.bfloat16)
    low = (values - high.astype(jnp.float32)).astype(jnp.bfloat16)
    return high, low


def product(a, b):
    return jnp.dot(a, b, preferred_element_type=jnp.float32)


def table_times(table, values):
    high, low = parts(values)
    return product(table[0], high) + (product(table[0], low) + product(table[1], high))


def times_table(values, table):
    high, low = parts(values)
    return product(high, table[0]) + (product(high, table[1]) + product(low, table[0]))


def core_kernel(place, weights, orbitals, out, sums, rows):
    depth, base, slots = place[0], place[1], out.shape[0]
    first_z, first_x, first_y = place[2], place[3], place[4]
    len_z, len_x, len_y = place[5], place[6], place[7]
    start_z, start_x, start_y = place[8], place[9], place[10]
    weight = weights[...]

    def add_plane(p, carry):
        i = jnp.minimum(first_z + p, BOX - 1)
        values = orbitals[0, :, pl.ds(pl.multiple_of(i * PLANE, LANES), PLANE)].astype(jnp.float32)
        total = jnp.sum(values * values * weight, axis=0, keepdims=True)
        for g in range(GROUPS):
            sums[pl.ds(p * GROUPS + g, 1), :] = total[:, g * WIDE : (g + 1) * WIDE]
        return carry

    lax.fori_loop(0, CORE, add_plane, 0)
    count = CORE * GROUPS
    for r in range(8):
        rows[pl.ds(r, count, stride=8), 0:BOX] = sums[:, r * BOX : (r + 1) * BOX]

    row = lax.broadcasted_iota(jnp.int32, (8, LANES), 0)
    lane = lax.broadcasted_iota(jnp.int32, (8, LANES), 1)

    def pack(k, carry):
        p = lax.rem(base + k - start_z + 2 * depth, depth)
        held = p < len_z
        p = jnp.minimum(p, CORE - 1)
        cells = rows[pl.ds(p * BOX + first_x, CORE), :]
        packed = jnp.zeros((8, LANES), jnp.float32)
        for q in range(4):
            turned = pltpu.roll(cells[8 * q : 8 * q + 8], lax.rem(32 * q - first_y + LANES, LANES), 1)
            keep = (row + 8 * q < len_x) & (lane >= 32 * q) & (lane < 32 * q + len_y) & held
            packed = jnp.where(keep, turned, packed)
        for s in range(8):
            out[k, :, s * LANES : (s + 1) * LANES] = packed[s : s + 1]
        first = jnp.where(lane[0:1] == 0, start_x, start_y)
        out[k, :, PACK:PIECE] = first.astype(jnp.float32)
        return carry

    lax.fori_loop(0, slots, pack, 0)


def core_pieces(orbitals, weights, place, slots):
    return pl.pallas_call(
        core_kernel,
        out_shape=jax.ShapeDtypeStruct((slots, 1, PIECE), jnp.float32),
        in_specs=[
            pl.BlockSpec(memory_space=pltpu.SMEM),
            pl.BlockSpec(memory_space=pltpu.VMEM),
            pl.BlockSpec(memory_space=pltpu.VMEM),
        ],
        out_specs=pl.BlockSpec(memory_space=pltpu.VMEM),
        scratch_shapes=[
            pltpu.VMEM((CORE * GROUPS, WIDE), jnp.float32),
            pltpu.VMEM((CORE * BOX + CORE, LANES), jnp.float32),
        ],
        cost_estimate=pl.CostEstimate(flops=40_000_000, bytes_accessed=4_000_000, transcendentals=0),
        name="core_pieces",
    )(place, weights, orbitals)


def plane_kernel(group, pieces, outer, table_x, table_y, spectrum, density, packed):
    slots = pieces.shape[0]
    count_x, count_y = outer.shape
    groups = slots // group
    column = lax.broadcasted_iota(jnp.int32, (count_x, CORE), 1)
    cell_x = lax.broadcasted_iota(jnp.int32, (count_x, CORE), 0)
    row = lax.broadcasted_iota(jnp.int32, (CORE, count_y), 0)
    cell_y = lax.broadcasted_iota(jnp.int32, (CORE, count_y), 1)
    lefts, rights = [], []
    for j in range(groups):
        total = pieces[j * group, :, 0:PACK]
        for m in range(1, group):
            total = total + pieces[j * group + m, :, 0:PACK]
        for s in range(8):
            packed[8 * j + s : 8 * j + s + 1, :] = total[:, s * LANES : (s + 1) * LANES]
        tile = packed[8 * j : 8 * j + 8, :]
        square = jnp.concatenate([tile[:, 32 * q : 32 * q + 32] for q in range(4)], axis=0)
        first = pieces[j * group, :, PACK : PACK + LANES].astype(jnp.int32)
        away_x = cell_x - first[:, 0:1]
        away_y = cell_y - first[:, 1:2]
        left = jnp.where(away_x < 0, away_x + count_x, away_x) == column
        right = jnp.where(away_y < 0, away_y + count_y, away_y) == row
        right = jnp.where(right, 1.0, 0.0).astype(jnp.bfloat16)
        high = square.astype(jnp.bfloat16)
        rest = square - high.astype(jnp.float32)
        middle = rest.astype(jnp.bfloat16)
        low = (rest - middle.astype(jnp.float32)).astype(jnp.bfloat16)
        lefts.append(jnp.where(left, 1.0, 0.0).astype(jnp.bfloat16))
        rights.append([product(part, right).astype(jnp.bfloat16) for part in (high, middle, low)])
    left = jnp.concatenate(lefts, axis=1)
    placed = outer[...]
    for part in range(2, -1, -1):
        placed = placed + product(left, jnp.concatenate([r[part] for r in rights], axis=0))
    density[...] = placed
    spectrum[...] = times_table(table_times(table_x, placed), table_y)


def plane_spectrum(pieces, group, outer, table_x, table_y):
    shape = jax.ShapeDtypeStruct(outer.shape, jnp.float32)
    return pl.pallas_call(
        lambda *refs: plane_kernel(group, *refs),
        out_shape=(shape, shape),
        in_specs=[pl.BlockSpec(memory_space=pltpu.VMEM)] * 4,
        out_specs=(pl.BlockSpec(memory_space=pltpu.VMEM),) * 2,
        scratch_shapes=[pltpu.VMEM((8 * (pieces.shape[0] // group), LANES), jnp.float32)],
        name="plane_spectrum",
    )(pieces, outer, table_x, table_y)


def wave_squares(index, count):
    folded = jnp.where(index > count // 2, index - count, index)
    wave = 2.0 * math.pi / (count * spacing) * folded.astype(jnp.float32)
    return wave * wave


def column_kernel(count_z, count_x, count_y, device, values, table, out):
    rows, lanes = values.shape
    deep = rows // count_z
    transformed = table_times(table, values[...])
    row = lax.broadcasted_iota(jnp.int32, (rows, lanes), 0)
    lane = lax.broadcasted_iota(jnp.int32, (rows, lanes), 1)
    cell = (device[0] * deep + row % deep) * lanes + lane
    square = (
        wave_squares(row // deep, count_z)
        + wave_squares(cell // count_y, count_x)
        + wave_squares(cell % count_y, count_y)
    )
    scale = 4.0 * math.pi / float(count_z * count_x * count_y)
    kernel = jnp.where(square > 0, scale / jnp.where(square > 0, square, 1.0), 0.0)
    out[...] = table_times(table, transformed * kernel)


def column_hartree(values, table, device, counts):
    return pl.pallas_call(
        lambda *refs: column_kernel(*counts, *refs),
        out_shape=jax.ShapeDtypeStruct(values.shape, jnp.float32),
        in_specs=[
            pl.BlockSpec(memory_space=pltpu.SMEM),
            pl.BlockSpec(memory_space=pltpu.VMEM),
            pl.BlockSpec(memory_space=pltpu.VMEM),
        ],
        out_specs=pl.BlockSpec(memory_space=pltpu.VMEM),
        name="column_hartree",
    )(device, values, table)


def window_kernel(corners, spectrum, exchange, table_x, table_y, potential, out, wide, cut):
    slots = out.shape[0]
    count_x, count_y = spectrum.shape
    plane = times_table(table_times(table_x, spectrum[...]), table_y) + exchange[...]
    potential[...] = plane
    tall = count_x + BOX
    tiles = count_y // LANES
    for t in range(tiles):
        part = plane[:, t * LANES : (t + 1) * LANES]
        wide[t * tall : t * tall + count_x, :] = part
        wide[t * tall + count_x : (t + 1) * tall, :] = part[0:BOX]
    lane = lax.broadcasted_iota(jnp.int32, (BOX, LANES), 1)

    def cut_window(k, carry):
        x, y = corners[k, 0], corners[k, 1]
        tile = y // LANES
        over = y - tile * LANES
        near = wide[pl.ds(tile * tall + x, BOX), :]
        far = wide[pl.ds(lax.rem(tile + 1, tiles) * tall + x, BOX), :]
        turned = pltpu.roll(jnp.where(lane < over, far, near), lax.rem(LANES - over, LANES), 1)
        cut[pl.ds(pl.multiple_of(k * BOX, 8), BOX), :] = turned
        return carry

    lax.fori_loop(0, slots, cut_window, 0)
    count = slots * GROUPS
    flat = jnp.concatenate(
        [cut[pl.ds(r, count, stride=8), :][:, 0:BOX] for r in range(8)], axis=1
    )
    for k in range(slots):
        for g in range(GROUPS):
            out[k, :, g * WIDE : (g + 1) * WIDE] = flat[k * GROUPS + g : k * GROUPS + g + 1, :]


def plane_windows(spectrum, exchange, table_x, table_y, corners):
    slots = corners.shape[0]
    count_x, count_y = spectrum.shape
    return pl.pallas_call(
        window_kernel,
        out_shape=(
            jax.ShapeDtypeStruct(spectrum.shape, jnp.float32),
            jax.ShapeDtypeStruct((slots, 1, PLANE), jnp.float32),
        ),
        in_specs=[pl.BlockSpec(memory_space=pltpu.SMEM)]
        + [pl.BlockSpec(memory_space=pltpu.VMEM)] * 4,
        out_specs=(pl.BlockSpec(memory_space=pltpu.VMEM),) * 2,
        scratch_shapes=[
            pltpu.VMEM((count_y // LANES * (count_x + BOX), LANES), jnp.float32),
            pltpu.VMEM((slots * BOX, LANES), jnp.float32),
        ],
        name="plane_windows",
    )(corners, spectrum, exchange, table_x, table_y)


def box_kernel(first, windows, out):
    depth = windows.shape[0]

    def copy_plane(i, carry):
        z = lax.rem(first[0] + i, depth)
        out[i] = windows[z]
        return carry

    lax.fori_loop(0, BOX, copy_plane, 0)


def box_planes(windows, first):
    return pl.pallas_call(
        box_kernel,
        out_shape=jax.ShapeDtypeStruct((BOX, 1, PLANE), jnp.float32),
        in_specs=[pl.BlockSpec(memory_space=pltpu.SMEM), pl.BlockSpec(memory_space=pltpu.VMEM)],
        out_specs=pl.BlockSpec(memory_space=pltpu.VMEM),
        name="box_planes",
    )(first, windows)


def body(orbitals, occupations, patch_sign, corners, core_span, outer_density):
    slab_count = lax.axis_size("slab")
    sub_count = lax.axis_size("sub")
    devices = slab_count * sub_count
    z_dev, x_dev, count_y = outer_density.shape
    count_x = x_dev * sub_count
    count_z = z_dev * slab_count
    device = lax.axis_index("slab") * sub_count + lax.axis_index("sub")
    table_x = hartley(count_x)
    table_y = hartley(count_y)
    per_device = count_x * count_y // devices
    deep = max(1, per_device // count_y)
    table_z = hartley(count_z, deep)

    own = lax.dynamic_index_in_dim(corners, device, 0, False)
    span = core_span[0]
    start = (own + span[:3]) % jnp.array([count_z, count_x, count_y], jnp.int32)
    place = jnp.concatenate([jnp.array([count_z, 0], jnp.int32), span, start])
    weights = (occupations[0] * patch_sign[0]).astype(jnp.float32)
    weights = jnp.broadcast_to(weights[:, None], (weights.shape[0], 1))

    outer = lax.all_to_all(outer_density, "sub", 0, 0, tiled=True).reshape(count_x, count_y)
    pieces = core_pieces(orbitals, weights, place, devices)
    pieces = lax.all_to_all(pieces, AXES, 0, 0, tiled=True)
    spectrum, density = plane_spectrum(pieces, KINDS, outer, table_x, table_y)
    chunk = (devices, deep, per_device // deep)
    spectrum = lax.all_to_all(spectrum.reshape(chunk), AXES, 0, 0, tiled=True)
    exchange = exchange_correlation(density)
    spectrum = column_hartree(
        spectrum.reshape(devices * deep, per_device // deep),
        table_z,
        jnp.reshape(device, (1,)),
        (count_z, count_x, count_y),
    )
    spectrum = lax.all_to_all(spectrum.reshape(chunk), AXES, 0, 0, tiled=True)
    potential, windows = plane_windows(
        spectrum.reshape(count_x, count_y), exchange, table_x, table_y, corners[:, 1:3]
    )
    windows = lax.all_to_all(windows, AXES, 0, 0, tiled=True)
    potential = lax.all_to_all(potential.reshape(z_dev, x_dev, count_y), "sub", 0, 0, tiled=True)
    box = box_planes(windows, own[0:1])
    return (box.reshape(1, BOX * PLANE), potential)


def solution(mesh):
    placed = (
        P(("slab", "sub"), None, None),
        P(("slab", "sub"), None),
        P(("slab", "sub")),
        P(),
        P(("slab", "sub"), None),
        P("slab", "sub", None),
    )
    return jax.shard_map(
        body,
        mesh=mesh,
        in_specs=placed,
        out_specs=(P(("slab", "sub"), None), P("slab", "sub", None)),
        check_vma=False,
    )
```

profile of v0, /device:TPU:0, one launch (start us, length us, event | category | flops | bytes accessed | tf_op | source)
XLA Modules:
  0.0 100.6 jit_solution(17097737944963159813)
XLA Ops:
  0.6 4.2 %all-to-all-start.1 = ((f32[4,64,256]{2,1,0:T(8,128)}), f32[4,64,256]{2,1,0:T(8,128)S(1)}, u32[]{:S(2)}, u32[]{:S(2)}) async-start(f32[4,64,256]{2,1,0:T(8,128)} %param.16), calls=%async_computation.1 | async-start | bytes 524288 | tf_op jit(solution)/shard_map/all_to_all | solution.py:309
  4.9 0.0 copy-start.3
  5.5 0.8 constant_dynamic-slice_fusion
  6.3 0.1 copy.16
  6.4 0.0 copy-start.2
  6.4 0.8 and_select_fusion
  7.2 0.7 convert_bitcast_fusion
  7.9 0.7 copy.15.weights
  8.6 1.3 %pad_add_fusion.place = s32[11]{0:T(128)} fusion(s32[3]{0:T(128)S(1)} %and_select_fusion, s32[6]{0:T(128)} %bitcast.25, s32[2]{0:T(128)} %constant.47.clone), kind=kLoop, calls=%fused_computation.2 | loop fusion | flops 22 | bytes 88 | tf_op jit(solution)/shard_map/concatenate | solution.py:305
  9.9 9.1 %core_pieces.1 = f32[32,1,1152]{2,1,0:T(1,128)} custom-call(s32[11]{0:T(128)} %pad_add_fusion.place, f32[16,1]{1,0:T(8,128)} %copy.15.weights, bf16[1,16,110592]{2,1,0:T(8,128)(2,1)} %orbitals.1), custom_call_target="tpu_custom_call" | custom-call | flops 40000000 | bytes 4000000 | tf_op jit(solution)/shard_map/core_pieces/pallas_call | solution.py:110
  18.9 0.0 all-to-all-done.1
  19.0 0.0 copy-start
  19.0 15.5 %all_to_all.30.refs_0_ = f32[32,1,1152]{2,1,0:T(1,128)} all-to-all(f32[32,1,1152]{2,1,0:T(1,128)} %core_pieces.1), channel_id=1, replica_groups=mesh['slab'=8,'sub'=4] {'slab','sub'}, dimensions={0} | all-to-all | bytes 294912 | tf_op jit(solution)/shard_map/all_to_all | solution.py:311
  34.5 0.0 copy-done
  34.5 3.0 %plane_spectrum.1 = (f32[256,256]{1,0:T(8,128)}, f32[256,256]{1,0:T(8,128)}) custom-call(f32[32,1,1152]{2,1,0:T(1,128)} %all_to_all.30.refs_0_, f32[256,256]{1,0:T(8,128)} %bitcast.17, bf16[2,256,256]{2,1,0:T(8,128)(2,1)} %constant.48.clone.refs_2_.refs_3_.table_x.table_y, bf16[2,256,256]{2,1,0:T(8,128)(2,1)} %constant.48.clone.refs_2_.refs_3_.table_x.table_y), custom_call_target="tpu_custom_call" | custom-call | tf_op jit(solution)/shard_map/plane_spectrum/pallas_call | solution.py:167
  37.5 13.9 %all_to_all.31 = f32[32,8,256]{2,1,0:T(8,128)} all-to-all(f32[32,8,256]{2,1,0:T(8,128)} %bitcast.23), channel_id=1, replica_groups=mesh['slab'=8,'sub'=4] {'slab','sub'}, dimensions={0} | all-to-all | bytes 524288 | tf_op jit(solution)/shard_map/all_to_all | solution.py:314
  51.3 2.7 %column_hartree.1 = f32[256,256]{1,0:T(8,128)} custom-call(s32[1]{0:T(128)} %bitcast.1.refs_0_, f32[256,256]{1,0:T(8,128)} %bitcast.20, bf16[2,256,256]{2,1,0:T(8,128)(2,1)} %constant.49.clone.refs_2_), custom_call_target="tpu_custom_call" | custom-call | tf_op jit(solution)/shard_map/column_hartree/pallas_call | solution.py:201
  54.0 2.6 %all-to-all-start.3 = ((f32[32,8,256]{2,1,0:T(8,128)}), f32[32,8,256]{2,1,0:T(8,128)S(1)}, u32[]{:S(2)}, u32[]{:S(2)}) async-start(f32[32,8,256]{2,1,0:T(8,128)} %bitcast.19), calls=%async_computation.3 | async-start | bytes 524288 | tf_op jit(solution)/shard_map/all_to_all | solution.py:322
  56.6 0.0 copy-done.3
  56.6 0.7 copy.17.corners
  57.3 2.2 %subtract_add_fusion.exchange = f32[256,256]{1,0:T(8,128)} fusion(f32[256,256]{1,0:T(8,128)} %get-tuple-element.7), kind=kLoop, calls=%fused_computation | loop fusion | flops 851968 | bytes 524288 | tf_op jit(solution)/shard_map/add | solution.py:32
  59.5 0.0 copy-done.2
  59.5 7.7 %all-to-all-done.3 = f32[32,8,256]{2,1,0:T(8,128)S(1)} async-done(((f32[32,8,256]{2,1,0:T(8,128)}), f32[32,8,256]{2,1,0:T(8,128)S(1)}, u32[]{:S(2)}, u32[]{:S(2)}) %all-to-all-start.3) | async-done | bytes 262176 | tf_op jit(solution)/shard_map/all_to_all | solution.py:322
  67.2 0.0 copy-start.1
  67.2 0.7 copy-done.1
  67.9 5.2 %plane_windows.1 = (f32[256,256]{1,0:T(8,128)}, f32[32,1,2304]{2,1,0:T(1,128)}) custom-call(s32[32,2]{1,0:T(8,128)} %copy.17.corners, f32[256,256]{1,0:T(8,128)} %bitcast.18, f32[256,256]{1,0:T(8,128)} %subtract_add_fusion.exchange, bf16[2,256,256]{2,1,0:T(8,128)(2,1)} %constant.48.clone.refs_2_.refs_3_.table_x.table_y, ...), custom_call_target="tpu_custom_call" | custom-call | tf_op jit(solution)/shard_map/plane_windows/pallas_call | solution.py:250
  73.1 9.4 %all_to_all.32 = f32[4,64,256]{2,1,0:T(8,128)S(1)} all-to-all(f32[4,64,256]{2,1,0:T(8,128)} %bitcast.22), channel_id=1, replica_groups=mesh['slab'=8,'sub'=4] {'sub'}, dimensions={0} | all-to-all | bytes 524288 | tf_op jit(solution)/shard_map/all_to_all | solution.py:327
  82.5 14.7 %all_to_all.33.windows = f32[32,1,2304]{2,1,0:T(1,128)} all-to-all(f32[32,1,2304]{2,1,0:T(1,128)} %get-tuple-element.8), channel_id=1, replica_groups=mesh['slab'=8,'sub'=4] {'slab','sub'}, dimensions={0} | all-to-all | bytes 589824 | tf_op jit(solution)/shard_map/all_to_all | solution.py:326
  97.2 2.7 %box_planes.1 = f32[48,1,2304]{2,1,0:T(1,128)} custom-call(s32[1]{0:T(128)} %bitcast.24, f32[32,1,2304]{2,1,0:T(1,128)} %all_to_all.33.windows), custom_call_target="tpu_custom_call" | custom-call | tf_op jit(solution)/shard_map/box_planes/pallas_call | solution.py:279
  99.9 0.7 copy.20
  (1 shorter events, 0.0 us)
Async XLA Ops:
  0.6 18.3 %all-to-all-start.1 = ((f32[4,64,256]{2,1,0:T(8,128)}), f32[4,64,256]{2,1,0:T(8,128)S(1)}, u32[]{:S(2)}, u32[]{:S(2)}) async-start(f32[4,64,256]{2,1,0:T(8,128)} %param.16), calls=%async_computation.1 | async-start | bytes 524288 | tf_op jit(solution)/shard_map/all_to_all | solution.py:309
  4.9 51.7 %copy-start.3 = (s32[32,3]{0,1:T(4,128)S(1)}, s32[32,3]{0,1:T(4,128)}, u32[]{:S(2)}) copy-start(s32[32,3]{0,1:T(4,128)} %param.14) | copy-start | bytes 1156
  6.4 53.1 %copy-start.2 = (s32[1,3]{1,0:T(1,128)}, s32[1,3]{1,0:T(1,128)S(1)}, u32[]{:S(2)}) copy-start(s32[1,3]{1,0:T(1,128)S(1)} %copy.16) | copy-start | bytes 40
  19.0 15.5 %copy-start = (f32[4,64,256]{2,1,0:T(8,128)}, f32[4,64,256]{2,1,0:T(8,128)S(1)}, u32[]{:S(2)}) copy-start(f32[4,64,256]{2,1,0:T(8,128)S(1)} %all-to-all-done.1) | copy-start | bytes 786436
  54.0 13.2 %all-to-all-start.3 = ((f32[32,8,256]{2,1,0:T(8,128)}), f32[32,8,256]{2,1,0:T(8,128)S(1)}, u32[]{:S(2)}, u32[]{:S(2)}) async-start(f32[32,8,256]{2,1,0:T(8,128)} %bitcast.19), calls=%async_computation.3 | async-start | bytes 524288 | tf_op jit(solution)/shard_map/all_to_all | solution.py:322
  67.2 0.7 copy-start.1
where the time goes:
time: 101 us
  blocking collectives  53.4 us (53%)
  Pallas kernels  22.7 us (22%)
  waiting for transfers between devices  7.67 us (8%)
  starting transfers between devices  6.83 us (7%)
  other arithmetic  4.98 us (5%)
  local copies, waits for them, and re-layouts  3.64 us (4%)
  between operations  1.33 us (1%)
    all_to_all x1, blocking collectives, body(): pieces = lax.all_to_all(pieces, AXES, 0, 0, tiled=True)  15.5 us
    all_to_all x1, blocking collectives, body(): windows = lax.all_to_all(windows, AXES, 0, 0, tiled=True)  14.7 us
    all_to_all x1, blocking collectives, body(): spectrum = lax.all_to_all(spectrum.reshape(chunk), AXES, 0, 0, tiled=True)  13.9 us
    all_to_all x1, blocking collectives, body(): lax.all_to_all(potential.reshape(z_dev, x_dev, count_y), 'sub', 0, 0, til...  9.38 us
    pallas_call x1, Pallas kernels, core_pieces(): pl.pallas_call(core_kernel, out_shape=jax.ShapeDtypeStruct((slots, 1, PIE...  9.08 us
    all_to_all x1, waiting for transfers between devices, body(): spectrum = lax.all_to_all(spectrum.reshape(chunk), AXES, 0, 0, tiled=True)  7.67 us
    pallas_call x1, Pallas kernels, plane_windows(): pl.pallas_call(window_kernel, out_shape=(jax.ShapeDtypeStruct(spectrum.sh...  5.23 us
    all_to_all x1, starting transfers between devices, body(): lax.all_to_all(outer_density, 'sub', 0, 0, tiled=True)  4.25 us
  transfers between devices with their start and end apart: 2, of which 1 were waited for; matrix products, arithmetic and copies ran while one was open for 7% of the time, Pallas kernels for 9%

commit v1 on v0

v1 whole, which is shorter than its diff:
```python
import math

import jax
import jax.numpy as jnp
import numpy as np
from jax import lax
from jax.experimental import pallas as pl
from jax.experimental.pallas import tpu as pltpu
from jax.sharding import PartitionSpec as P

BOX = 48
CORE = 32
PLANE = BOX * BOX
GROUPS = 6
WIDE = PLANE // GROUPS
PACK = CORE * CORE
LANES = 128
PIECE = PACK + LANES
KINDS = 8

spacing = 0.35
floor_density = 0.001

AXES = ("slab", "sub")


def exchange_correlation(density):
    clipped = jnp.maximum(density, floor_density)
    radius = jnp.cbrt(3.0 / (4.0 * math.pi * clipped))
    exchange = -jnp.cbrt(3.0 * clipped / math.pi)
    correlation = -0.44 / (radius + 7.8) - 0.44 * radius / (3.0 * (radius + 7.8) ** 2)
    return exchange + correlation


def split_table(table):
    high = table.astype(np.float32).astype(jnp.bfloat16)
    low = (table - high.astype(np.float64)).astype(np.float32).astype(jnp.bfloat16)
    return np.stack([high, low])


def hartley(count, repeat=1):
    index = np.arange(count)
    angle = 2.0 * np.pi / count * (np.outer(index, index) % count)
    return split_table(np.kron(np.cos(angle) + np.sin(angle), np.eye(repeat)))


def parts(values):
    high = values.astype(jnp.bfloat16)
    low = (values - high.astype(jnp.float32)).astype(jnp.bfloat16)
    return high, low


def product(a, b):
    return jnp.dot(a, b, preferred_element_type=jnp.float32)


def table_times(table, values):
    high, low = parts(values)
    return product(table[0], high) + (product(table[0], low) + product(table[1], high))


def times_table(values, table):
    high, low = parts(values)
    return product(high, table[0]) + (product(high, table[1]) + product(low, table[0]))


def small_call(kernel, name, megabytes, **kwargs):
    limit = pltpu.CompilerParams(vmem_limit_bytes=megabytes * 2**20)
    return pl.pallas_call(kernel, compiler_params=limit, name=name, **kwargs)


def in_vmem(count):
    return [pl.BlockSpec(memory_space=pltpu.VMEM)] * count


def in_smem(count):
    return [pl.BlockSpec(memory_space=pltpu.SMEM)] * count


def anywhere(count):
    return [pl.BlockSpec(memory_space=pl.ANY)] * count


def row_sums(tiles):
    row = lax.broadcasted_iota(jnp.int32, (8, LANES), 0)
    top = row < 4
    fours = [
        jnp.where(top, tiles[i], tiles[i + 4])
        + pltpu.roll(jnp.where(top, tiles[i + 4], tiles[i]), 4, 0)
        for i in range(4)
    ]
    for step in (2, 1):
        early = (row % (2 * step)) < step
        fours = [
            jnp.where(
                early,
                fours[i] + pltpu.roll(fours[i], 8 - step, 0),
                fours[i + step] + pltpu.roll(fours[i + step], step, 0),
            )
            for i in range(step)
        ]
    return fours[0]


CHUNK = 8
UNROLL = 4


def core_kernel(
    base, depth, count_x, count_y, device, corners, span, occupations, sign, orbitals, out,
    buffer, sums, rows, arrived,
):
    own, slots, orbital_count = device[0], out.shape[0], orbitals.shape[1]
    first_z, first_x, first_y = span[0, 0], span[0, 1], span[0, 2]
    len_z, len_x, len_y = span[0, 3], span[0, 4], span[0, 5]
    begin = jnp.minimum(first_z, BOX - CORE)
    chunks = CORE // CHUNK
    copies = [
        pltpu.make_async_copy(
            orbitals.at[0, :, pl.ds(pl.multiple_of((begin + c * CHUNK) * PLANE, LANES), CHUNK * PLANE)],
            buffer.at[c],
            arrived.at[c],
        )
        for c in range(chunks)
    ]
    for copy in copies:
        copy.start()
    orbital = lax.broadcasted_iota(jnp.int32, (orbital_count, LANES), 0)
    weight = jnp.zeros((orbital_count, LANES), jnp.int32)
    for o in range(orbital_count):
        weight = jnp.where(orbital == o, occupations[0, o], weight)
    weight = (weight * sign[0]).astype(jnp.float32)
    groups = CHUNK * GROUPS // 8
    tiles = WIDE // LANES
    for c in range(chunks):
        copies[c].wait()

        def add_rows(b, carry, c=c):
            for q in range(tiles):
                cells = []
                for s in range(8):
                    lane = pl.multiple_of((8 * b + s) * WIDE + q * LANES, LANES)
                    values = buffer[c, :, pl.ds(lane, LANES)].astype(jnp.float32)
                    values = values * values * weight
                    cells.append(sum(values[8 * h : 8 * h + 8] for h in range(orbital_count // 8)))
                at = pl.multiple_of((c * groups + b) * 8, 8)
                sums[pl.ds(at, 8), q * LANES : (q + 1) * LANES] = row_sums(cells)
            return carry

        lax.fori_loop(0, groups, add_rows, 0)
    count = CORE * GROUPS
    for r in range(8):
        rows[pl.ds(r, count, stride=8), 0:BOX] = sums[:, r * BOX : (r + 1) * BOX]

    start_z = lax.rem(corners[0, own] + first_z, depth) - base(own)
    start_x = lax.rem(corners[1, own] + first_x, count_x)
    start_y = lax.rem(corners[2, own] + first_y, count_y)
    row = lax.broadcasted_iota(jnp.int32, (8, LANES), 0)
    lane = lax.broadcasted_iota(jnp.int32, (8, LANES), 1)
    first = jnp.where(lane[0:1] == 0, start_x, start_y).astype(jnp.float32)

    def pack(step, carry):
        turned = []
        for h in range(UNROLL):
            p = lax.rem(UNROLL * step + h - start_z + depth, depth)
            local = jnp.minimum(p + first_z - begin, CORE - 1)
            cells = rows[pl.ds(local * BOX + first_x, CORE), :]
            for q in range(4):
                turn = lax.rem(32 * q - first_y + LANES, LANES)
                turned.append(pltpu.roll(cells[8 * q : 8 * q + 8], turn, 1))
        for h in range(UNROLL):
            k = UNROLL * step + h
            held = lax.rem(k - start_z + depth, depth) < len_z
            packed = jnp.zeros((8, LANES), jnp.float32)
            for q in range(4):
                keep = (row + 8 * q < len_x) & (lane >= 32 * q) & (lane < 32 * q + len_y) & held
                packed = jnp.where(keep, turned[4 * h + q], packed)
            for s in range(8):
                out[k, :, s * LANES : (s + 1) * LANES] = packed[s : s + 1]
            out[k, :, PACK:PIECE] = first
        return carry

    lax.fori_loop(0, slots // UNROLL, pack, 0)


def core_pieces(device, corners, span, occupations, sign, orbitals, slots, base, counts):
    orbital_count = orbitals.shape[1]
    return small_call(
        lambda *refs: core_kernel(base, *counts, *refs),
        "core_pieces",
        8,
        out_shape=jax.ShapeDtypeStruct((slots, 1, PIECE), jnp.float32),
        in_specs=in_smem(5) + anywhere(1),
        out_specs=in_vmem(1)[0],
        scratch_shapes=[
            pltpu.VMEM((CORE // CHUNK, orbital_count, CHUNK * PLANE), orbitals.dtype),
            pltpu.VMEM((CORE * GROUPS, WIDE), jnp.float32),
            pltpu.VMEM((CORE * BOX + CORE, LANES), jnp.float32),
            pltpu.SemaphoreType.DMA((CORE // CHUNK,)),
        ],
        cost_estimate=pl.CostEstimate(flops=40_000_000, bytes_accessed=4_000_000, transcendentals=0),
    )(device, corners, span, occupations, sign, orbitals)


def plane_kernel(group, pieces, outer, table_x, table_y, spectrum, density, packed):
    slots = pieces.shape[0]
    count_x, count_y = outer.shape
    groups = slots // group
    column = lax.broadcasted_iota(jnp.int32, (count_x, CORE), 1)
    cell_x = lax.broadcasted_iota(jnp.int32, (count_x, CORE), 0)
    row = lax.broadcasted_iota(jnp.int32, (CORE, count_y), 0)
    cell_y = lax.broadcasted_iota(jnp.int32, (CORE, count_y), 1)
    lefts, rights = [], []
    for j in range(groups):
        total = pieces[j * group, :, 0:PACK]
        for m in range(1, group):
            total = total + pieces[j * group + m, :, 0:PACK]
        for s in range(8):
            packed[8 * j + s : 8 * j + s + 1, :] = total[:, s * LANES : (s + 1) * LANES]
        tile = packed[8 * j : 8 * j + 8, :]
        square = jnp.concatenate([tile[:, 32 * q : 32 * q + 32] for q in range(4)], axis=0)
        first = pieces[j * group, :, PACK : PACK + LANES].astype(jnp.int32)
        away_x = cell_x - first[:, 0:1]
        away_y = cell_y - first[:, 1:2]
        left = jnp.where(away_x < 0, away_x + count_x, away_x) == column
        right = jnp.where(away_y < 0, away_y + count_y, away_y) == row
        right = jnp.where(right, 1.0, 0.0).astype(jnp.bfloat16)
        high = square.astype(jnp.bfloat16)
        rest = square - high.astype(jnp.float32)
        middle = rest.astype(jnp.bfloat16)
        low = (rest - middle.astype(jnp.float32)).astype(jnp.bfloat16)
        lefts.append(jnp.where(left, 1.0, 0.0).astype(jnp.bfloat16))
        rights.append([product(part, right).astype(jnp.bfloat16) for part in (high, middle, low)])
    left = jnp.concatenate(lefts, axis=1)
    placed = outer[...]
    for part in range(2, -1, -1):
        placed = placed + product(left, jnp.concatenate([r[part] for r in rights], axis=0))
    density[...] = placed
    spectrum[...] = times_table(table_times(table_x, placed), table_y)


def plane_spectrum(pieces, group, outer, table_x, table_y):
    shape = jax.ShapeDtypeStruct(outer.shape, jnp.float32)
    return small_call(
        lambda *refs: plane_kernel(group, *refs),
        "plane_spectrum",
        12,
        out_shape=(shape, shape),
        in_specs=in_vmem(4),
        out_specs=in_vmem(2),
        scratch_shapes=[pltpu.VMEM((8 * (pieces.shape[0] // group), LANES), jnp.float32)],
    )(pieces, outer, table_x, table_y)


def wave_squares(index, count):
    folded = jnp.where(index > count // 2, index - count, index)
    wave = 2.0 * math.pi / (count * spacing) * folded.astype(jnp.float32)
    return wave * wave


def column_kernel(count_z, count_x, count_y, device, values, table, out):
    rows, lanes = values.shape
    deep = rows // count_z
    transformed = table_times(table, values[...])
    row = lax.broadcasted_iota(jnp.int32, (rows, lanes), 0)
    lane = lax.broadcasted_iota(jnp.int32, (rows, lanes), 1)
    cell = (device[0] * deep + row % deep) * lanes + lane
    square = (
        wave_squares(row // deep, count_z)
        + wave_squares(cell // count_y, count_x)
        + wave_squares(cell % count_y, count_y)
    )
    scale = 4.0 * math.pi / float(count_z * count_x * count_y)
    kernel = jnp.where(square > 0, scale / jnp.where(square > 0, square, 1.0), 0.0)
    out[...] = table_times(table, transformed * kernel)


def column_hartree(values, table, device, counts):
    return small_call(
        lambda *refs: column_kernel(*counts, *refs),
        "column_hartree",
        12,
        out_shape=jax.ShapeDtypeStruct(values.shape, jnp.float32),
        in_specs=in_smem(1) + in_vmem(2),
        out_specs=in_vmem(1)[0],
    )(device, values, table)


def window_kernel(fragment, device, corners, spectrum, exchange, table_x, table_y, *refs):
    *blocks, out, wide, cut = refs
    slots = out.shape[0]
    count_x, count_y = spectrum.shape
    x_dev = count_x // len(blocks)
    plane = times_table(table_times(table_x, spectrum[...]), table_y) + exchange[...]
    tall = count_x + BOX
    tiles = count_y // LANES
    for t in range(tiles):
        part = plane[:, t * LANES : (t + 1) * LANES]
        wide[t * tall : t * tall + count_x, :] = part
        wide[t * tall + count_x : (t + 1) * tall, :] = part[0:BOX]
    sub = lax.rem(device[0], len(blocks))
    for d, block in enumerate(blocks):
        for t in range(tiles):
            at = pl.multiple_of(t * tall + (sub ^ d) * x_dev, 8)
            block[:, t * LANES : (t + 1) * LANES] = wide[pl.ds(at, x_dev), :]
    lane = lax.broadcasted_iota(jnp.int32, (BOX, LANES), 1)

    def cut_windows(step, carry):
        turned = []
        for h in range(UNROLL):
            f = fragment(UNROLL * step + h, device[0])
            x, y = corners[1, f], corners[2, f]
            tile = y // LANES
            over = y - tile * LANES
            near = wide[pl.ds(tile * tall + x, BOX), :]
            far = wide[pl.ds(lax.rem(tile + 1, tiles) * tall + x, BOX), :]
            turn = lax.rem(LANES - over, LANES)
            turned.append(pltpu.roll(jnp.where(lane < over, far, near), turn, 1))
        for h in range(UNROLL):
            at = pl.multiple_of((UNROLL * step + h) * BOX, 8)
            cut[pl.ds(at, BOX), :] = turned[h]
        return carry

    lax.fori_loop(0, slots // UNROLL, cut_windows, 0)
    count = slots * GROUPS
    flat = jnp.concatenate(
        [cut[pl.ds(r, count, stride=8), :][:, 0:BOX] for r in range(8)], axis=1
    )
    for k in range(slots):
        for g in range(GROUPS):
            out[k, :, g * WIDE : (g + 1) * WIDE] = flat[k * GROUPS + g : k * GROUPS + g + 1, :]


def plane_windows(
    device, corners, spectrum, exchange, table_x, table_y, blocks, slots, fragment
):
    count_x, count_y = spectrum.shape
    block = jax.ShapeDtypeStruct((count_x // blocks, count_y), jnp.float32)
    return small_call(
        lambda *refs: window_kernel(fragment, *refs),
        "plane_windows",
        12,
        out_shape=[block] * blocks + [jax.ShapeDtypeStruct((slots, 1, PLANE), jnp.float32)],
        in_specs=in_smem(2) + in_vmem(4),
        out_specs=in_vmem(blocks + 1),
        scratch_shapes=[
            pltpu.VMEM((count_y // LANES * (count_x + BOX), LANES), jnp.float32),
            pltpu.VMEM((slots * BOX, LANES), jnp.float32),
        ],
    )(device, corners, spectrum, exchange, table_x, table_y)


def output_kernel(base, device, corners, windows, *refs):
    *blocks, box, potential, copied = refs
    depth = windows.shape[0]
    first = corners[0, device[0]] - base(device[0])
    sub = lax.rem(device[0], len(blocks))
    copies = [
        pltpu.make_async_copy(block, potential.at[sub ^ d], copied.at[BOX + d])
        for d, block in enumerate(blocks)
    ]
    for i in range(BOX):
        z = lax.rem(first + i, depth)
        copies.append(pltpu.make_async_copy(windows.at[z], box.at[i], copied.at[i]))
    for copy in copies:
        copy.start()
    for copy in copies:
        copy.wait()


def outputs(device, corners, windows, blocks, base):
    count = len(blocks)
    return small_call(
        lambda *refs: output_kernel(base, *refs),
        "outputs",
        4,
        out_shape=(
            jax.ShapeDtypeStruct((BOX, 1, PLANE), jnp.float32),
            jax.ShapeDtypeStruct((count,) + blocks[0].shape, jnp.float32),
        ),
        in_specs=in_smem(2) + anywhere(1 + count),
        out_specs=tuple(anywhere(2)),
        scratch_shapes=[pltpu.SemaphoreType.DMA((BOX + count,))],
    )(device, corners, windows, *blocks)


def body(orbitals, occupations, patch_sign, corners, core_span, outer_density):
    slab_count = lax.axis_size("slab")
    sub_count = lax.axis_size("sub")
    devices = slab_count * sub_count
    z_dev, x_dev, count_y = outer_density.shape
    count_x = x_dev * sub_count
    count_z = z_dev * slab_count
    device = lax.axis_index("slab") * sub_count + lax.axis_index("sub")
    table_x = hartley(count_x)
    table_y = hartley(count_y)
    per_device = count_x * count_y // devices
    deep = max(1, per_device // count_y)
    table_z = hartley(count_z, deep)

    device = jnp.reshape(device, (1,))
    assert z_dev == sub_count
    reach = (BOX + z_dev - 2) // z_dev + 1
    if slab_count <= reach:
        slots, group = devices, KINDS

        def base(own):
            return 0

        def fragment(slot, own):
            return slot

        def spread(pieces):
            return lax.all_to_all(pieces, AXES, 0, 0, tiled=True)

        collect = spread
    else:
        slots, group = reach * sub_count, sub_count

        def base(own):
            return own - lax.rem(own, sub_count)

        def fragment(slot, own):
            away = slot // sub_count * sub_count
            return lax.rem(base(own) - away + devices, devices) + lax.rem(slot, sub_count)

        def passed(pieces, sign):
            pieces = pieces.reshape((reach, sub_count) + pieces.shape[1:])
            pieces = lax.all_to_all(pieces, "sub", 1, 1, tiled=True)
            moved = [pieces[0]]
            for d in range(1, reach):
                ring = [(i, (i + sign * d) % slab_count) for i in range(slab_count)]
                moved.append(lax.ppermute(pieces[d], "slab", ring))
            return jnp.concatenate(moved, axis=0)

        def spread(pieces):
            return passed(pieces, 1)

        def collect(pieces):
            return passed(pieces, -1)

    corners, span, occupations, orbitals = (
        pltpu.with_memory_space_constraint(argument, pltpu.HBM)
        for argument in (corners.T, core_span, occupations, orbitals)
    )
    counts = (count_z, count_x, count_y)
    outer = lax.all_to_all(outer_density, "sub", 0, 0, tiled=True).reshape(count_x, count_y)
    pieces = core_pieces(
        device, corners, span, occupations, patch_sign, orbitals, slots, base, counts
    )
    pieces = spread(pieces)
    spectrum, density = plane_spectrum(pieces, group, outer, table_x, table_y)
    chunk = (devices, deep, per_device // deep)
    spectrum = lax.all_to_all(spectrum.reshape(chunk), AXES, 0, 0, tiled=True)
    exchange = exchange_correlation(density)
    spectrum = column_hartree(
        spectrum.reshape(devices * deep, per_device // deep), table_z, device, counts
    )
    spectrum = lax.all_to_all(spectrum.reshape(chunk), AXES, 0, 0, tiled=True)
    *blocks, windows = plane_windows(
        device,
        corners,
        spectrum.reshape(count_x, count_y),
        exchange,
        table_x,
        table_y,
        sub_count,
        slots,
        fragment,
    )
    blocks = [
        lax.ppermute(block, "sub", [(i, i ^ d) for i in range(sub_count)]) if d else block
        for d, block in enumerate(blocks)
    ]
    windows = collect(windows)
    box, potential = outputs(device, corners, windows, blocks, base)
    return (box.reshape(1, BOX * PLANE), potential)


def solution(mesh):
    placed = (
        P(("slab", "sub"), None, None),
        P(("slab", "sub"), None),
        P(("slab", "sub")),
        P(),
        P(("slab", "sub"), None),
        P("slab", "sub", None),
    )
    return jax.shard_map(
        body,
        mesh=mesh,
        in_specs=placed,
        out_specs=(P(("slab", "sub"), None), P("slab", "sub", None)),
        check_vma=False,
    )
```

time: 101 us -> 73.1 us (0.72)
  blocking collectives: 53.4 us -> 26.5 us
  waiting for transfers between devices: 7.67 us -> 20.7 us
  Pallas kernels: 22.7 us -> 12.1 us
  starting transfers between devices: 6.83 us -> 11.5 us
  other arithmetic: 4.98 us -> 0.54 us
  local copies, waits for them, and re-layouts: 3.64 us -> 0.01 us
    all_to_all x3 -> x1, blocking collectives: 39.6 us -> 14 us  [spread(): return lax.all_to_all(pieces, AXES, 0, 0, tiled=True)]
    pallas_call x5, Pallas kernels: 22.7 us -> 12.1 us  [the longest x1 4.15 us: core_pieces(): small_call(lambda *refs: core_kernel(base, *counts, *refs), 'core_pieces'...]
    ppermute x0 -> x3, waiting for transfers between devices: none -> 5.52 us  [body(): lax.ppermute(block, 'sub', [(i, i ^ d) for i in range(sub_count)])]
    all_to_all x0 -> x1, waiting for transfers between devices: none -> 3.95 us  [spread(): return lax.all_to_all(pieces, AXES, 0, 0, tiled=True)]
    all_to_all x0 -> x1, starting transfers between devices: none -> 2.59 us  [spread(): return lax.all_to_all(pieces, AXES, 0, 0, tiled=True)]
    all_to_all x1, waiting for transfers between devices: 7.67 us -> 10 us  [body(): spectrum = lax.all_to_all(spectrum.reshape(chunk), AXES, 0, 0, tiled=True)]
    unnamed x11 -> x4, local copies, waits for them, and re-layouts: 2.19 us -> 0.01 us
    ppermute x0 -> x3, starting transfers between devices: none -> 1.93 us  [body(): lax.ppermute(block, 'sub', [(i, i ^ d) for i in range(sub_count)])]
  transfers between devices with their start and end apart: 2 -> 6, of which waited for: 1 -> 5; matrix products, arithmetic and copies ran while one was open for 7% -> 1% of each run, Pallas kernels for 9% -> 6%
where the time goes in v1:
time: 73.1 us; the launch traced here: 72.7 us
  blocking collectives  26.5 us (36%)
  waiting for transfers between devices  20.7 us (28%)
  Pallas kernels  12.1 us (17%)
  starting transfers between devices  11.5 us (16%)
  between operations  1.34 us (2%)
    all_to_all x1, blocking collectives, spread(): return lax.all_to_all(pieces, AXES, 0, 0, tiled=True)  14 us
    all_to_all x1, blocking collectives, body(): spectrum = lax.all_to_all(spectrum.reshape(chunk), AXES, 0, 0, tiled=True)  12.5 us
    all_to_all x1, waiting for transfers between devices, body(): spectrum = lax.all_to_all(spectrum.reshape(chunk), AXES, 0, 0, tiled=True)  10 us
    ppermute x3, waiting for transfers between devices, body(): lax.ppermute(block, 'sub', [(i, i ^ d) for i in range(sub_count)])  5.52 us
    all_to_all x1, starting transfers between devices, body(): lax.all_to_all(outer_density, 'sub', 0, 0, tiled=True)  4.38 us
    pallas_call x1, Pallas kernels, core_pieces(): small_call(lambda *refs: core_kernel(base, *counts, *refs), 'core_pieces'...  4.15 us
    all_to_all x1, waiting for transfers between devices, spread(): return lax.all_to_all(pieces, AXES, 0, 0, tiled=True)  3.95 us
    pallas_call x1, Pallas kernels, plane_windows(): small_call(lambda *refs: window_kernel(fragment, *refs), 'plane_windows',...  3.2 us
  transfers between devices with their start and end apart: 6, of which 5 were waited for; matrix products, arithmetic and copies ran while one was open for 1% of the time, Pallas kernels for 6%

profile of v1, /device:TPU:0, one launch (start us, length us, event | category | flops | bytes accessed | tf_op | source)
XLA Modules:
  0.0 72.7 jit_solution(10777804559430684578)
XLA Ops:
  0.6 0.0 copy-start
  0.6 0.0 copy-start.1
  0.7 4.4 %all-to-all-start.1 = ((f32[4,64,256]{2,1,0:T(8,128)}), f32[4,64,256]{2,1,0:T(8,128)S(1)}, u32[]{:S(2)}, u32[]{:S(2)}) async-start(f32[4,64,256]{2,1,0:T(8,128)} %param.14), calls=%async_computation.1 | async-start | bytes 524288 | tf_op jit(solution)/shard_map/all_to_all | solution.py:447
  5.7 4.1 %core_pieces.1 = f32[32,1,1152]{2,1,0:T(1,128)S(1)} custom-call(s32[1]{0:T(128)} %bitcast.refs_0_, s32[3,32]{1,0:T(4,128)} %bitcast.12, s32[1,6]{1,0:T(1,128)} %refs_2_.3, s32[1,16]{1,0:T(1,128)} %refs_3_.2, s32[1]{0:T(128)S(6)} %copy.11.refs_4_, bf16[1,16,110592]{2,1,0:T(8,128)(2,1)} %refs_5_.2), custom_call_target="tpu_custom_call" | custom-call | flops 40000000 | bytes 4000000 | tf_op jit(solution)/shard_map/core_pieces/pallas_call | solution.py:188
  9.8 1.2 %all-to-all-done.1 = f32[4,64,256]{2,1,0:T(8,128)S(1)} async-done(((f32[4,64,256]{2,1,0:T(8,128)}), f32[4,64,256]{2,1,0:T(8,128)S(1)}, u32[]{:S(2)}, u32[]{:S(2)}) %all-to-all-start.1) | async-done | bytes 262176 | tf_op jit(solution)/shard_map/all_to_all | solution.py:447
  11.0 14.0 %all_to_all.25.refs_0_ = f32[32,1,1152]{2,1,0:T(1,128)S(1)} all-to-all(f32[32,1,1152]{2,1,0:T(1,128)S(1)} %core_pieces.1), channel_id=1, replica_groups=mesh['slab'=8,'sub'=4] {'slab','sub'}, dimensions={0} | all-to-all | bytes 294912 | tf_op jit(solution)/shard_map/all_to_all | solution.py:414
  25.1 0.0 copy-done
  25.1 1.1 %plane_spectrum.1 = (f32[256,256]{1,0:T(8,128)S(1)}, f32[256,256]{1,0:T(8,128)S(1)}) custom-call(f32[32,1,1152]{2,1,0:T(1,128)S(1)} %all_to_all.25.refs_0_, f32[256,256]{1,0:T(8,128)S(1)} %bitcast.8, bf16[2,256,256]{2,1,0:T(8,128)(2,1)S(1)} %copy-done, bf16[2,256,256]{2,1,0:T(8,128)(2,1)S(1)} %copy-done), custom_call_target="tpu_custom_call" | custom-call | tf_op jit(solution)/shard_map/plane_spectrum/pallas_call | solution.py:244
  26.2 12.5 %all_to_all.26 = f32[32,8,256]{2,1,0:T(8,128)S(1)} all-to-all(f32[32,8,256]{2,1,0:T(8,128)S(1)} %bitcast.11), channel_id=1, replica_groups=mesh['slab'=8,'sub'=4] {'slab','sub'}, dimensions={0} | all-to-all | bytes 524288 | tf_op jit(solution)/shard_map/all_to_all | solution.py:454
  38.6 0.0 copy-done.1
  38.7 1.6 %column_hartree.1 = f32[256,256]{1,0:T(8,128)} custom-call(s32[1]{0:T(128)} %bitcast.refs_0_, f32[256,256]{1,0:T(8,128)S(1)} %bitcast.10, bf16[2,256,256]{2,1,0:T(8,128)(2,1)S(1)} %copy-done.1), custom_call_target="tpu_custom_call" | custom-call | tf_op jit(solution)/shard_map/column_hartree/pallas_call | solution.py:279
  40.3 2.6 %all-to-all-start.3 = ((f32[32,8,256]{2,1,0:T(8,128)}), f32[32,8,256]{2,1,0:T(8,128)S(1)}, u32[]{:S(2)}, u32[]{:S(2)}) async-start(f32[32,8,256]{2,1,0:T(8,128)} %bitcast.5), calls=%async_computation.3 | async-start | bytes 524288 | tf_op jit(solution)/shard_map/all_to_all | solution.py:459
  42.9 0.5 subtract_add_fusion.refs_3_
  43.4 10.0 %all-to-all-done.3 = f32[32,8,256]{2,1,0:T(8,128)S(1)} async-done(((f32[32,8,256]{2,1,0:T(8,128)}), f32[32,8,256]{2,1,0:T(8,128)S(1)}, u32[]{:S(2)}, u32[]{:S(2)}) %all-to-all-start.3) | async-done | bytes 262176 | tf_op jit(solution)/shard_map/all_to_all | solution.py:459
  53.5 3.2 %plane_windows.1 = (f32[64,256]{1,0:T(8,128)S(1)}, f32[64,256]{1,0:T(8,128)S(1)}, f32[64,256]{1,0:T(8,128)S(1)}, f32[64,256]{1,0:T(8,128)S(1)}, f32[32,1,2304]{2,1,0:T(1,128)}) custom-call(s32[1]{0:T(128)} %bitcast.refs_0_, s32[3,32]{1,0:T(4,128)} %bitcast.13, f32[256,256]{1,0:T(8,128)S(1)} %bitcast.9, f32[256,256]{1,0:T(8,128)S(1)} %subtract_add_fusion.refs_3_, ...), custom_call_target="tpu_custom_call" | custom-call | tf_op jit(solution)/shard_map/plane_windows/pallas_call | solution.py:339
  56.7 2.6 %all-to-all-start.4 = ((f32[32,1,2304]{2,1,0:T(1,128)}), f32[32,1,2304]{2,1,0:T(1,128)S(1)}, u32[]{:S(2)}, u32[]{:S(2)}) async-start(f32[32,1,2304]{2,1,0:T(1,128)} %get-tuple-element.13), calls=%async_computation.4 | async-start | bytes 589824 | tf_op jit(solution)/shard_map/all_to_all | solution.py:414
  59.3 0.2 collective-permute-start
  59.4 1.6 %collective-permute-start.1 = (f32[64,256]{1,0:T(8,128)S(1)}, f32[64,256]{1,0:T(8,128)S(1)}, u32[]{:S(2)}, u32[]{:S(2)}) collective-permute-start(f32[64,256]{1,0:T(8,128)S(1)} %get-tuple-element.16), channel_id=1, source_target_pairs={{0,2},{1,3},{2,0},{3,1},{4,6},{5,7},{6,4},{7,5},{8,10},{9,11},{10,... | collective-permute-start | bytes 196616 | tf_op jit(solution)/shard_map/ppermute | solution.py:472
  61.1 0.1 collective-permute-start.2
  61.2 0.0 collective-permute-done.refs_4_
  61.2 5.1 %collective-permute-done.1.refs_5_ = f32[64,256]{1,0:T(8,128)S(1)} collective-permute-done((f32[64,256]{1,0:T(8,128)S(1)}, f32[64,256]{1,0:T(8,128)S(1)}, u32[]{:S(2)}, u32[]{:S(2)}) %collective-permute-start.1) | collective-permute-done | bytes 65568 | tf_op jit(solution)/shard_map/ppermute | solution.py:472
  66.3 0.4 collective-permute-done.2.refs_6_
  66.7 3.9 %all-to-all-done.4.refs_2_ = f32[32,1,2304]{2,1,0:T(1,128)S(1)} async-done(((f32[32,1,2304]{2,1,0:T(1,128)}), f32[32,1,2304]{2,1,0:T(1,128)S(1)}, u32[]{:S(2)}, u32[]{:S(2)}) %all-to-all-start.4) | async-done | bytes 294944 | tf_op jit(solution)/shard_map/all_to_all | solution.py:414
  70.7 2.0 %outputs.1 = (f32[48,1,2304]{2,1,0:T(1,128)}, f32[4,64,256]{2,1,0:T(8,128)}) custom-call(s32[1]{0:T(128)} %bitcast.refs_0_, s32[3,32]{1,0:T(4,128)} %bitcast.14, f32[32,1,2304]{2,1,0:T(1,128)S(1)} %all-to-all-done.4.refs_2_, f32[64,256]{1,0:T(8,128)S(1)} %get-tuple-element.14.refs_3_, f32[64,256]{1,0:T(8,128)S(1)} %collective-permute-done.refs_4_, ...), custom_call_target="tpu_custom_call" | custom-call | tf_op jit(solution)/shard_map/outputs/pallas_call | solution.py:373
Async XLA Ops:
  0.6 24.4 %copy-start = (bf16[2,256,256]{2,1,0:T(8,128)(2,1)S(1)}, bf16[2,256,256]{2,1,0:T(8,128)(2,1)}, u32[]{:S(2)}) copy-start(bf16[2,256,256]{2,1,0:T(8,128)(2,1)} %constant.31.clone.refs_2_.refs_3_.refs_4_.refs_5_) | copy-start | bytes 786436
  0.6 38.0 %copy-start.1 = (bf16[2,256,256]{2,1,0:T(8,128)(2,1)S(1)}, bf16[2,256,256]{2,1,0:T(8,128)(2,1)}, u32[]{:S(2)}) copy-start(bf16[2,256,256]{2,1,0:T(8,128)(2,1)} %constant.32.clone.refs_2_) | copy-start | bytes 786436
  0.7 10.4 %all-to-all-start.1 = ((f32[4,64,256]{2,1,0:T(8,128)}), f32[4,64,256]{2,1,0:T(8,128)S(1)}, u32[]{:S(2)}, u32[]{:S(2)}) async-start(f32[4,64,256]{2,1,0:T(8,128)} %param.14), calls=%async_computation.1 | async-start | bytes 524288 | tf_op jit(solution)/shard_map/all_to_all | solution.py:447
  40.3 13.2 %all-to-all-start.3 = ((f32[32,8,256]{2,1,0:T(8,128)}), f32[32,8,256]{2,1,0:T(8,128)S(1)}, u32[]{:S(2)}, u32[]{:S(2)}) async-start(f32[32,8,256]{2,1,0:T(8,128)} %bitcast.5), calls=%async_computation.3 | async-start | bytes 524288 | tf_op jit(solution)/shard_map/all_to_all | solution.py:459
  56.7 14.0 %all-to-all-start.4 = ((f32[32,1,2304]{2,1,0:T(1,128)}), f32[32,1,2304]{2,1,0:T(1,128)S(1)}, u32[]{:S(2)}, u32[]{:S(2)}) async-start(f32[32,1,2304]{2,1,0:T(1,128)} %get-tuple-element.13), calls=%async_computation.4 | async-start | bytes 589824 | tf_op jit(solution)/shard_map/all_to_all | solution.py:414
  59.3 1.9 %collective-permute-start = (f32[64,256]{1,0:T(8,128)S(1)}, f32[64,256]{1,0:T(8,128)S(1)}, u32[]{:S(2)}, u32[]{:S(2)}) collective-permute-start(f32[64,256]{1,0:T(8,128)S(1)} %get-tuple-element.15), channel_id=1, source_target_pairs={{0,1},{1,0},{2,3},{3,2},{4,5},{5,4},{6,7},{7,6},{8,9},{9,8},{10,11... | collective-permute-start | bytes 196616 | tf_op jit(solution)/shard_map/ppermute | solution.py:472
  59.4 6.9 %collective-permute-start.1 = (f32[64,256]{1,0:T(8,128)S(1)}, f32[64,256]{1,0:T(8,128)S(1)}, u32[]{:S(2)}, u32[]{:S(2)}) collective-permute-start(f32[64,256]{1,0:T(8,128)S(1)} %get-tuple-element.16), channel_id=1, source_target_pairs={{0,2},{1,3},{2,0},{3,1},{4,6},{5,7},{6,4},{7,5},{8,10},{9,11},{10,... | collective-permute-start | bytes 196616 | tf_op jit(solution)/shard_map/ppermute | solution.py:472
  61.1 5.6 %collective-permute-start.2 = (f32[64,256]{1,0:T(8,128)S(1)}, f32[64,256]{1,0:T(8,128)S(1)}, u32[]{:S(2)}, u32[]{:S(2)}) collective-permute-start(f32[64,256]{1,0:T(8,128)S(1)} %get-tuple-element.17), channel_id=1, source_target_pairs={{0,3},{1,2},{2,1},{3,0},{4,7},{5,6},{6,5},{7,4},{8,11},{9,10},{10,... | collective-permute-start | bytes 196616 | tf_op jit(solution)/shard_map/ppermute | solution.py:472

commit v2 on v1

--- a/solution.py
+++ b/solution.py
@@ -79,6 +79,10 @@
 
 def anywhere(count):
     return [pl.BlockSpec(memory_space=pl.ANY)] * count
+
+
+def kept(shape):
+    return pltpu.VMEM(shape, jnp.float32)
 
 
 def row_sums(tiles):
@@ -102,14 +106,16 @@
     return fours[0]
 
 
+CORNERS = pltpu.HBM
 CHUNK = 8
 UNROLL = 4
 
 
 def core_kernel(
-    base, depth, count_x, count_y, device, corners, span, occupations, sign, orbitals, out,
-    buffer, sums, rows, arrived,
+    base, depth, count_x, count_y, device, corners, span, occupations, sign, orbitals, outer, out,
+    *refs,
 ):
+    *blocks, buffer, sums, rows, arrived, filled = refs
     own, slots, orbital_count = device[0], out.shape[0], orbitals.shape[1]
     first_z, first_x, first_y = span[0, 0], span[0, 1], span[0, 2]
     len_z, len_x, len_y = span[0, 3], span[0, 4], span[0, 5]
@@ -125,6 +131,13 @@
     ]
     for copy in copies:
         copy.start()
+    sub = lax.rem(own, len(blocks))
+    fills = [
+        pltpu.make_async_copy(outer.at[sub ^ d], block, filled.at[d])
+        for d, block in enumerate(blocks)
+    ]
+    for fill in fills:
+        fill.start()
     orbital = lax.broadcasted_iota(jnp.int32, (orbital_count, LANES), 0)
     weight = jnp.zeros((orbital_count, LANES), jnp.int32)
     for o in range(orbital_count):
@@ -147,7 +160,7 @@
                 sums[pl.ds(at, 8), q * LANES : (q + 1) * LANES] = row_sums(cells)
             return carry
 
-        lax.fori_loop(0, groups, add_rows, 0)
+        lax.fori_loop(0, groups, add_rows, 0, unroll=2)
     count = CORE * GROUPS
     for r in range(8):
         rows[pl.ds(r, count, stride=8), 0:BOX] = sums[:, r * BOX : (r + 1) * BOX]
@@ -181,30 +194,39 @@
         return carry
 
     lax.fori_loop(0, slots // UNROLL, pack, 0)
-
-
-def core_pieces(device, corners, span, occupations, sign, orbitals, slots, base, counts):
+    for fill in fills:
+        fill.wait()
+
+
+def core_pieces(device, corners, span, occupations, sign, orbitals, outer, slots, base, counts):
     orbital_count = orbitals.shape[1]
+    blocks = outer.shape[0]
     return small_call(
         lambda *refs: core_kernel(base, *counts, *refs),
         "core_pieces",
         8,
-        out_shape=jax.ShapeDtypeStruct((slots, 1, PIECE), jnp.float32),
-        in_specs=in_smem(5) + anywhere(1),
-        out_specs=in_vmem(1)[0],
+        out_shape=[kept((slots, 1, PIECE))] + [kept(outer.shape[1:])] * blocks,
+        in_specs=in_smem(5) + anywhere(2),
+        out_specs=in_vmem(1 + blocks),
         scratch_shapes=[
             pltpu.VMEM((CORE // CHUNK, orbital_count, CHUNK * PLANE), orbitals.dtype),
             pltpu.VMEM((CORE * GROUPS, WIDE), jnp.float32),
             pltpu.VMEM((CORE * BOX + CORE, LANES), jnp.float32),
             pltpu.SemaphoreType.DMA((CORE // CHUNK,)),
+            pltpu.SemaphoreType.DMA((blocks,)),
         ],
         cost_estimate=pl.CostEstimate(flops=40_000_000, bytes_accessed=4_000_000, transcendentals=0),
-    )(device, corners, span, occupations, sign, orbitals)
-
-
-def plane_kernel(group, pieces, outer, table_x, table_y, spectrum, density, packed):
+    )(device, corners, span, occupations, sign, orbitals, outer)
+
+
+def plane_kernel(group, device, pieces, table_x, table_y, *refs):
+    *blocks, spectrum, density, packed = refs
     slots = pieces.shape[0]
-    count_x, count_y = outer.shape
+    count_x, count_y = density.shape
+    sub = lax.rem(device[0], len(blocks))
+    x_dev = count_x // len(blocks)
+    for d, block in enumerate(blocks):
+        density[pl.ds(pl.multiple_of((sub ^ d) * x_dev, 8), x_dev), :] = block[...]
     groups = slots // group
     column = lax.broadcasted_iota(jnp.int32, (count_x, CORE), 1)
     cell_x = lax.broadcasted_iota(jnp.int32, (count_x, CORE), 0)
@@ -232,24 +254,24 @@
         lefts.append(jnp.where(left, 1.0, 0.0).astype(jnp.bfloat16))
         rights.append([product(part, right).astype(jnp.bfloat16) for part in (high, middle, low)])
     left = jnp.concatenate(lefts, axis=1)
-    placed = outer[...]
+    placed = density[...]
     for part in range(2, -1, -1):
         placed = placed + product(left, jnp.concatenate([r[part] for r in rights], axis=0))
     density[...] = placed
     spectrum[...] = times_table(table_times(table_x, placed), table_y)
 
 
-def plane_spectrum(pieces, group, outer, table_x, table_y):
-    shape = jax.ShapeDtypeStruct(outer.shape, jnp.float32)
+def plane_spectrum(device, pieces, group, table_x, table_y, blocks):
+    shape = (blocks[0].shape[0] * len(blocks), blocks[0].shape[1])
     return small_call(
         lambda *refs: plane_kernel(group, *refs),
         "plane_spectrum",
         12,
-        out_shape=(shape, shape),
-        in_specs=in_vmem(4),
+        out_shape=(kept(shape), kept(shape)),
+        in_specs=in_smem(1) + in_vmem(3 + len(blocks)),
         out_specs=in_vmem(2),
         scratch_shapes=[pltpu.VMEM((8 * (pieces.shape[0] // group), LANES), jnp.float32)],
-    )(pieces, outer, table_x, table_y)
+    )(device, pieces, table_x, table_y, *blocks)
 
 
 def wave_squares(index, count):
@@ -280,7 +302,7 @@
         lambda *refs: column_kernel(*counts, *refs),
         "column_hartree",
         12,
-        out_shape=jax.ShapeDtypeStruct(values.shape, jnp.float32),
+        out_shape=kept(values.shape),
         in_specs=in_smem(1) + in_vmem(2),
         out_specs=in_vmem(1)[0],
     )(device, values, table)
@@ -335,12 +357,12 @@
     device, corners, spectrum, exchange, table_x, table_y, blocks, slots, fragment
 ):
     count_x, count_y = spectrum.shape
-    block = jax.ShapeDtypeStruct((count_x // blocks, count_y), jnp.float32)
+    block = kept((count_x // blocks, count_y))
     return small_call(
         lambda *refs: window_kernel(fragment, *refs),
         "plane_windows",
         12,
-        out_shape=[block] * blocks + [jax.ShapeDtypeStruct((slots, 1, PLANE), jnp.float32)],
+        out_shape=[block] * blocks + [kept((slots, 1, PLANE))],
         in_specs=in_smem(2) + in_vmem(4),
         out_specs=in_vmem(blocks + 1),
         scratch_shapes=[
@@ -439,17 +461,25 @@
         def collect(pieces):
             return passed(pieces, -1)
 
-    corners, span, occupations, orbitals = (
+    span, occupations, orbitals, outer_density = (
         pltpu.with_memory_space_constraint(argument, pltpu.HBM)
-        for argument in (corners.T, core_span, occupations, orbitals)
-    )
+        for argument in (core_span, occupations, orbitals, outer_density)
+    )
+    corners = pltpu.with_memory_space_constraint(corners.T, CORNERS)
     counts = (count_z, count_x, count_y)
-    outer = lax.all_to_all(outer_density, "sub", 0, 0, tiled=True).reshape(count_x, count_y)
-    pieces = core_pieces(
-        device, corners, span, occupations, patch_sign, orbitals, slots, base, counts
-    )
+
+    def swapped(blocks):
+        return [
+            lax.ppermute(block, "sub", [(i, i ^ d) for i in range(sub_count)]) if d else block
+            for d, block in enumerate(blocks)
+        ]
+
+    pieces, *blocks = core_pieces(
+        device, corners, span, occupations, patch_sign, orbitals, outer_density, slots, base, counts
+    )
+    blocks = swapped(blocks)
     pieces = spread(pieces)
-    spectrum, density = plane_spectrum(pieces, group, outer, table_x, table_y)
+    spectrum, density = plane_spectrum(device, pieces, group, table_x, table_y, blocks)
     chunk = (devices, deep, per_device // deep)
     spectrum = lax.all_to_all(spectrum.reshape(chunk), AXES, 0, 0, tiled=True)
     exchange = exchange_correlation(density)
@@ -468,10 +498,7 @@
         slots,
         fragment,
     )
-    blocks = [
-        lax.ppermute(block, "sub", [(i, i ^ d) for i in range(sub_count)]) if d else block
-        for d, block in enumerate(blocks)
-    ]
+    blocks = swapped(blocks)
     windows = collect(windows)
     box, potential = outputs(device, corners, windows, blocks, base)
     return (box.reshape(1, BOX * PLANE), potential)

time: 73.1 us -> 71 us (0.971)
  blocking collectives: 26.5 us -> 13.7 us
  waiting for transfers between devices: 20.7 us -> 26 us
  starting transfers between devices: 11.5 us -> 16.4 us
    all_to_all x1 -> x0, blocking collectives: 14 us -> none  [spread(): return lax.all_to_all(pieces, AXES, 0, 0, tiled=True)]
    all_to_all x1 -> x2, starting transfers between devices: 2.59 us -> 9.92 us  [spread(): return lax.all_to_all(pieces, AXES, 0, 0, tiled=True)]
    ppermute x3 -> x6, waiting for transfers between devices: 5.52 us -> 10.5 us  [swapped(): lax.ppermute(block, 'sub', [(i, i ^ d) for i in range(sub_count)])]
    all_to_all x1 -> x0, starting transfers between devices: 4.38 us -> none  [body(): lax.all_to_all(outer_density, 'sub', 0, 0, tiled=True)]
    ppermute x3 -> x6, starting transfers between devices: 1.93 us -> 3.88 us  [swapped(): lax.ppermute(block, 'sub', [(i, i ^ d) for i in range(sub_count)])]
    all_to_all x1 -> x2, waiting for transfers between devices: 3.95 us -> 5.47 us  [spread(): return lax.all_to_all(pieces, AXES, 0, 0, tiled=True)]
    all_to_all x1 -> x0, waiting for transfers between devices: 1.2 us -> none  [body(): lax.all_to_all(outer_density, 'sub', 0, 0, tiled=True)]
    all_to_all x1, blocking collectives: 12.5 us -> 13.7 us  [body(): spectrum = lax.all_to_all(spectrum.reshape(chunk), AXES, 0, 0, tiled=True)]
  transfers between devices with their start and end apart: 6 -> 9, of which waited for: 5 -> 7; matrix products, arithmetic and copies ran while one was open for 1% -> 1% of each run, Pallas kernels for 6% -> 0%
where the time goes in v2:
time: 71 us; the launch traced here: 70.6 us
  waiting for transfers between devices  26 us (37%)
  starting transfers between devices  16.4 us (23%)
  blocking collectives  13.7 us (19%)
  Pallas kernels  12.6 us (18%)
  between operations  1.41 us (2%)
    all_to_all x1, blocking collectives, body(): spectrum = lax.all_to_all(spectrum.reshape(chunk), AXES, 0, 0, tiled=True)  13.7 us
    ppermute x6, waiting for transfers between devices, swapped(): lax.ppermute(block, 'sub', [(i, i ^ d) for i in range(sub_count)])  10.5 us
    all_to_all x1, waiting for transfers between devices, body(): spectrum = lax.all_to_all(spectrum.reshape(chunk), AXES, 0, 0, tiled=True)  10 us
    all_to_all x2, starting transfers between devices, spread(): return lax.all_to_all(pieces, AXES, 0, 0, tiled=True)  9.92 us
    all_to_all x2, waiting for transfers between devices, spread(): return lax.all_to_all(pieces, AXES, 0, 0, tiled=True)  5.47 us
    pallas_call x1, Pallas kernels, core_pieces(): small_call(lambda *refs: core_kernel(base, *counts, *refs), 'core_pieces'...  4.69 us
    ppermute x6, starting transfers between devices, swapped(): lax.ppermute(block, 'sub', [(i, i ^ d) for i in range(sub_count)])  3.88 us
    pallas_call x1, Pallas kernels, plane_windows(): small_call(lambda *refs: window_kernel(fragment, *refs), 'plane_windows',...  3.2 us
  transfers between devices with their start and end apart: 9, of which 7 were waited for; matrix products, arithmetic and copies ran while one was open for 1% of the time, Pallas kernels for 0%

profile of v2, /device:TPU:0, one launch (start us, length us, event | category | flops | bytes accessed | tf_op | source)
XLA Modules:
  0.0 70.6 jit_solution(7634663049369372341)
XLA Ops:
  0.6 0.0 copy-start
  0.6 0.0 copy-start.1
  1.4 4.7 %core_pieces.1 = (f32[32,1,1152]{2,1,0:T(1,128)}, f32[64,256]{1,0:T(8,128)S(1)}, f32[64,256]{1,0:T(8,128)S(1)}, f32[64,256]{1,0:T(8,128)S(1)}, f32[64,256]{1,0:T(8,128)S(1)}) custom-call(s32[1]{0:T(128)} %bitcast.refs_0_, s32[3,32]{1,0:T(4,128)} %bitcast.10, s32[1,6]{1,0:T(1,128)} %refs_2_.3, s32[1,16]{1,0:T(1,128)} %refs_3_.2, s32[1]{0:T(128)S(6)} %copy.11.refs_4_, ...), custom_call_target="tpu_custom_call" | custom-call | flops 40000000 | bytes 4000000 | tf_op jit(solution)/shard_map/core_pieces/pallas_call | solution.py:204
  6.1 7.3 %all-to-all-start = ((f32[32,1,1152]{2,1,0:T(1,128)}), f32[32,1,1152]{2,1,0:T(1,128)S(1)}, u32[]{:S(2)}, u32[]{:S(2)}) async-start(f32[32,1,1152]{2,1,0:T(1,128)} %get-tuple-element.16), calls=%async_computation | async-start | bytes 294912 | tf_op jit(solution)/shard_map/all_to_all | solution.py:436
  13.4 0.3 collective-permute-start
  13.7 1.6 %collective-permute-start.1 = (f32[64,256]{1,0:T(8,128)S(1)}, f32[64,256]{1,0:T(8,128)S(1)}, u32[]{:S(2)}, u32[]{:S(2)}) collective-permute-start(f32[64,256]{1,0:T(8,128)S(1)} %get-tuple-element.19), channel_id=1, source_target_pairs={{0,2},{1,3},{2,0},{3,1},{4,6},{5,7},{6,4},{7,5},{8,10},{9,11},{10,... | collective-permute-start | bytes 196616 | tf_op jit(solution)/shard_map/ppermute | solution.py:473
  15.3 0.0 collective-permute-start.2
  15.4 0.0 collective-permute-done.refs_5_
  15.4 3.9 %collective-permute-done.1.refs_6_ = f32[64,256]{1,0:T(8,128)S(1)} collective-permute-done((f32[64,256]{1,0:T(8,128)S(1)}, f32[64,256]{1,0:T(8,128)S(1)}, u32[]{:S(2)}, u32[]{:S(2)}) %collective-permute-start.1) | collective-permute-done | bytes 65568 | tf_op jit(solution)/shard_map/ppermute | solution.py:473
  19.3 1.0 %collective-permute-done.2.refs_7_ = f32[64,256]{1,0:T(8,128)S(1)} collective-permute-done((f32[64,256]{1,0:T(8,128)S(1)}, f32[64,256]{1,0:T(8,128)S(1)}, u32[]{:S(2)}, u32[]{:S(2)}) %collective-permute-start.2) | collective-permute-done | bytes 65568 | tf_op jit(solution)/shard_map/ppermute | solution.py:473
  20.3 1.5 %all-to-all-done.refs_1_ = f32[32,1,1152]{2,1,0:T(1,128)S(1)} async-done(((f32[32,1,1152]{2,1,0:T(1,128)}), f32[32,1,1152]{2,1,0:T(1,128)S(1)}, u32[]{:S(2)}, u32[]{:S(2)}) %all-to-all-start) | async-done | bytes 147488 | tf_op jit(solution)/shard_map/all_to_all | solution.py:436
  21.8 0.0 copy-done
  21.9 1.1 %plane_spectrum.1 = (f32[256,256]{1,0:T(8,128)S(1)}, f32[256,256]{1,0:T(8,128)S(1)}) custom-call(s32[1]{0:T(128)} %bitcast.refs_0_, f32[32,1,1152]{2,1,0:T(1,128)S(1)} %all-to-all-done.refs_1_, bf16[2,256,256]{2,1,0:T(8,128)(2,1)S(1)} %copy-done, bf16[2,256,256]{2,1,0:T(8,128)(2,1)S(1)} %copy-done, f32[64,256]{1,0:T(8,128)S(1)} %get-tuple-element.17.refs_4_, ...), custom_call_target="tpu_custom_call" | custom-call | tf_op jit(solution)/shard_map/plane_spectrum/pallas_call | solution.py:266
  22.9 13.7 %all_to_all.20 = f32[32,8,256]{2,1,0:T(8,128)S(1)} all-to-all(f32[32,8,256]{2,1,0:T(8,128)S(1)} %bitcast.9), channel_id=1, replica_groups=mesh['slab'=8,'sub'=4] {'slab','sub'}, dimensions={0} | all-to-all | bytes 524288 | tf_op jit(solution)/shard_map/all_to_all | solution.py:484
  36.6 0.0 copy-done.1
  36.6 1.6 %column_hartree.1 = f32[256,256]{1,0:T(8,128)} custom-call(s32[1]{0:T(128)} %bitcast.refs_0_, f32[256,256]{1,0:T(8,128)S(1)} %bitcast.8, bf16[2,256,256]{2,1,0:T(8,128)(2,1)S(1)} %copy-done.1), custom_call_target="tpu_custom_call" | custom-call | tf_op jit(solution)/shard_map/column_hartree/pallas_call | solution.py:301
  38.2 2.6 %all-to-all-start.2 = ((f32[32,8,256]{2,1,0:T(8,128)}), f32[32,8,256]{2,1,0:T(8,128)S(1)}, u32[]{:S(2)}, u32[]{:S(2)}) async-start(f32[32,8,256]{2,1,0:T(8,128)} %bitcast.4), calls=%async_computation.2 | async-start | bytes 524288 | tf_op jit(solution)/shard_map/all_to_all | solution.py:489
  40.8 0.5 subtract_add_fusion.refs_3_
  41.4 10.0 %all-to-all-done.2 = f32[32,8,256]{2,1,0:T(8,128)S(1)} async-done(((f32[32,8,256]{2,1,0:T(8,128)}), f32[32,8,256]{2,1,0:T(8,128)S(1)}, u32[]{:S(2)}, u32[]{:S(2)}) %all-to-all-start.2) | async-done | bytes 262176 | tf_op jit(solution)/shard_map/all_to_all | solution.py:489
  51.4 3.2 %plane_windows.1 = (f32[64,256]{1,0:T(8,128)S(1)}, f32[64,256]{1,0:T(8,128)S(1)}, f32[64,256]{1,0:T(8,128)S(1)}, f32[64,256]{1,0:T(8,128)S(1)}, f32[32,1,2304]{2,1,0:T(1,128)}) custom-call(s32[1]{0:T(128)} %bitcast.refs_0_, s32[3,32]{1,0:T(4,128)} %bitcast.11, f32[256,256]{1,0:T(8,128)S(1)} %bitcast.7, f32[256,256]{1,0:T(8,128)S(1)} %subtract_add_fusion.refs_3_, ...), custom_call_target="tpu_custom_call" | custom-call | tf_op jit(solution)/shard_map/plane_windows/pallas_call | solution.py:361
  54.6 2.6 %all-to-all-start.3 = ((f32[32,1,2304]{2,1,0:T(1,128)}), f32[32,1,2304]{2,1,0:T(1,128)S(1)}, u32[]{:S(2)}, u32[]{:S(2)}) async-start(f32[32,1,2304]{2,1,0:T(1,128)} %get-tuple-element.23), calls=%async_computation.3 | async-start | bytes 589824 | tf_op jit(solution)/shard_map/all_to_all | solution.py:436
  57.2 0.2 collective-permute-start.3
  57.4 1.6 %collective-permute-start.4 = (f32[64,256]{1,0:T(8,128)S(1)}, f32[64,256]{1,0:T(8,128)S(1)}, u32[]{:S(2)}, u32[]{:S(2)}) collective-permute-start(f32[64,256]{1,0:T(8,128)S(1)} %get-tuple-element.26), channel_id=1, source_target_pairs={{0,2},{1,3},{2,0},{3,1},{4,6},{5,7},{6,4},{7,5},{8,10},{9,11},{10,... | collective-permute-start | bytes 196616 | tf_op jit(solution)/shard_map/ppermute | solution.py:473
  59.0 0.1 collective-permute-start.5
  59.1 0.0 collective-permute-done.3.refs_4_
  59.1 5.1 %collective-permute-done.4.refs_5_ = f32[64,256]{1,0:T(8,128)S(1)} collective-permute-done((f32[64,256]{1,0:T(8,128)S(1)}, f32[64,256]{1,0:T(8,128)S(1)}, u32[]{:S(2)}, u32[]{:S(2)}) %collective-permute-start.4) | collective-permute-done | bytes 65568 | tf_op jit(solution)/shard_map/ppermute | solution.py:473
  64.2 0.4 collective-permute-done.5.refs_6_
  64.6 3.9 %all-to-all-done.3.refs_2_ = f32[32,1,2304]{2,1,0:T(1,128)S(1)} async-done(((f32[32,1,2304]{2,1,0:T(1,128)}), f32[32,1,2304]{2,1,0:T(1,128)S(1)}, u32[]{:S(2)}, u32[]{:S(2)}) %all-to-all-start.3) | async-done | bytes 294944 | tf_op jit(solution)/shard_map/all_to_all | solution.py:436
  68.6 2.0 %outputs.1 = (f32[48,1,2304]{2,1,0:T(1,128)}, f32[4,64,256]{2,1,0:T(8,128)}) custom-call(s32[1]{0:T(128)} %bitcast.refs_0_, s32[3,32]{1,0:T(4,128)} %bitcast.12, f32[32,1,2304]{2,1,0:T(1,128)S(1)} %all-to-all-done.3.refs_2_, f32[64,256]{1,0:T(8,128)S(1)} %get-tuple-element.24.refs_3_, f32[64,256]{1,0:T(8,128)S(1)} %collective-permute-done.3.refs_4_, ...), custom_call_target="tpu_custom_call" | custom-call | tf_op jit(solution)/shard_map/outputs/pallas_call | solution.py:395
Async XLA Ops:
  0.6 21.2 %copy-start = (bf16[2,256,256]{2,1,0:T(8,128)(2,1)S(1)}, bf16[2,256,256]{2,1,0:T(8,128)(2,1)}, u32[]{:S(2)}) copy-start(bf16[2,256,256]{2,1,0:T(8,128)(2,1)} %constant.31.clone.refs_2_.refs_3_.refs_4_.refs_5_) | copy-start | bytes 786436
  0.6 36.0 %copy-start.1 = (bf16[2,256,256]{2,1,0:T(8,128)(2,1)S(1)}, bf16[2,256,256]{2,1,0:T(8,128)(2,1)}, u32[]{:S(2)}) copy-start(bf16[2,256,256]{2,1,0:T(8,128)(2,1)} %constant.32.clone.refs_2_) | copy-start | bytes 786436
  6.1 15.8 %all-to-all-start = ((f32[32,1,1152]{2,1,0:T(1,128)}), f32[32,1,1152]{2,1,0:T(1,128)S(1)}, u32[]{:S(2)}, u32[]{:S(2)}) async-start(f32[32,1,1152]{2,1,0:T(1,128)} %get-tuple-element.16), calls=%async_computation | async-start | bytes 294912 | tf_op jit(solution)/shard_map/all_to_all | solution.py:436
  13.4 2.0 %collective-permute-start = (f32[64,256]{1,0:T(8,128)S(1)}, f32[64,256]{1,0:T(8,128)S(1)}, u32[]{:S(2)}, u32[]{:S(2)}) collective-permute-start(f32[64,256]{1,0:T(8,128)S(1)} %get-tuple-element.18), channel_id=1, source_target_pairs={{0,1},{1,0},{2,3},{3,2},{4,5},{5,4},{6,7},{7,6},{8,9},{9,8},{10,11... | collective-permute-start | bytes 196616 | tf_op jit(solution)/shard_map/ppermute | solution.py:473
  13.7 5.6 %collective-permute-start.1 = (f32[64,256]{1,0:T(8,128)S(1)}, f32[64,256]{1,0:T(8,128)S(1)}, u32[]{:S(2)}, u32[]{:S(2)}) collective-permute-start(f32[64,256]{1,0:T(8,128)S(1)} %get-tuple-element.19), channel_id=1, source_target_pairs={{0,2},{1,3},{2,0},{3,1},{4,6},{5,7},{6,4},{7,5},{8,10},{9,11},{10,... | collective-permute-start | bytes 196616 | tf_op jit(solution)/shard_map/ppermute | solution.py:473
  15.3 5.0 %collective-permute-start.2 = (f32[64,256]{1,0:T(8,128)S(1)}, f32[64,256]{1,0:T(8,128)S(1)}, u32[]{:S(2)}, u32[]{:S(2)}) collective-permute-start(f32[64,256]{1,0:T(8,128)S(1)} %get-tuple-element.20), channel_id=1, source_target_pairs={{0,3},{1,2},{2,1},{3,0},{4,7},{5,6},{6,5},{7,4},{8,11},{9,10},{10,... | collective-permute-start | bytes 196616 | tf_op jit(solution)/shard_map/ppermute | solution.py:473
  38.2 13.2 %all-to-all-start.2 = ((f32[32,8,256]{2,1,0:T(8,128)}), f32[32,8,256]{2,1,0:T(8,128)S(1)}, u32[]{:S(2)}, u32[]{:S(2)}) async-start(f32[32,8,256]{2,1,0:T(8,128)} %bitcast.4), calls=%async_computation.2 | async-start | bytes 524288 | tf_op jit(solution)/shard_map/all_to_all | solution.py:489
  54.6 14.0 %all-to-all-start.3 = ((f32[32,1,2304]{2,1,0:T(1,128)}), f32[32,1,2304]{2,1,0:T(1,128)S(1)}, u32[]{:S(2)}, u32[]{:S(2)}) async-start(f32[32,1,2304]{2,1,0:T(1,128)} %get-tuple-element.23), calls=%async_computation.3 | async-start | bytes 589824 | tf_op jit(solution)/shard_map/all_to_all | solution.py:436
  57.2 1.9 %collective-permute-start.3 = (f32[64,256]{1,0:T(8,128)S(1)}, f32[64,256]{1,0:T(8,128)S(1)}, u32[]{:S(2)}, u32[]{:S(2)}) collective-permute-start(f32[64,256]{1,0:T(8,128)S(1)} %get-tuple-element.25), channel_id=1, source_target_pairs={{0,1},{1,0},{2,3},{3,2},{4,5},{5,4},{6,7},{7,6},{8,9},{9,8},{10,11... | collective-permute-start | bytes 196616 | tf_op jit(solution)/shard_map/ppermute | solution.py:473
  57.4 6.9 %collective-permute-start.4 = (f32[64,256]{1,0:T(8,128)S(1)}, f32[64,256]{1,0:T(8,128)S(1)}, u32[]{:S(2)}, u32[]{:S(2)}) collective-permute-start(f32[64,256]{1,0:T(8,128)S(1)} %get-tuple-element.26), channel_id=1, source_target_pairs={{0,2},{1,3},{2,0},{3,1},{4,6},{5,7},{6,4},{7,5},{8,10},{9,11},{10,... | collective-permute-start | bytes 196616 | tf_op jit(solution)/shard_map/ppermute | solution.py:473
  59.0 5.6 %collective-permute-start.5 = (f32[64,256]{1,0:T(8,128)S(1)}, f32[64,256]{1,0:T(8,128)S(1)}, u32[]{:S(2)}, u32[]{:S(2)}) collective-permute-start(f32[64,256]{1,0:T(8,128)S(1)} %get-tuple-element.27), channel_id=1, source_target_pairs={{0,3},{1,2},{2,1},{3,0},{4,7},{5,6},{6,5},{7,4},{8,11},{9,10},{10,... | collective-permute-start | bytes 196616 | tf_op jit(solution)/shard_map/ppermute | solution.py:473

commit v3 on v2

--- a/solution.py
+++ b/solution.py
@@ -64,9 +64,9 @@
     return product(high, table[0]) + (product(high, table[1]) + product(low, table[0]))
 
 
-def small_call(kernel, name, megabytes, **kwargs):
+def small_call(kernel, megabytes, **kwargs):
     limit = pltpu.CompilerParams(vmem_limit_bytes=megabytes * 2**20)
-    return pl.pallas_call(kernel, compiler_params=limit, name=name, **kwargs)
+    return pl.pallas_call(kernel, compiler_params=limit, **kwargs)
 
 
 def in_vmem(count):
@@ -106,7 +106,6 @@
     return fours[0]
 
 
-CORNERS = pltpu.HBM
 CHUNK = 8
 UNROLL = 4
 
@@ -203,7 +202,6 @@
     blocks = outer.shape[0]
     return small_call(
         lambda *refs: core_kernel(base, *counts, *refs),
-        "core_pieces",
         8,
         out_shape=[kept((slots, 1, PIECE))] + [kept(outer.shape[1:])] * blocks,
         in_specs=in_smem(5) + anywhere(2),
@@ -265,7 +263,6 @@
     shape = (blocks[0].shape[0] * len(blocks), blocks[0].shape[1])
     return small_call(
         lambda *refs: plane_kernel(group, *refs),
-        "plane_spectrum",
         12,
         out_shape=(kept(shape), kept(shape)),
         in_specs=in_smem(1) + in_vmem(3 + len(blocks)),
@@ -300,7 +297,6 @@
 def column_hartree(values, table, device, counts):
     return small_call(
         lambda *refs: column_kernel(*counts, *refs),
-        "column_hartree",
         12,
         out_shape=kept(values.shape),
         in_specs=in_smem(1) + in_vmem(2),
@@ -360,7 +356,6 @@
     block = kept((count_x // blocks, count_y))
     return small_call(
         lambda *refs: window_kernel(fragment, *refs),
-        "plane_windows",
         12,
         out_shape=[block] * blocks + [kept((slots, 1, PLANE))],
         in_specs=in_smem(2) + in_vmem(4),
@@ -394,7 +389,6 @@
     count = len(blocks)
     return small_call(
         lambda *refs: output_kernel(base, *refs),
-        "outputs",
         4,
         out_shape=(
             jax.ShapeDtypeStruct((BOX, 1, PLANE), jnp.float32),
@@ -461,11 +455,12 @@
         def collect(pieces):
             return passed(pieces, -1)
 
-    span, occupations, orbitals, outer_density = (
+    corners = corners.T
+    arguments = [
         pltpu.with_memory_space_constraint(argument, pltpu.HBM)
-        for argument in (core_span, occupations, orbitals, outer_density)
-    )
-    corners = pltpu.with_memory_space_constraint(corners.T, CORNERS)
+        for argument in (corners, core_span, occupations, patch_sign, orbitals, outer_density)
+    ]
+    arguments[3] = patch_sign
     counts = (count_z, count_x, count_y)
 
     def swapped(blocks):
@@ -474,15 +469,14 @@
             for d, block in enumerate(blocks)
         ]
 
-    pieces, *blocks = core_pieces(
-        device, corners, span, occupations, patch_sign, orbitals, outer_density, slots, base, counts
-    )
+    pieces, *blocks = core_pieces(device, *arguments, slots, base, counts)
     blocks = swapped(blocks)
     pieces = spread(pieces)
     spectrum, density = plane_spectrum(device, pieces, group, table_x, table_y, blocks)
     chunk = (devices, deep, per_device // deep)
+    exchange = exchange_correlation(density)
+    spectrum, exchange = lax.optimization_barrier((spectrum, exchange))
     spectrum = lax.all_to_all(spectrum.reshape(chunk), AXES, 0, 0, tiled=True)
-    exchange = exchange_correlation(density)
     spectrum = column_hartree(
         spectrum.reshape(devices * deep, per_device // deep), table_z, device, counts
     )

time: 71 us -> 70.2 us (0.989)
  blocking collectives: 13.7 us -> 26.4 us
  waiting for transfers between devices: 26 us -> 16 us
  starting transfers between devices: 16.4 us -> 13.8 us
  Pallas kernels: 12.6 us -> 11.8 us
    all_to_all x1 -> x2, blocking collectives: 13.7 us -> 26.4 us  [body(): spectrum = lax.all_to_all(spectrum.reshape(chunk), AXES, 0, 0, tiled=True)]
    all_to_all x1 -> x0, waiting for transfers between devices: 10 us -> none  [body(): spectrum = lax.all_to_all(spectrum.reshape(chunk), AXES, 0, 0, tiled=True)]
    all_to_all x1 -> x0, starting transfers between devices: 2.59 us -> none  [body(): spectrum = lax.all_to_all(spectrum.reshape(chunk), AXES, 0, 0, tiled=True)]
    pallas_call x5, Pallas kernels: 12.6 us -> 11.8 us  [the longest x1 4.78 us: core_pieces(): small_call(lambda *refs: core_kernel(base, *counts, *refs), 8, out_shape=...]
  transfers between devices with their start and end apart: 9 -> 8, of which waited for: 7 -> 6; matrix products, arithmetic and copies ran while one was open for 1% -> 0% of each run, Pallas kernels for 0% -> 0%
where the time goes in v3:
time: 70.2 us; the launch traced here: 69.9 us
  blocking collectives  26.4 us (38%)
  waiting for transfers between devices  16 us (23%)
  starting transfers between devices  13.8 us (20%)
  Pallas kernels  11.8 us (17%)
  between operations  1.42 us (2%)
    all_to_all x2, blocking collectives, body(): spectrum = lax.all_to_all(spectrum.reshape(chunk), AXES, 0, 0, tiled=True)  26.4 us
    ppermute x6, waiting for transfers between devices, swapped(): lax.ppermute(block, 'sub', [(i, i ^ d) for i in range(sub_count)])  10.5 us
    all_to_all x2, starting transfers between devices, spread(): return lax.all_to_all(pieces, AXES, 0, 0, tiled=True)  9.92 us
    all_to_all x2, waiting for transfers between devices, spread(): return lax.all_to_all(pieces, AXES, 0, 0, tiled=True)  5.47 us
    pallas_call x1, Pallas kernels, core_pieces(): small_call(lambda *refs: core_kernel(base, *counts, *refs), 8, out_shape=...  4.78 us
    ppermute x6, starting transfers between devices, swapped(): lax.ppermute(block, 'sub', [(i, i ^ d) for i in range(sub_count)])  3.88 us
    pallas_call x1, Pallas kernels, plane_windows(): small_call(lambda *refs: window_kernel(fragment, *refs), 12, out_shape=[b...  3.07 us
    pallas_call x1, Pallas kernels, outputs(): small_call(lambda *refs: output_kernel(base, *refs), 4, out_shape=(jax.Sh...  1.89 us
  transfers between devices with their start and end apart: 8, of which 6 were waited for; matrix products, arithmetic and copies ran while one was open for 0% of the time, Pallas kernels for 0%

profile of v3, /device:TPU:0, one launch (start us, length us, event | category | flops | bytes accessed | tf_op | source)
XLA Modules:
  0.0 69.9 jit_solution(11230535605244607440)
XLA Ops:
  0.6 0.0 copy-start
  0.6 0.0 copy-start.1
  1.4 0.0 copy-start.2
  1.4 4.8 %shard_map.104 = (f32[32,1,1152]{2,1,0:T(1,128)}, f32[64,256]{1,0:T(8,128)S(1)}, f32[64,256]{1,0:T(8,128)S(1)}, f32[64,256]{1,0:T(8,128)S(1)}, f32[64,256]{1,0:T(8,128)S(1)}) custom-call(s32[1]{0:T(128)} %bitcast.refs_0_, s32[3,32]{1,0:T(4,128)} %bitcast.11, s32[1,6]{1,0:T(1,128)} %refs_2_.3, s32[1,16]{1,0:T(1,128)} %refs_3_.2, s32[1]{0:T(128)S(6)} %copy.11.refs_4_, ...), custom_call_target="tpu_custom_call" | custom-call | flops 40000000 | bytes 4000000 | tf_op jit(solution)/shard_map/pallas_call | solution.py:203
  6.2 7.3 %all-to-all-start = ((f32[32,1,1152]{2,1,0:T(1,128)}), f32[32,1,1152]{2,1,0:T(1,128)S(1)}, u32[]{:S(2)}, u32[]{:S(2)}) async-start(f32[32,1,1152]{2,1,0:T(1,128)} %get-tuple-element.18), calls=%async_computation | async-start | bytes 294912 | tf_op jit(solution)/shard_map/all_to_all | solution.py:430
  13.5 0.3 collective-permute-start
  13.8 1.6 %collective-permute-start.1 = (f32[64,256]{1,0:T(8,128)S(1)}, f32[64,256]{1,0:T(8,128)S(1)}, u32[]{:S(2)}, u32[]{:S(2)}) collective-permute-start(f32[64,256]{1,0:T(8,128)S(1)} %get-tuple-element.21), channel_id=1, source_target_pairs={{0,2},{1,3},{2,0},{3,1},{4,6},{5,7},{6,4},{7,5},{8,10},{9,11},{10,... | collective-permute-start | bytes 196616 | tf_op jit(solution)/shard_map/ppermute | solution.py:468
  15.4 0.0 collective-permute-start.2
  15.5 0.0 collective-permute-done.refs_5_
  15.5 3.9 %collective-permute-done.1.refs_6_ = f32[64,256]{1,0:T(8,128)S(1)} collective-permute-done((f32[64,256]{1,0:T(8,128)S(1)}, f32[64,256]{1,0:T(8,128)S(1)}, u32[]{:S(2)}, u32[]{:S(2)}) %collective-permute-start.1) | collective-permute-done | bytes 65568 | tf_op jit(solution)/shard_map/ppermute | solution.py:468
  19.4 1.0 %collective-permute-done.2.refs_7_ = f32[64,256]{1,0:T(8,128)S(1)} collective-permute-done((f32[64,256]{1,0:T(8,128)S(1)}, f32[64,256]{1,0:T(8,128)S(1)}, u32[]{:S(2)}, u32[]{:S(2)}) %collective-permute-start.2) | collective-permute-done | bytes 65568 | tf_op jit(solution)/shard_map/ppermute | solution.py:468
  20.4 1.5 %all-to-all-done.refs_1_ = f32[32,1,1152]{2,1,0:T(1,128)S(1)} async-done(((f32[32,1,1152]{2,1,0:T(1,128)}), f32[32,1,1152]{2,1,0:T(1,128)S(1)}, u32[]{:S(2)}, u32[]{:S(2)}) %all-to-all-start) | async-done | bytes 147488 | tf_op jit(solution)/shard_map/all_to_all | solution.py:430
  21.9 0.0 copy-done
  21.9 1.1 %shard_map.105 = (f32[256,256]{1,0:T(8,128)S(1)}, f32[256,256]{1,0:T(8,128)S(1)}) custom-call(s32[1]{0:T(128)} %bitcast.refs_0_, f32[32,1,1152]{2,1,0:T(1,128)S(1)} %all-to-all-done.refs_1_, bf16[2,256,256]{2,1,0:T(8,128)(2,1)S(1)} %copy-done, bf16[2,256,256]{2,1,0:T(8,128)(2,1)S(1)} %copy-done, f32[64,256]{1,0:T(8,128)S(1)} %get-tuple-element.19.refs_4_, ...), custom_call_target="tpu_custom_call" | custom-call | tf_op jit(solution)/shard_map/pallas_call | solution.py:264
  23.0 0.5 subtract_add_fusion.refs_3_
  23.6 13.7 %all_to_all.20 = f32[32,8,256]{2,1,0:T(8,128)S(1)} all-to-all(f32[32,8,256]{2,1,0:T(8,128)S(1)} %bitcast.10), channel_id=1, replica_groups=mesh['slab'=8,'sub'=4] {'slab','sub'}, dimensions={0} | all-to-all | bytes 524288 | tf_op jit(solution)/shard_map/all_to_all | solution.py:479
  37.2 0.0 copy-done.1
  37.2 0.9 %shard_map.106 = f32[256,256]{1,0:T(8,128)S(1)} custom-call(s32[1]{0:T(128)} %bitcast.refs_0_, f32[256,256]{1,0:T(8,128)S(1)} %bitcast.8, bf16[2,256,256]{2,1,0:T(8,128)(2,1)S(1)} %copy-done.1), custom_call_target="tpu_custom_call" | custom-call | tf_op jit(solution)/shard_map/pallas_call | solution.py:298
  38.2 12.8 %all_to_all.21 = f32[32,8,256]{2,1,0:T(8,128)S(1)} all-to-all(f32[32,8,256]{2,1,0:T(8,128)S(1)} %bitcast.9), channel_id=1, replica_groups=mesh['slab'=8,'sub'=4] {'slab','sub'}, dimensions={0} | all-to-all | bytes 524288 | tf_op jit(solution)/shard_map/all_to_all | solution.py:483
  51.0 0.0 copy-done.2
  51.0 3.1 %shard_map.107 = (f32[64,256]{1,0:T(8,128)S(1)}, f32[64,256]{1,0:T(8,128)S(1)}, f32[64,256]{1,0:T(8,128)S(1)}, f32[64,256]{1,0:T(8,128)S(1)}, f32[32,1,2304]{2,1,0:T(1,128)}) custom-call(s32[1]{0:T(128)} %bitcast.refs_0_, s32[3,32]{1,0:T(4,128)S(1)} %bitcast.12, f32[256,256]{1,0:T(8,128)S(1)} %bitcast.7, f32[256,256]{1,0:T(8,128)S(1)} %subtract_add_fusion.refs_3_, ...), custom_call_target="tpu_custom_call" | custom-call | tf_op jit(solution)/shard_map/pallas_call | solution.py:357
  54.0 2.6 %all-to-all-start.3 = ((f32[32,1,2304]{2,1,0:T(1,128)}), f32[32,1,2304]{2,1,0:T(1,128)S(1)}, u32[]{:S(2)}, u32[]{:S(2)}) async-start(f32[32,1,2304]{2,1,0:T(1,128)} %get-tuple-element.27), calls=%async_computation.3 | async-start | bytes 589824 | tf_op jit(solution)/shard_map/all_to_all | solution.py:430
  56.6 0.2 collective-permute-start.3
  56.8 1.6 %collective-permute-start.4 = (f32[64,256]{1,0:T(8,128)S(1)}, f32[64,256]{1,0:T(8,128)S(1)}, u32[]{:S(2)}, u32[]{:S(2)}) collective-permute-start(f32[64,256]{1,0:T(8,128)S(1)} %get-tuple-element.30), channel_id=1, source_target_pairs={{0,2},{1,3},{2,0},{3,1},{4,6},{5,7},{6,4},{7,5},{8,10},{9,11},{10,... | collective-permute-start | bytes 196616 | tf_op jit(solution)/shard_map/ppermute | solution.py:468
  58.5 0.1 collective-permute-start.5
  58.6 0.0 collective-permute-done.3.refs_4_
  58.6 5.1 %collective-permute-done.4.refs_5_ = f32[64,256]{1,0:T(8,128)S(1)} collective-permute-done((f32[64,256]{1,0:T(8,128)S(1)}, f32[64,256]{1,0:T(8,128)S(1)}, u32[]{:S(2)}, u32[]{:S(2)}) %collective-permute-start.4) | collective-permute-done | bytes 65568 | tf_op jit(solution)/shard_map/ppermute | solution.py:468
  63.7 0.4 collective-permute-done.5.refs_6_
  64.1 3.9 %all-to-all-done.3.refs_2_ = f32[32,1,2304]{2,1,0:T(1,128)S(1)} async-done(((f32[32,1,2304]{2,1,0:T(1,128)}), f32[32,1,2304]{2,1,0:T(1,128)S(1)}, u32[]{:S(2)}, u32[]{:S(2)}) %all-to-all-start.3) | async-done | bytes 294944 | tf_op jit(solution)/shard_map/all_to_all | solution.py:430
  68.0 1.9 %shard_map.108 = (f32[48,1,2304]{2,1,0:T(1,128)}, f32[4,64,256]{2,1,0:T(8,128)}) custom-call(s32[1]{0:T(128)} %bitcast.refs_0_, s32[3,32]{1,0:T(4,128)S(1)} %bitcast.13, f32[32,1,2304]{2,1,0:T(1,128)S(1)} %all-to-all-done.3.refs_2_, f32[64,256]{1,0:T(8,128)S(1)} %get-tuple-element.28.refs_3_, f32[64,256]{1,0:T(8,128)S(1)} %collective-permute-done.3.refs_4_, ...), custom_call_target="tpu_custom_call" | custom-call | tf_op jit(solution)/shard_map/pallas_call | solution.py:390
Async XLA Ops:
  0.6 21.3 %copy-start = (bf16[2,256,256]{2,1,0:T(8,128)(2,1)S(1)}, bf16[2,256,256]{2,1,0:T(8,128)(2,1)}, u32[]{:S(2)}) copy-start(bf16[2,256,256]{2,1,0:T(8,128)(2,1)} %constant.31.clone.refs_2_.refs_3_.refs_4_.refs_5_) | copy-start | bytes 786436
  0.6 36.6 %copy-start.1 = (bf16[2,256,256]{2,1,0:T(8,128)(2,1)S(1)}, bf16[2,256,256]{2,1,0:T(8,128)(2,1)}, u32[]{:S(2)}) copy-start(bf16[2,256,256]{2,1,0:T(8,128)(2,1)} %constant.32.clone.refs_2_) | copy-start | bytes 786436
  1.4 49.6 %copy-start.2 = (s32[32,3]{0,1:T(4,128)S(1)}, s32[32,3]{0,1:T(4,128)}, u32[]{:S(2)}) copy-start(s32[32,3]{0,1:T(4,128)} %param.12) | copy-start | bytes 1156
  6.2 15.8 %all-to-all-start = ((f32[32,1,1152]{2,1,0:T(1,128)}), f32[32,1,1152]{2,1,0:T(1,128)S(1)}, u32[]{:S(2)}, u32[]{:S(2)}) async-start(f32[32,1,1152]{2,1,0:T(1,128)} %get-tuple-element.18), calls=%async_computation | async-start | bytes 294912 | tf_op jit(solution)/shard_map/all_to_all | solution.py:430
  13.5 2.0 %collective-permute-start = (f32[64,256]{1,0:T(8,128)S(1)}, f32[64,256]{1,0:T(8,128)S(1)}, u32[]{:S(2)}, u32[]{:S(2)}) collective-permute-start(f32[64,256]{1,0:T(8,128)S(1)} %get-tuple-element.20), channel_id=1, source_target_pairs={{0,1},{1,0},{2,3},{3,2},{4,5},{5,4},{6,7},{7,6},{8,9},{9,8},{10,11... | collective-permute-start | bytes 196616 | tf_op jit(solution)/shard_map/ppermute | solution.py:468
  13.8 5.6 %collective-permute-start.1 = (f32[64,256]{1,0:T(8,128)S(1)}, f32[64,256]{1,0:T(8,128)S(1)}, u32[]{:S(2)}, u32[]{:S(2)}) collective-permute-start(f32[64,256]{1,0:T(8,128)S(1)} %get-tuple-element.21), channel_id=1, source_target_pairs={{0,2},{1,3},{2,0},{3,1},{4,6},{5,7},{6,4},{7,5},{8,10},{9,11},{10,... | collective-permute-start | bytes 196616 | tf_op jit(solution)/shard_map/ppermute | solution.py:468
  15.4 5.0 %collective-permute-start.2 = (f32[64,256]{1,0:T(8,128)S(1)}, f32[64,256]{1,0:T(8,128)S(1)}, u32[]{:S(2)}, u32[]{:S(2)}) collective-permute-start(f32[64,256]{1,0:T(8,128)S(1)} %get-tuple-element.22), channel_id=1, source_target_pairs={{0,3},{1,2},{2,1},{3,0},{4,7},{5,6},{6,5},{7,4},{8,11},{9,10},{10,... | collective-permute-start | bytes 196616 | tf_op jit(solution)/shard_map/ppermute | solution.py:468
  54.0 14.0 %all-to-all-start.3 = ((f32[32,1,2304]{2,1,0:T(1,128)}), f32[32,1,2304]{2,1,0:T(1,128)S(1)}, u32[]{:S(2)}, u32[]{:S(2)}) async-start(f32[32,1,2304]{2,1,0:T(1,128)} %get-tuple-element.27), calls=%async_computation.3 | async-start | bytes 589824 | tf_op jit(solution)/shard_map/all_to_all | solution.py:430
  56.6 1.9 %collective-permute-start.3 = (f32[64,256]{1,0:T(8,128)S(1)}, f32[64,256]{1,0:T(8,128)S(1)}, u32[]{:S(2)}, u32[]{:S(2)}) collective-permute-start(f32[64,256]{1,0:T(8,128)S(1)} %get-tuple-element.29), channel_id=1, source_target_pairs={{0,1},{1,0},{2,3},{3,2},{4,5},{5,4},{6,7},{7,6},{8,9},{9,8},{10,11... | collective-permute-start | bytes 196616 | tf_op jit(solution)/shard_map/ppermute | solution.py:468
  56.8 6.9 %collective-permute-start.4 = (f32[64,256]{1,0:T(8,128)S(1)}, f32[64,256]{1,0:T(8,128)S(1)}, u32[]{:S(2)}, u32[]{:S(2)}) collective-permute-start(f32[64,256]{1,0:T(8,128)S(1)} %get-tuple-element.30), channel_id=1, source_target_pairs={{0,2},{1,3},{2,0},{3,1},{4,6},{5,7},{6,4},{7,5},{8,10},{9,11},{10,... | collective-permute-start | bytes 196616 | tf_op jit(solution)/shard_map/ppermute | solution.py:468
  58.5 5.6 %collective-permute-start.5 = (f32[64,256]{1,0:T(8,128)S(1)}, f32[64,256]{1,0:T(8,128)S(1)}, u32[]{:S(2)}, u32[]{:S(2)}) collective-permute-start(f32[64,256]{1,0:T(8,128)S(1)} %get-tuple-element.31), channel_id=1, source_target_pairs={{0,3},{1,2},{2,1},{3,0},{4,7},{5,6},{6,5},{7,4},{8,11},{9,10},{10,... | collective-permute-start | bytes 196616 | tf_op jit(solution)/shard_map/ppermute | solution.py:468

commit v4 on v3

--- a/solution.py
+++ b/solution.py
@@ -106,37 +106,61 @@
     return fours[0]
 
 
-CHUNK = 8
-UNROLL = 4
-
-
-def core_kernel(
-    base, depth, count_x, count_y, device, corners, span, occupations, sign, orbitals, outer, out,
-    *refs,
-):
-    *blocks, buffer, sums, rows, arrived, filled = refs
-    own, slots, orbital_count = device[0], out.shape[0], orbitals.shape[1]
-    first_z, first_x, first_y = span[0, 0], span[0, 1], span[0, 2]
-    len_z, len_x, len_y = span[0, 3], span[0, 4], span[0, 5]
-    begin = jnp.minimum(first_z, BOX - CORE)
-    chunks = CORE // CHUNK
-    copies = [
-        pltpu.make_async_copy(
-            orbitals.at[0, :, pl.ds(pl.multiple_of((begin + c * CHUNK) * PLANE, LANES), CHUNK * PLANE)],
-            buffer.at[c],
-            arrived.at[c],
-        )
-        for c in range(chunks)
-    ]
-    for copy in copies:
-        copy.start()
-    sub = lax.rem(own, len(blocks))
+def block_kernel(device, outer, *refs):
+    *blocks, filled = refs
+    sub = lax.rem(device[0], len(blocks))
     fills = [
         pltpu.make_async_copy(outer.at[sub ^ d], block, filled.at[d])
         for d, block in enumerate(blocks)
     ]
     for fill in fills:
         fill.start()
+    for fill in fills:
+        fill.wait()
+
+
+def outer_blocks(device, outer):
+    count = outer.shape[0]
+    return small_call(
+        block_kernel,
+        4,
+        out_shape=[kept(outer.shape[1:])] * count,
+        in_specs=in_smem(1) + anywhere(1),
+        out_specs=in_vmem(count),
+        scratch_shapes=[pltpu.SemaphoreType.DMA((count,))],
+    )(device, outer)
+
+
+CHUNK = 8
+UNROLL = 4
+
+
+def core_kernel(
+    base, depth, count_x, count_y, device, sign, corner_table, span_row, occupation_row, orbitals,
+    out, buffer, sums, rows, corners, span, occupations, arrived, staged,
+):
+    own, slots, orbital_count = device[0], out.shape[0], orbitals.shape[1]
+    scalars = [
+        pltpu.make_async_copy(source, target, staged.at[n])
+        for n, (source, target) in enumerate(
+            [(span_row, span), (occupation_row, occupations), (corner_table, corners)]
+        )
+    ]
+    for copy in scalars:
+        copy.start()
+    chunks = BOX // CHUNK
+    copies = []
+    for c in range(chunks):
+        part = pl.ds(c * CHUNK * PLANE, CHUNK * PLANE)
+        copies.append(
+            pltpu.make_async_copy(orbitals.at[0, :, part], buffer.at[:, part], arrived.at[c])
+        )
+        copies[c].start()
+    for copy in scalars:
+        copy.wait()
+    first_z, first_x, first_y = span[0, 0], span[0, 1], span[0, 2]
+    len_z, len_x, len_y = span[0, 3], span[0, 4], span[0, 5]
+    begin = jnp.minimum(first_z, BOX - CORE)
     orbital = lax.broadcasted_iota(jnp.int32, (orbital_count, LANES), 0)
     weight = jnp.zeros((orbital_count, LANES), jnp.int32)
     for o in range(orbital_count):
@@ -144,15 +168,19 @@
     weight = (weight * sign[0]).astype(jnp.float32)
     groups = CHUNK * GROUPS // 8
     tiles = WIDE // LANES
-    for c in range(chunks):
+    ahead = chunks - CORE // CHUNK
+    for c in range(ahead):
         copies[c].wait()
+    for c in range(CORE // CHUNK):
+        copies[c + ahead].wait()
 
         def add_rows(b, carry, c=c):
             for q in range(tiles):
                 cells = []
                 for s in range(8):
-                    lane = pl.multiple_of((8 * b + s) * WIDE + q * LANES, LANES)
-                    values = buffer[c, :, pl.ds(lane, LANES)].astype(jnp.float32)
+                    line = begin * GROUPS + (c * groups + b) * 8 + s
+                    lane = pl.multiple_of(line * WIDE + q * LANES, LANES)
+                    values = buffer[:, pl.ds(lane, LANES)].astype(jnp.float32)
                     values = values * values * weight
                     cells.append(sum(values[8 * h : 8 * h + 8] for h in range(orbital_count // 8)))
                 at = pl.multiple_of((c * groups + b) * 8, 8)
@@ -193,28 +221,28 @@
         return carry
 
     lax.fori_loop(0, slots // UNROLL, pack, 0)
-    for fill in fills:
-        fill.wait()
-
-
-def core_pieces(device, corners, span, occupations, sign, orbitals, outer, slots, base, counts):
+
+
+def core_pieces(device, sign, corners, span, occupations, orbitals, slots, base, counts):
     orbital_count = orbitals.shape[1]
-    blocks = outer.shape[0]
     return small_call(
         lambda *refs: core_kernel(base, *counts, *refs),
         8,
-        out_shape=[kept((slots, 1, PIECE))] + [kept(outer.shape[1:])] * blocks,
-        in_specs=in_smem(5) + anywhere(2),
-        out_specs=in_vmem(1 + blocks),
+        out_shape=kept((slots, 1, PIECE)),
+        in_specs=in_smem(2) + anywhere(4),
+        out_specs=in_vmem(1)[0],
         scratch_shapes=[
-            pltpu.VMEM((CORE // CHUNK, orbital_count, CHUNK * PLANE), orbitals.dtype),
+            pltpu.VMEM((orbital_count, BOX * PLANE), orbitals.dtype),
             pltpu.VMEM((CORE * GROUPS, WIDE), jnp.float32),
             pltpu.VMEM((CORE * BOX + CORE, LANES), jnp.float32),
-            pltpu.SemaphoreType.DMA((CORE // CHUNK,)),
-            pltpu.SemaphoreType.DMA((blocks,)),
+            pltpu.SMEM(corners.shape, jnp.int32),
+            pltpu.SMEM(span.shape, jnp.int32),
+            pltpu.SMEM(occupations.shape, jnp.int32),
+            pltpu.SemaphoreType.DMA((BOX // CHUNK,)),
+            pltpu.SemaphoreType.DMA((3,)),
         ],
         cost_estimate=pl.CostEstimate(flops=40_000_000, bytes_accessed=4_000_000, transcendentals=0),
-    )(device, corners, span, occupations, sign, orbitals, outer)
+    )(device, sign, corners, span, occupations, orbitals)
 
 
 def plane_kernel(group, device, pieces, table_x, table_y, *refs):
@@ -304,8 +332,10 @@
     )(device, values, table)
 
 
-def window_kernel(fragment, device, corners, spectrum, exchange, table_x, table_y, *refs):
-    *blocks, out, wide, cut = refs
+def window_kernel(fragment, device, corner_table, spectrum, exchange, table_x, table_y, *refs):
+    *blocks, out, wide, cut, corners, staged = refs
+    scalars = pltpu.make_async_copy(corner_table, corners, staged)
+    scalars.start()
     slots = out.shape[0]
     count_x, count_y = spectrum.shape
     x_dev = count_x // len(blocks)
@@ -322,6 +352,7 @@
             at = pl.multiple_of(t * tall + (sub ^ d) * x_dev, 8)
             block[:, t * LANES : (t + 1) * LANES] = wide[pl.ds(at, x_dev), :]
     lane = lax.broadcasted_iota(jnp.int32, (BOX, LANES), 1)
+    scalars.wait()
 
     def cut_windows(step, carry):
         turned = []
@@ -358,11 +389,13 @@
         lambda *refs: window_kernel(fragment, *refs),
         12,
         out_shape=[block] * blocks + [kept((slots, 1, PLANE))],
-        in_specs=in_smem(2) + in_vmem(4),
+        in_specs=in_smem(1) + anywhere(1) + in_vmem(4),
         out_specs=in_vmem(blocks + 1),
         scratch_shapes=[
             pltpu.VMEM((count_y // LANES * (count_x + BOX), LANES), jnp.float32),
             pltpu.VMEM((slots * BOX, LANES), jnp.float32),
+            pltpu.SMEM(corners.shape, jnp.int32),
+            pltpu.SemaphoreType.DMA,
         ],
     )(device, corners, spectrum, exchange, table_x, table_y)
 
@@ -370,7 +403,9 @@
 def output_kernel(base, device, corners, windows, *refs):
     *blocks, box, potential, copied = refs
     depth = windows.shape[0]
-    first = corners[0, device[0]] - base(device[0])
+    row = corners[0:1, :]
+    own = lax.broadcasted_iota(jnp.int32, row.shape, 1) == device[0]
+    first = jnp.sum(jnp.where(own, row, 0)) - base(device[0])
     sub = lax.rem(device[0], len(blocks))
     copies = [
         pltpu.make_async_copy(block, potential.at[sub ^ d], copied.at[BOX + d])
@@ -394,7 +429,7 @@
             jax.ShapeDtypeStruct((BOX, 1, PLANE), jnp.float32),
             jax.ShapeDtypeStruct((count,) + blocks[0].shape, jnp.float32),
         ),
-        in_specs=in_smem(2) + anywhere(1 + count),
+        in_specs=in_smem(1) + in_vmem(1) + anywhere(1 + count),
         out_specs=tuple(anywhere(2)),
         scratch_shapes=[pltpu.SemaphoreType.DMA((BOX + count,))],
     )(device, corners, windows, *blocks)
@@ -455,13 +490,12 @@
         def collect(pieces):
             return passed(pieces, -1)
 
+    counts = (count_z, count_x, count_y)
     corners = corners.T
     arguments = [
         pltpu.with_memory_space_constraint(argument, pltpu.HBM)
-        for argument in (corners, core_span, occupations, patch_sign, orbitals, outer_density)
+        for argument in (corners, core_span, occupations, orbitals, outer_density)
     ]
-    arguments[3] = patch_sign
-    counts = (count_z, count_x, count_y)
 
     def swapped(blocks):
         return [
@@ -469,8 +503,10 @@
             for d, block in enumerate(blocks)
         ]
 
-    pieces, *blocks = core_pieces(device, *arguments, slots, base, counts)
+    blocks = outer_blocks(device, arguments.pop())
     blocks = swapped(blocks)
+    pieces = core_pieces(device, patch_sign, *arguments, slots, base, counts)
+    pieces, blocks = lax.optimization_barrier((pieces, blocks))
     pieces = spread(pieces)
     spectrum, density = plane_spectrum(device, pieces, group, table_x, table_y, blocks)
     chunk = (devices, deep, per_device // deep)

time: 70.2 us -> 69.6 us (level)
  blocking collectives: 26.4 us -> 39.6 us
  waiting for transfers between devices: 16 us -> 9.47 us
  starting transfers between devices: 13.8 us -> 7.68 us
  Pallas kernels: 11.8 us -> 10.6 us
    all_to_all x0 -> x1, blocking collectives: none -> 14.3 us  [spread(): return lax.all_to_all(pieces, AXES, 0, 0, tiled=True)]
    all_to_all x2 -> x1, starting transfers between devices: 9.92 us -> 2.61 us  [spread(): return lax.all_to_all(pieces, AXES, 0, 0, tiled=True)]
    ppermute x6, waiting for transfers between devices: 10.5 us -> 5.53 us  [swapped(): lax.ppermute(block, 'sub', [(i, i ^ d) for i in range(sub_count)])]
    all_to_all x2 -> x1, waiting for transfers between devices: 5.47 us -> 3.95 us  [spread(): return lax.all_to_all(pieces, AXES, 0, 0, tiled=True)]
    ppermute x6, starting transfers between devices: 3.88 us -> 5.08 us  [swapped(): lax.ppermute(block, 'sub', [(i, i ^ d) for i in range(sub_count)])]
    all_to_all x2, blocking collectives: 26.4 us -> 25.3 us  [body(): spectrum = lax.all_to_all(spectrum.reshape(chunk), AXES, 0, 0, tiled=True)]
    pallas_call x1, Pallas kernels: 4.78 us -> 3.69 us  [core_pieces(): small_call(lambda *refs: core_kernel(base, *counts, *refs), 8, out_shape=...]
    pallas_call x0 -> x1, Pallas kernels: none -> 1.03 us  [outer_blocks(): small_call(block_kernel, 4, out_shape=[kept(outer.shape[1:])] * count, in...]
  transfers between devices with their start and end apart: 8 -> 7, of which waited for: 6 -> 3; matrix products, arithmetic and copies ran while one was open for 0% -> 0% of each run, Pallas kernels for 0% -> 5%
where the time goes in v4:
time: 69.6 us; the launch traced here: 69.3 us
  blocking collectives  39.6 us (57%)
  Pallas kernels  10.6 us (15%)
  waiting for transfers between devices  9.47 us (14%)
  starting transfers between devices  7.68 us (11%)
  between operations  1.39 us (2%)
    all_to_all x2, blocking collectives, body(): spectrum = lax.all_to_all(spectrum.reshape(chunk), AXES, 0, 0, tiled=True)  25.3 us
    all_to_all x1, blocking collectives, spread(): return lax.all_to_all(pieces, AXES, 0, 0, tiled=True)  14.3 us
    ppermute x6, waiting for transfers between devices, swapped(): lax.ppermute(block, 'sub', [(i, i ^ d) for i in range(sub_count)])  5.53 us
    ppermute x6, starting transfers between devices, swapped(): lax.ppermute(block, 'sub', [(i, i ^ d) for i in range(sub_count)])  5.08 us
    all_to_all x1, waiting for transfers between devices, spread(): return lax.all_to_all(pieces, AXES, 0, 0, tiled=True)  3.95 us
    pallas_call x1, Pallas kernels, core_pieces(): small_call(lambda *refs: core_kernel(base, *counts, *refs), 8, out_shape=...  3.69 us
    all_to_all x1, starting transfers between devices, spread(): return lax.all_to_all(pieces, AXES, 0, 0, tiled=True)  2.61 us
    pallas_call x1, Pallas kernels, plane_windows(): small_call(lambda *refs: window_kernel(fragment, *refs), 12, out_shape=[b...  2.53 us
  transfers between devices with their start and end apart: 7, of which 3 were waited for; matrix products, arithmetic and copies ran while one was open for 0% of the time, Pallas kernels for 5%

profile of v4, /device:TPU:0, one launch (start us, length us, event | category | flops | bytes accessed | tf_op | source)
XLA Modules:
  0.0 69.3 jit_solution(2138339158420389719)
XLA Ops:
  0.6 0.0 copy-start
  0.6 0.0 copy-start.1
  0.7 1.0 %shard_map.105 = (f32[64,256]{1,0:T(8,128)S(1)}, f32[64,256]{1,0:T(8,128)S(1)}, f32[64,256]{1,0:T(8,128)S(1)}, f32[64,256]{1,0:T(8,128)S(1)}) custom-call(s32[1]{0:T(128)} %bitcast.refs_0_.device, f32[4,64,256]{2,1,0:T(8,128)} %outer.1), custom_call_target="tpu_custom_call" | custom-call | tf_op jit(solution)/shard_map/pallas_call | solution.py:124
  1.7 0.6 collective-permute-start
  2.3 2.6 %collective-permute-start.1 = (f32[64,256]{1,0:T(8,128)S(1)}, f32[64,256]{1,0:T(8,128)S(1)}, u32[]{:S(2)}, u32[]{:S(2)}) collective-permute-start(f32[64,256]{1,0:T(8,128)S(1)} %get-tuple-element.24), channel_id=1, source_target_pairs={{0,2},{1,3},{2,0},{3,1},{4,6},{5,7},{6,4},{7,5},{8,10},{9,11},{10,... | collective-permute-start | bytes 196616 | tf_op jit(solution)/shard_map/ppermute | solution.py:502
  4.8 0.0 collective-permute-start.2
  5.5 0.0 copy-start.2
  5.5 3.7 %shard_map.104 = f32[32,1,1152]{2,1,0:T(1,128)S(1)} custom-call(s32[1]{0:T(128)} %bitcast.refs_0_.device, s32[1]{0:T(128)S(6)} %copy.11.refs_1_, s32[3,32]{1,0:T(4,128)} %bitcast.11, s32[1,6]{1,0:T(1,128)} %refs_3_.2, s32[1,16]{1,0:T(1,128)} %refs_4_.2, bf16[1,16,110592]{2,1,0:T(8,128)(2,1)} %refs_5_.2), custom_call_target="tpu_custom_call" | custom-call | flops 40000000 | bytes 4000000 | tf_op jit(solution)/shard_map/pallas_call | solution.py:228
  9.2 0.0 collective-permute-done.refs_5_
  9.2 0.0 collective-permute-done.1.refs_6_
  9.2 0.0 collective-permute-done.2.refs_7_
  9.2 14.3 %all_to_all.20.refs_1_ = f32[32,1,1152]{2,1,0:T(1,128)S(1)} all-to-all(f32[32,1,1152]{2,1,0:T(1,128)S(1)} %shard_map.104), channel_id=1, replica_groups=mesh['slab'=8,'sub'=4] {'slab','sub'}, dimensions={0} | all-to-all | bytes 294912 | tf_op jit(solution)/shard_map/all_to_all | solution.py:465
  23.6 0.0 copy-done
  23.6 1.1 %shard_map.106 = (f32[256,256]{1,0:T(8,128)S(1)}, f32[256,256]{1,0:T(8,128)S(1)}) custom-call(s32[1]{0:T(128)} %bitcast.refs_0_.device, f32[32,1,1152]{2,1,0:T(1,128)S(1)} %all_to_all.20.refs_1_, bf16[2,256,256]{2,1,0:T(8,128)(2,1)S(1)} %copy-done, bf16[2,256,256]{2,1,0:T(8,128)(2,1)S(1)} %copy-done, f32[64,256]{1,0:T(8,128)S(1)} %get-tuple-element.27.refs_4_, ...), custom_call_target="tpu_custom_call" | custom-call | tf_op jit(solution)/shard_map/pallas_call | solution.py:292
  24.6 0.5 subtract_add_fusion.refs_3_
  25.2 12.5 %all_to_all.21 = f32[32,8,256]{2,1,0:T(8,128)S(1)} all-to-all(f32[32,8,256]{2,1,0:T(8,128)S(1)} %bitcast.10), channel_id=1, replica_groups=mesh['slab'=8,'sub'=4] {'slab','sub'}, dimensions={0} | all-to-all | bytes 524288 | tf_op jit(solution)/shard_map/all_to_all | solution.py:515
  37.7 0.0 copy-done.1
  37.7 0.9 %shard_map.107 = f32[256,256]{1,0:T(8,128)S(1)} custom-call(s32[1]{0:T(128)} %bitcast.refs_0_.device, f32[256,256]{1,0:T(8,128)S(1)} %bitcast.8, bf16[2,256,256]{2,1,0:T(8,128)(2,1)S(1)} %copy-done.1), custom_call_target="tpu_custom_call" | custom-call | tf_op jit(solution)/shard_map/pallas_call | solution.py:326
  38.6 12.8 %all_to_all.22 = f32[32,8,256]{2,1,0:T(8,128)S(1)} all-to-all(f32[32,8,256]{2,1,0:T(8,128)S(1)} %bitcast.9), channel_id=1, replica_groups=mesh['slab'=8,'sub'=4] {'slab','sub'}, dimensions={0} | all-to-all | bytes 524288 | tf_op jit(solution)/shard_map/all_to_all | solution.py:519
  51.4 0.0 copy-done.2
  51.4 2.5 %shard_map.108 = (f32[64,256]{1,0:T(8,128)S(1)}, f32[64,256]{1,0:T(8,128)S(1)}, f32[64,256]{1,0:T(8,128)S(1)}, f32[64,256]{1,0:T(8,128)S(1)}, f32[32,1,2304]{2,1,0:T(1,128)}) custom-call(s32[1]{0:T(128)} %bitcast.refs_0_.device, s32[3,32]{1,0:T(4,128)S(1)} %bitcast.12, f32[256,256]{1,0:T(8,128)S(1)} %bitcast.7, f32[256,256]{1,0:T(8,128)S(1)} %subtract_add_fusion.refs_3_, ...), custom_call_target="tpu_custom_call" | custom-call | tf_op jit(solution)/shard_map/pallas_call | solution.py:388
  53.9 2.6 %all-to-all-start.3 = ((f32[32,1,2304]{2,1,0:T(1,128)}), f32[32,1,2304]{2,1,0:T(1,128)S(1)}, u32[]{:S(2)}, u32[]{:S(2)}) async-start(f32[32,1,2304]{2,1,0:T(1,128)} %get-tuple-element.35), calls=%async_computation.3 | async-start | bytes 589824 | tf_op jit(solution)/shard_map/all_to_all | solution.py:465
  56.6 0.2 collective-permute-start.3
  56.7 1.6 %collective-permute-start.4 = (f32[64,256]{1,0:T(8,128)S(1)}, f32[64,256]{1,0:T(8,128)S(1)}, u32[]{:S(2)}, u32[]{:S(2)}) collective-permute-start(f32[64,256]{1,0:T(8,128)S(1)} %get-tuple-element.38), channel_id=1, source_target_pairs={{0,2},{1,3},{2,0},{3,1},{4,6},{5,7},{6,4},{7,5},{8,10},{9,11},{10,... | collective-permute-start | bytes 196616 | tf_op jit(solution)/shard_map/ppermute | solution.py:502
  58.4 0.1 collective-permute-start.5
  58.5 0.0 collective-permute-done.3.refs_4_
  58.5 5.1 %collective-permute-done.4.refs_5_ = f32[64,256]{1,0:T(8,128)S(1)} collective-permute-done((f32[64,256]{1,0:T(8,128)S(1)}, f32[64,256]{1,0:T(8,128)S(1)}, u32[]{:S(2)}, u32[]{:S(2)}) %collective-permute-start.4) | collective-permute-done | bytes 65568 | tf_op jit(solution)/shard_map/ppermute | solution.py:502
  63.6 0.4 collective-permute-done.5.refs_6_
  64.0 3.9 %all-to-all-done.3.refs_2_ = f32[32,1,2304]{2,1,0:T(1,128)S(1)} async-done(((f32[32,1,2304]{2,1,0:T(1,128)}), f32[32,1,2304]{2,1,0:T(1,128)S(1)}, u32[]{:S(2)}, u32[]{:S(2)}) %all-to-all-start.3) | async-done | bytes 294944 | tf_op jit(solution)/shard_map/all_to_all | solution.py:465
  68.0 1.4 %shard_map.109 = (f32[48,1,2304]{2,1,0:T(1,128)}, f32[4,64,256]{2,1,0:T(8,128)}) custom-call(s32[1]{0:T(128)} %bitcast.refs_0_.device, s32[3,32]{1,0:T(4,128)S(1)} %bitcast.13, f32[32,1,2304]{2,1,0:T(1,128)S(1)} %all-to-all-done.3.refs_2_, f32[64,256]{1,0:T(8,128)S(1)} %get-tuple-element.36.refs_3_, f32[64,256]{1,0:T(8,128)S(1)} %collective-permute-done.3.refs_4_, ...), custom_call_target="tpu_custom_call" | custom-call | tf_op jit(solution)/shard_map/pallas_call | solution.py:425
Async XLA Ops:
  0.6 22.9 %copy-start = (bf16[2,256,256]{2,1,0:T(8,128)(2,1)S(1)}, bf16[2,256,256]{2,1,0:T(8,128)(2,1)}, u32[]{:S(2)}) copy-start(bf16[2,256,256]{2,1,0:T(8,128)(2,1)} %constant.31.clone.refs_2_.refs_3_.refs_4_.refs_5_) | copy-start | bytes 786436
  0.6 37.0 %copy-start.1 = (bf16[2,256,256]{2,1,0:T(8,128)(2,1)S(1)}, bf16[2,256,256]{2,1,0:T(8,128)(2,1)}, u32[]{:S(2)}) copy-start(bf16[2,256,256]{2,1,0:T(8,128)(2,1)} %constant.32.clone.refs_2_) | copy-start | bytes 786436
  1.7 7.5 %collective-permute-start = (f32[64,256]{1,0:T(8,128)S(1)}, f32[64,256]{1,0:T(8,128)S(1)}, u32[]{:S(2)}, u32[]{:S(2)}) collective-permute-start(f32[64,256]{1,0:T(8,128)S(1)} %get-tuple-element.23), channel_id=1, source_target_pairs={{0,1},{1,0},{2,3},{3,2},{4,5},{5,4},{6,7},{7,6},{8,9},{9,8},{10,11... | collective-permute-start | bytes 196616 | tf_op jit(solution)/shard_map/ppermute | solution.py:502
  2.3 7.0 %collective-permute-start.1 = (f32[64,256]{1,0:T(8,128)S(1)}, f32[64,256]{1,0:T(8,128)S(1)}, u32[]{:S(2)}, u32[]{:S(2)}) collective-permute-start(f32[64,256]{1,0:T(8,128)S(1)} %get-tuple-element.24), channel_id=1, source_target_pairs={{0,2},{1,3},{2,0},{3,1},{4,6},{5,7},{6,4},{7,5},{8,10},{9,11},{10,... | collective-permute-start | bytes 196616 | tf_op jit(solution)/shard_map/ppermute | solution.py:502
  4.8 4.4 %collective-permute-start.2 = (f32[64,256]{1,0:T(8,128)S(1)}, f32[64,256]{1,0:T(8,128)S(1)}, u32[]{:S(2)}, u32[]{:S(2)}) collective-permute-start(f32[64,256]{1,0:T(8,128)S(1)} %get-tuple-element.25), channel_id=1, source_target_pairs={{0,3},{1,2},{2,1},{3,0},{4,7},{5,6},{6,5},{7,4},{8,11},{9,10},{10,... | collective-permute-start | bytes 196616 | tf_op jit(solution)/shard_map/ppermute | solution.py:502
  5.5 45.9 %copy-start.2 = (s32[32,3]{0,1:T(4,128)S(1)}, s32[32,3]{0,1:T(4,128)}, u32[]{:S(2)}) copy-start(s32[32,3]{0,1:T(4,128)} %param.12) | copy-start | bytes 1156
  53.9 14.0 %all-to-all-start.3 = ((f32[32,1,2304]{2,1,0:T(1,128)}), f32[32,1,2304]{2,1,0:T(1,128)S(1)}, u32[]{:S(2)}, u32[]{:S(2)}) async-start(f32[32,1,2304]{2,1,0:T(1,128)} %get-tuple-element.35), calls=%async_computation.3 | async-start | bytes 589824 | tf_op jit(solution)/shard_map/all_to_all | solution.py:465
  56.6 1.9 %collective-permute-start.3 = (f32[64,256]{1,0:T(8,128)S(1)}, f32[64,256]{1,0:T(8,128)S(1)}, u32[]{:S(2)}, u32[]{:S(2)}) collective-permute-start(f32[64,256]{1,0:T(8,128)S(1)} %get-tuple-element.37), channel_id=1, source_target_pairs={{0,1},{1,0},{2,3},{3,2},{4,5},{5,4},{6,7},{7,6},{8,9},{9,8},{10,11... | collective-permute-start | bytes 196616 | tf_op jit(solution)/shard_map/ppermute | solution.py:502
  56.7 6.9 %collective-permute-start.4 = (f32[64,256]{1,0:T(8,128)S(1)}, f32[64,256]{1,0:T(8,128)S(1)}, u32[]{:S(2)}, u32[]{:S(2)}) collective-permute-start(f32[64,256]{1,0:T(8,128)S(1)} %get-tuple-element.38), channel_id=1, source_target_pairs={{0,2},{1,3},{2,0},{3,1},{4,6},{5,7},{6,4},{7,5},{8,10},{9,11},{10,... | collective-permute-start | bytes 196616 | tf_op jit(solution)/shard_map/ppermute | solution.py:502
  58.4 5.6 %collective-permute-start.5 = (f32[64,256]{1,0:T(8,128)S(1)}, f32[64,256]{1,0:T(8,128)S(1)}, u32[]{:S(2)}, u32[]{:S(2)}) collective-permute-start(f32[64,256]{1,0:T(8,128)S(1)} %get-tuple-element.39), channel_id=1, source_target_pairs={{0,3},{1,2},{2,1},{3,0},{4,7},{5,6},{6,5},{7,4},{8,11},{9,10},{10,... | collective-permute-start | bytes 196616 | tf_op jit(solution)/shard_map/ppermute | solution.py:502

commit v5 on v4

--- a/solution.py
+++ b/solution.py
@@ -26,10 +26,11 @@
 
 def exchange_correlation(density):
     clipped = jnp.maximum(density, floor_density)
-    radius = jnp.cbrt(3.0 / (4.0 * math.pi * clipped))
-    exchange = -jnp.cbrt(3.0 * clipped / math.pi)
-    correlation = -0.44 / (radius + 7.8) - 0.44 * radius / (3.0 * (radius + 7.8) ** 2)
-    return exchange + correlation
+    root = jnp.exp(jnp.log(clipped) * (1.0 / 3.0))
+    radius = (0.75 / math.pi) ** (1.0 / 3.0) / root
+    exchange = -((3.0 / math.pi) ** (1.0 / 3.0)) * root
+    inverse = 1.0 / (radius + 7.8)
+    return exchange - 0.44 * inverse - (0.44 / 3.0) * radius * inverse * inverse
 
 
 def split_table(table):
@@ -136,7 +137,7 @@
 
 
 def core_kernel(
-    base, depth, count_x, count_y, device, sign, corner_table, span_row, occupation_row, orbitals,
+    base, depth, count_x, count_y, device, corner_table, span_row, occupation_row, orbitals,
     out, buffer, sums, rows, corners, span, occupations, arrived, staged,
 ):
     own, slots, orbital_count = device[0], out.shape[0], orbitals.shape[1]
@@ -165,7 +166,10 @@
     weight = jnp.zeros((orbital_count, LANES), jnp.int32)
     for o in range(orbital_count):
         weight = jnp.where(orbital == o, occupations[0, o], weight)
-    weight = (weight * sign[0]).astype(jnp.float32)
+    sign = 1
+    for length in (len_z, len_x, len_y):
+        sign = jnp.where(length == CORE, sign, -sign)
+    weight = (weight * sign).astype(jnp.float32)
     groups = CHUNK * GROUPS // 8
     tiles = WIDE // LANES
     ahead = chunks - CORE // CHUNK
@@ -223,13 +227,13 @@
     lax.fori_loop(0, slots // UNROLL, pack, 0)
 
 
-def core_pieces(device, sign, corners, span, occupations, orbitals, slots, base, counts):
+def core_pieces(device, corners, span, occupations, orbitals, slots, base, counts):
     orbital_count = orbitals.shape[1]
     return small_call(
         lambda *refs: core_kernel(base, *counts, *refs),
         8,
         out_shape=kept((slots, 1, PIECE)),
-        in_specs=in_smem(2) + anywhere(4),
+        in_specs=in_smem(1) + anywhere(4),
         out_specs=in_vmem(1)[0],
         scratch_shapes=[
             pltpu.VMEM((orbital_count, BOX * PLANE), orbitals.dtype),
@@ -242,11 +246,11 @@
             pltpu.SemaphoreType.DMA((3,)),
         ],
         cost_estimate=pl.CostEstimate(flops=40_000_000, bytes_accessed=4_000_000, transcendentals=0),
-    )(device, sign, corners, span, occupations, orbitals)
+    )(device, corners, span, occupations, orbitals)
 
 
 def plane_kernel(group, device, pieces, table_x, table_y, *refs):
-    *blocks, spectrum, density, packed = refs
+    *blocks, spectrum, exchange, density, packed = refs
     slots = pieces.shape[0]
     count_x, count_y = density.shape
     sub = lax.rem(device[0], len(blocks))
@@ -283,7 +287,7 @@
     placed = density[...]
     for part in range(2, -1, -1):
         placed = placed + product(left, jnp.concatenate([r[part] for r in rights], axis=0))
-    density[...] = placed
+    exchange[...] = exchange_correlation(placed)
     spectrum[...] = times_table(table_times(table_x, placed), table_y)
 
 
@@ -295,7 +299,10 @@
         out_shape=(kept(shape), kept(shape)),
         in_specs=in_smem(1) + in_vmem(3 + len(blocks)),
         out_specs=in_vmem(2),
-        scratch_shapes=[pltpu.VMEM((8 * (pieces.shape[0] // group), LANES), jnp.float32)],
+        scratch_shapes=[
+            pltpu.VMEM(shape, jnp.float32),
+            pltpu.VMEM((8 * (pieces.shape[0] // group), LANES), jnp.float32),
+        ],
     )(device, pieces, table_x, table_y, *blocks)
 
 
@@ -505,13 +512,11 @@
 
     blocks = outer_blocks(device, arguments.pop())
     blocks = swapped(blocks)
-    pieces = core_pieces(device, patch_sign, *arguments, slots, base, counts)
+    pieces = core_pieces(device, *arguments, slots, base, counts)
     pieces, blocks = lax.optimization_barrier((pieces, blocks))
     pieces = spread(pieces)
-    spectrum, density = plane_spectrum(device, pieces, group, table_x, table_y, blocks)
+    spectrum, exchange = plane_spectrum(device, pieces, group, table_x, table_y, blocks)
     chunk = (devices, deep, per_device // deep)
-    exchange = exchange_correlation(density)
-    spectrum, exchange = lax.optimization_barrier((spectrum, exchange))
     spectrum = lax.all_to_all(spectrum.reshape(chunk), AXES, 0, 0, tiled=True)
     spectrum = column_hartree(
         spectrum.reshape(devices * deep, per_device // deep), table_z, device, counts

time: 69.6 us -> 68.5 us (0.984)
  transfers between devices with their start and end apart: 7 -> 7, of which waited for: 3 -> 4; matrix products, arithmetic and copies ran while one was open for 0% -> 0% of each run, Pallas kernels for 5% -> 5%
where the time goes in v5:
time: 68.5 us; the launch traced here: 68.2 us
  blocking collectives  39.3 us (57%)
  Pallas kernels  10.7 us (16%)
  waiting for transfers between devices  9.78 us (14%)
  starting transfers between devices  7.68 us (11%)
  between operations  0.73 us (1%)
    all_to_all x2, blocking collectives, body(): spectrum = lax.all_to_all(spectrum.reshape(chunk), AXES, 0, 0, tiled=True)  25.3 us
    all_to_all x1, blocking collectives, spread(): return lax.all_to_all(pieces, AXES, 0, 0, tiled=True)  14 us
    ppermute x6, waiting for transfers between devices, swapped(): lax.ppermute(block, 'sub', [(i, i ^ d) for i in range(sub_count)])  5.84 us
    ppermute x6, starting transfers between devices, swapped(): lax.ppermute(block, 'sub', [(i, i ^ d) for i in range(sub_count)])  5.08 us
    all_to_all x1, waiting for transfers between devices, spread(): return lax.all_to_all(pieces, AXES, 0, 0, tiled=True)  3.95 us
    pallas_call x1, Pallas kernels, core_pieces(): small_call(lambda *refs: core_kernel(base, *counts, *refs), 8, out_shape=...  3.68 us
    all_to_all x1, starting transfers between devices, spread(): return lax.all_to_all(pieces, AXES, 0, 0, tiled=True)  2.61 us
    pallas_call x1, Pallas kernels, plane_windows(): small_call(lambda *refs: window_kernel(fragment, *refs), 12, out_shape=[b...  2.53 us
  transfers between devices with their start and end apart: 7, of which 4 were waited for; matrix products, arithmetic and copies ran while one was open for 0% of the time, Pallas kernels for 5%

profile of v5, /device:TPU:0, one launch (start us, length us, event | category | flops | bytes accessed | tf_op | source)
XLA Modules:
  0.0 68.2 jit_solution(11737587002033119387)
XLA Ops:
  0.6 0.0 copy-start
  0.6 0.0 copy-start.1
  0.7 0.0 copy-start.2
  0.7 1.0 %shard_map.96 = (f32[64,256]{1,0:T(8,128)S(1)}, f32[64,256]{1,0:T(8,128)S(1)}, f32[64,256]{1,0:T(8,128)S(1)}, f32[64,256]{1,0:T(8,128)S(1)}) custom-call(s32[1]{0:T(128)} %bitcast.refs_0_.device, f32[4,64,256]{2,1,0:T(8,128)} %outer.1), custom_call_target="tpu_custom_call" | custom-call | tf_op jit(solution)/shard_map/pallas_call | solution.py:125
  1.7 0.6 collective-permute-start
  2.3 2.6 %collective-permute-start.1 = (f32[64,256]{1,0:T(8,128)S(1)}, f32[64,256]{1,0:T(8,128)S(1)}, u32[]{:S(2)}, u32[]{:S(2)}) collective-permute-start(f32[64,256]{1,0:T(8,128)S(1)} %get-tuple-element.22), channel_id=1, source_target_pairs={{0,2},{1,3},{2,0},{3,1},{4,6},{5,7},{6,4},{7,5},{8,10},{9,11},{10,... | collective-permute-start | bytes 196616 | tf_op jit(solution)/shard_map/ppermute | solution.py:509
  4.8 0.0 collective-permute-start.2
  4.9 3.7 %shard_map.95 = f32[32,1,1152]{2,1,0:T(1,128)S(1)} custom-call(s32[1]{0:T(128)} %bitcast.refs_0_.device, s32[3,32]{1,0:T(4,128)} %bitcast.11, s32[1,6]{1,0:T(1,128)} %refs_2_.3, s32[1,16]{1,0:T(1,128)} %refs_3_.2, bf16[1,16,110592]{2,1,0:T(8,128)(2,1)} %refs_4_.2), custom_call_target="tpu_custom_call" | custom-call | flops 40000000 | bytes 4000000 | tf_op jit(solution)/shard_map/pallas_call | solution.py:232
  8.5 0.0 collective-permute-done.refs_5_
  8.6 0.0 collective-permute-done.1.refs_6_
  8.6 0.3 collective-permute-done.2.refs_7_
  8.9 14.0 %all_to_all.20.refs_1_ = f32[32,1,1152]{2,1,0:T(1,128)S(1)} all-to-all(f32[32,1,1152]{2,1,0:T(1,128)S(1)} %shard_map.95), channel_id=1, replica_groups=mesh['slab'=8,'sub'=4] {'slab','sub'}, dimensions={0} | all-to-all | bytes 294912 | tf_op jit(solution)/shard_map/all_to_all | solution.py:472
  22.9 0.0 copy-done
  22.9 1.2 %shard_map.97 = (f32[256,256]{1,0:T(8,128)S(1)}, f32[256,256]{1,0:T(8,128)S(1)}) custom-call(s32[1]{0:T(128)} %bitcast.refs_0_.device, f32[32,1,1152]{2,1,0:T(1,128)S(1)} %all_to_all.20.refs_1_, bf16[2,256,256]{2,1,0:T(8,128)(2,1)S(1)} %copy-done, bf16[2,256,256]{2,1,0:T(8,128)(2,1)S(1)} %copy-done, f32[64,256]{1,0:T(8,128)S(1)} %get-tuple-element.25.refs_4_, ...), custom_call_target="tpu_custom_call" | custom-call | tf_op jit(solution)/shard_map/pallas_call | solution.py:296
  24.1 12.5 %all_to_all.21 = f32[32,8,256]{2,1,0:T(8,128)S(1)} all-to-all(f32[32,8,256]{2,1,0:T(8,128)S(1)} %bitcast.10), channel_id=1, replica_groups=mesh['slab'=8,'sub'=4] {'slab','sub'}, dimensions={0} | all-to-all | bytes 524288 | tf_op jit(solution)/shard_map/all_to_all | solution.py:520
  36.6 0.0 copy-done.1
  36.6 0.9 %shard_map.98 = f32[256,256]{1,0:T(8,128)S(1)} custom-call(s32[1]{0:T(128)} %bitcast.refs_0_.device, f32[256,256]{1,0:T(8,128)S(1)} %bitcast.8, bf16[2,256,256]{2,1,0:T(8,128)(2,1)S(1)} %copy-done.1), custom_call_target="tpu_custom_call" | custom-call | tf_op jit(solution)/shard_map/pallas_call | solution.py:333
  37.5 12.8 %all_to_all.22 = f32[32,8,256]{2,1,0:T(8,128)S(1)} all-to-all(f32[32,8,256]{2,1,0:T(8,128)S(1)} %bitcast.9), channel_id=1, replica_groups=mesh['slab'=8,'sub'=4] {'slab','sub'}, dimensions={0} | all-to-all | bytes 524288 | tf_op jit(solution)/shard_map/all_to_all | solution.py:524
  50.3 0.0 copy-done.2
  50.3 2.5 %shard_map.99 = (f32[64,256]{1,0:T(8,128)S(1)}, f32[64,256]{1,0:T(8,128)S(1)}, f32[64,256]{1,0:T(8,128)S(1)}, f32[64,256]{1,0:T(8,128)S(1)}, f32[32,1,2304]{2,1,0:T(1,128)}) custom-call(s32[1]{0:T(128)} %bitcast.refs_0_.device, s32[3,32]{1,0:T(4,128)S(1)} %bitcast.12, f32[256,256]{1,0:T(8,128)S(1)} %bitcast.7, f32[256,256]{1,0:T(8,128)S(1)} %get-tuple-element.30.refs_3_, ...), custom_call_target="tpu_custom_call" | custom-call | tf_op jit(solution)/shard_map/pallas_call | solution.py:395
  52.8 2.6 %all-to-all-start.3 = ((f32[32,1,2304]{2,1,0:T(1,128)}), f32[32,1,2304]{2,1,0:T(1,128)S(1)}, u32[]{:S(2)}, u32[]{:S(2)}) async-start(f32[32,1,2304]{2,1,0:T(1,128)} %get-tuple-element.31), calls=%async_computation.3 | async-start | bytes 589824 | tf_op jit(solution)/shard_map/all_to_all | solution.py:472
  55.4 0.2 collective-permute-start.3
  55.6 1.6 %collective-permute-start.4 = (f32[64,256]{1,0:T(8,128)S(1)}, f32[64,256]{1,0:T(8,128)S(1)}, u32[]{:S(2)}, u32[]{:S(2)}) collective-permute-start(f32[64,256]{1,0:T(8,128)S(1)} %get-tuple-element.34), channel_id=1, source_target_pairs={{0,2},{1,3},{2,0},{3,1},{4,6},{5,7},{6,4},{7,5},{8,10},{9,11},{10,... | collective-permute-start | bytes 196616 | tf_op jit(solution)/shard_map/ppermute | solution.py:509
  57.3 0.1 collective-permute-start.5
  57.4 0.0 collective-permute-done.3.refs_4_
  57.4 5.1 %collective-permute-done.4.refs_5_ = f32[64,256]{1,0:T(8,128)S(1)} collective-permute-done((f32[64,256]{1,0:T(8,128)S(1)}, f32[64,256]{1,0:T(8,128)S(1)}, u32[]{:S(2)}, u32[]{:S(2)}) %collective-permute-start.4) | collective-permute-done | bytes 65568 | tf_op jit(solution)/shard_map/ppermute | solution.py:509
  62.5 0.4 collective-permute-done.5.refs_6_
  62.9 3.9 %all-to-all-done.3.refs_2_ = f32[32,1,2304]{2,1,0:T(1,128)S(1)} async-done(((f32[32,1,2304]{2,1,0:T(1,128)}), f32[32,1,2304]{2,1,0:T(1,128)S(1)}, u32[]{:S(2)}, u32[]{:S(2)}) %all-to-all-start.3) | async-done | bytes 294944 | tf_op jit(solution)/shard_map/all_to_all | solution.py:472
  66.8 1.4 %shard_map.100 = (f32[48,1,2304]{2,1,0:T(1,128)}, f32[4,64,256]{2,1,0:T(8,128)}) custom-call(s32[1]{0:T(128)} %bitcast.refs_0_.device, s32[3,32]{1,0:T(4,128)S(1)} %bitcast.13, f32[32,1,2304]{2,1,0:T(1,128)S(1)} %all-to-all-done.3.refs_2_, f32[64,256]{1,0:T(8,128)S(1)} %get-tuple-element.32.refs_3_, f32[64,256]{1,0:T(8,128)S(1)} %collective-permute-done.3.refs_4_, ...), custom_call_target="tpu_custom_call" | custom-call | tf_op jit(solution)/shard_map/pallas_call | solution.py:432
Async XLA Ops:
  0.6 22.3 %copy-start = (bf16[2,256,256]{2,1,0:T(8,128)(2,1)S(1)}, bf16[2,256,256]{2,1,0:T(8,128)(2,1)}, u32[]{:S(2)}) copy-start(bf16[2,256,256]{2,1,0:T(8,128)(2,1)} %constant.15.clone.refs_2_.refs_3_.refs_4_.refs_5_) | copy-start | bytes 786436
  0.6 35.9 %copy-start.1 = (bf16[2,256,256]{2,1,0:T(8,128)(2,1)S(1)}, bf16[2,256,256]{2,1,0:T(8,128)(2,1)}, u32[]{:S(2)}) copy-start(bf16[2,256,256]{2,1,0:T(8,128)(2,1)} %constant.16.clone.refs_2_) | copy-start | bytes 786436
  0.7 49.6 %copy-start.2 = (s32[32,3]{0,1:T(4,128)S(1)}, s32[32,3]{0,1:T(4,128)}, u32[]{:S(2)}) copy-start(s32[32,3]{0,1:T(4,128)} %param.11) | copy-start | bytes 1156
  1.7 6.8 %collective-permute-start = (f32[64,256]{1,0:T(8,128)S(1)}, f32[64,256]{1,0:T(8,128)S(1)}, u32[]{:S(2)}, u32[]{:S(2)}) collective-permute-start(f32[64,256]{1,0:T(8,128)S(1)} %get-tuple-element.21), channel_id=1, source_target_pairs={{0,1},{1,0},{2,3},{3,2},{4,5},{5,4},{6,7},{7,6},{8,9},{9,8},{10,11... | collective-permute-start | bytes 196616 | tf_op jit(solution)/shard_map/ppermute | solution.py:509
  2.3 6.3 %collective-permute-start.1 = (f32[64,256]{1,0:T(8,128)S(1)}, f32[64,256]{1,0:T(8,128)S(1)}, u32[]{:S(2)}, u32[]{:S(2)}) collective-permute-start(f32[64,256]{1,0:T(8,128)S(1)} %get-tuple-element.22), channel_id=1, source_target_pairs={{0,2},{1,3},{2,0},{3,1},{4,6},{5,7},{6,4},{7,5},{8,10},{9,11},{10,... | collective-permute-start | bytes 196616 | tf_op jit(solution)/shard_map/ppermute | solution.py:509
  4.8 4.1 %collective-permute-start.2 = (f32[64,256]{1,0:T(8,128)S(1)}, f32[64,256]{1,0:T(8,128)S(1)}, u32[]{:S(2)}, u32[]{:S(2)}) collective-permute-start(f32[64,256]{1,0:T(8,128)S(1)} %get-tuple-element.23), channel_id=1, source_target_pairs={{0,3},{1,2},{2,1},{3,0},{4,7},{5,6},{6,5},{7,4},{8,11},{9,10},{10,... | collective-permute-start | bytes 196616 | tf_op jit(solution)/shard_map/ppermute | solution.py:509
  52.8 14.0 %all-to-all-start.3 = ((f32[32,1,2304]{2,1,0:T(1,128)}), f32[32,1,2304]{2,1,0:T(1,128)S(1)}, u32[]{:S(2)}, u32[]{:S(2)}) async-start(f32[32,1,2304]{2,1,0:T(1,128)} %get-tuple-element.31), calls=%async_computation.3 | async-start | bytes 589824 | tf_op jit(solution)/shard_map/all_to_all | solution.py:472
  55.4 1.9 %collective-permute-start.3 = (f32[64,256]{1,0:T(8,128)S(1)}, f32[64,256]{1,0:T(8,128)S(1)}, u32[]{:S(2)}, u32[]{:S(2)}) collective-permute-start(f32[64,256]{1,0:T(8,128)S(1)} %get-tuple-element.33), channel_id=1, source_target_pairs={{0,1},{1,0},{2,3},{3,2},{4,5},{5,4},{6,7},{7,6},{8,9},{9,8},{10,11... | collective-permute-start | bytes 196616 | tf_op jit(solution)/shard_map/ppermute | solution.py:509
  55.6 6.9 %collective-permute-start.4 = (f32[64,256]{1,0:T(8,128)S(1)}, f32[64,256]{1,0:T(8,128)S(1)}, u32[]{:S(2)}, u32[]{:S(2)}) collective-permute-start(f32[64,256]{1,0:T(8,128)S(1)} %get-tuple-element.34), channel_id=1, source_target_pairs={{0,2},{1,3},{2,0},{3,1},{4,6},{5,7},{6,4},{7,5},{8,10},{9,11},{10,... | collective-permute-start | bytes 196616 | tf_op jit(solution)/shard_map/ppermute | solution.py:509
  57.3 5.6 %collective-permute-start.5 = (f32[64,256]{1,0:T(8,128)S(1)}, f32[64,256]{1,0:T(8,128)S(1)}, u32[]{:S(2)}, u32[]{:S(2)}) collective-permute-start(f32[64,256]{1,0:T(8,128)S(1)} %get-tuple-element.35), channel_id=1, source_target_pairs={{0,3},{1,2},{2,1},{3,0},{4,7},{5,6},{6,5},{7,4},{8,11},{9,10},{10,... | collective-permute-start | bytes 196616 | tf_op jit(solution)/shard_map/ppermute | solution.py:509

commit v6 on v5

--- a/solution.py
+++ b/solution.py
@@ -138,7 +138,8 @@
 
 def core_kernel(
     base, depth, count_x, count_y, device, corner_table, span_row, occupation_row, orbitals,
-    out, buffer, sums, rows, corners, span, occupations, arrived, staged,
+    out, buffer, sums, rows, corners, span, occupations, arrived, filled,
+    staged,
 ):
     own, slots, orbital_count = device[0], out.shape[0], orbitals.shape[1]
     scalars = [
@@ -149,19 +150,28 @@
     ]
     for copy in scalars:
         copy.start()
-    chunks = BOX // CHUNK
-    copies = []
-    for c in range(chunks):
+    loose = BOX - CORE
+    early = []
+    for c in range(loose // CHUNK, CORE // CHUNK):
         part = pl.ds(c * CHUNK * PLANE, CHUNK * PLANE)
-        copies.append(
-            pltpu.make_async_copy(orbitals.at[0, :, part], buffer.at[:, part], arrived.at[c])
-        )
-        copies[c].start()
+        copy = pltpu.make_async_copy(orbitals.at[0, :, part], buffer.at[:, part], arrived.at[c])
+        copy.start()
+        early.append(copy)
     for copy in scalars:
         copy.wait()
     first_z, first_x, first_y = span[0, 0], span[0, 1], span[0, 2]
     len_z, len_x, len_y = span[0, 3], span[0, 4], span[0, 5]
-    begin = jnp.minimum(first_z, BOX - CORE)
+    begin = jnp.minimum(first_z, loose)
+    late = []
+    for p in range(loose):
+        i = jnp.where(p < begin, p + CORE, p)
+        part = pl.ds(pl.multiple_of(i * PLANE, LANES), PLANE)
+        late.append(
+            pltpu.make_async_copy(
+                orbitals.at[0, :, part], buffer.at[:, p * PLANE : (p + 1) * PLANE], filled.at[p]
+            )
+        )
+        late[p].start()
     orbital = lax.broadcasted_iota(jnp.int32, (orbital_count, LANES), 0)
     weight = jnp.zeros((orbital_count, LANES), jnp.int32)
     for o in range(orbital_count):
@@ -172,17 +182,16 @@
     weight = (weight * sign).astype(jnp.float32)
     groups = CHUNK * GROUPS // 8
     tiles = WIDE // LANES
-    ahead = chunks - CORE // CHUNK
-    for c in range(ahead):
-        copies[c].wait()
-    for c in range(CORE // CHUNK):
-        copies[c + ahead].wait()
+    order = list(range(loose // CHUNK, CORE // CHUNK)) + list(range(loose // CHUNK))
+    for n, c in enumerate(order):
+        for copy in early[n : n + 1] or late[c * CHUNK : (c + 1) * CHUNK]:
+            copy.wait()
 
         def add_rows(b, carry, c=c):
             for q in range(tiles):
                 cells = []
                 for s in range(8):
-                    line = begin * GROUPS + (c * groups + b) * 8 + s
+                    line = (c * groups + b) * 8 + s
                     lane = pl.multiple_of(line * WIDE + q * LANES, LANES)
                     values = buffer[:, pl.ds(lane, LANES)].astype(jnp.float32)
                     values = values * values * weight
@@ -207,7 +216,7 @@
         turned = []
         for h in range(UNROLL):
             p = lax.rem(UNROLL * step + h - start_z + depth, depth)
-            local = jnp.minimum(p + first_z - begin, CORE - 1)
+            local = lax.rem(p + first_z, CORE)
             cells = rows[pl.ds(local * BOX + first_x, CORE), :]
             for q in range(4):
                 turn = lax.rem(32 * q - first_y + LANES, LANES)
@@ -236,13 +245,14 @@
         in_specs=in_smem(1) + anywhere(4),
         out_specs=in_vmem(1)[0],
         scratch_shapes=[
-            pltpu.VMEM((orbital_count, BOX * PLANE), orbitals.dtype),
+            pltpu.VMEM((orbital_count, CORE * PLANE), orbitals.dtype),
             pltpu.VMEM((CORE * GROUPS, WIDE), jnp.float32),
             pltpu.VMEM((CORE * BOX + CORE, LANES), jnp.float32),
             pltpu.SMEM(corners.shape, jnp.int32),
             pltpu.SMEM(span.shape, jnp.int32),
             pltpu.SMEM(occupations.shape, jnp.int32),
-            pltpu.SemaphoreType.DMA((BOX // CHUNK,)),
+            pltpu.SemaphoreType.DMA((CORE // CHUNK,)),
+            pltpu.SemaphoreType.DMA((BOX - CORE,)),
             pltpu.SemaphoreType.DMA((3,)),
         ],
         cost_estimate=pl.CostEstimate(flops=40_000_000, bytes_accessed=4_000_000, transcendentals=0),
@@ -340,7 +350,7 @@
 
 
 def window_kernel(fragment, device, corner_table, spectrum, exchange, table_x, table_y, *refs):
-    *blocks, out, wide, cut, corners, staged = refs
+    *blocks, out, wide, cut, ready, corners, staged, sent = refs
     scalars = pltpu.make_async_copy(corner_table, corners, staged)
     scalars.start()
     slots = out.shape[0]
@@ -377,14 +387,23 @@
             cut[pl.ds(at, BOX), :] = turned[h]
         return carry
 
-    lax.fori_loop(0, slots // UNROLL, cut_windows, 0)
-    count = slots * GROUPS
-    flat = jnp.concatenate(
-        [cut[pl.ds(r, count, stride=8), :][:, 0:BOX] for r in range(8)], axis=1
-    )
-    for k in range(slots):
-        for g in range(GROUPS):
-            out[k, :, g * WIDE : (g + 1) * WIDE] = flat[k * GROUPS + g : k * GROUPS + g + 1, :]
+    parts = len(range(0, slots, slots // 4))
+    many = slots // parts
+    copies = []
+    for n in range(parts):
+        lax.fori_loop(-(-n * many // UNROLL), -(-(n + 1) * many // UNROLL), cut_windows, 0)
+        at = n * many * BOX
+        lines = [cut[pl.ds(at + r, many * GROUPS, stride=8), :][:, 0:BOX] for r in range(8)]
+        flat = jnp.concatenate(lines, axis=1)
+        for k in range(many):
+            for g in range(GROUPS):
+                line = flat[k * GROUPS + g : k * GROUPS + g + 1, :]
+                ready[n * many + k, :, g * WIDE : (g + 1) * WIDE] = line
+        some = pl.ds(n * many, many)
+        copies.append(pltpu.make_async_copy(ready.at[some], out.at[some], sent.at[n]))
+        copies[n].start()
+    for copy in copies:
+        copy.wait()
 
 
 def plane_windows(
@@ -395,14 +414,16 @@
     return small_call(
         lambda *refs: window_kernel(fragment, *refs),
         12,
-        out_shape=[block] * blocks + [kept((slots, 1, PLANE))],
+        out_shape=[block] * blocks + [jax.ShapeDtypeStruct((slots, 1, PLANE), jnp.float32)],
         in_specs=in_smem(1) + anywhere(1) + in_vmem(4),
-        out_specs=in_vmem(blocks + 1),
+        out_specs=in_vmem(blocks) + anywhere(1),
         scratch_shapes=[
             pltpu.VMEM((count_y // LANES * (count_x + BOX), LANES), jnp.float32),
             pltpu.VMEM((slots * BOX, LANES), jnp.float32),
+            pltpu.VMEM((slots, 1, PLANE), jnp.float32),
             pltpu.SMEM(corners.shape, jnp.int32),
             pltpu.SemaphoreType.DMA,
+            pltpu.SemaphoreType.DMA((4,)),
         ],
     )(device, corners, spectrum, exchange, table_x, table_y)
 

time: 68.5 us -> 68.9 us (level)
  transfers between devices with their start and end apart: 7 -> 7, of which waited for: 4 -> 4; matrix products, arithmetic and copies ran while one was open for 0% -> 0% of each run, Pallas kernels for 5% -> 6%
where the time goes in v6:
time: 68.9 us; the launch traced here: 68.6 us
  blocking collectives  39.5 us (57%)
  Pallas kernels  11.1 us (16%)
  waiting for transfers between devices  9.59 us (14%)
  starting transfers between devices  7.68 us (11%)
  between operations  0.73 us (1%)
    all_to_all x2, blocking collectives, body(): spectrum = lax.all_to_all(spectrum.reshape(chunk), AXES, 0, 0, tiled=True)  25.3 us
    all_to_all x1, blocking collectives, spread(): return lax.all_to_all(pieces, AXES, 0, 0, tiled=True)  14.2 us
    ppermute x6, waiting for transfers between devices, swapped(): lax.ppermute(block, 'sub', [(i, i ^ d) for i in range(sub_count)])  5.64 us
    ppermute x6, starting transfers between devices, swapped(): lax.ppermute(block, 'sub', [(i, i ^ d) for i in range(sub_count)])  5.08 us
    all_to_all x1, waiting for transfers between devices, spread(): return lax.all_to_all(pieces, AXES, 0, 0, tiled=True)  3.95 us
    pallas_call x1, Pallas kernels, core_pieces(): small_call(lambda *refs: core_kernel(base, *counts, *refs), 8, out_shape=...  3.87 us
    pallas_call x1, Pallas kernels, plane_windows(): small_call(lambda *refs: window_kernel(fragment, *refs), 12, out_shape=[b...  2.74 us
    all_to_all x1, starting transfers between devices, spread(): return lax.all_to_all(pieces, AXES, 0, 0, tiled=True)  2.61 us
  transfers between devices with their start and end apart: 7, of which 4 were waited for; matrix products, arithmetic and copies ran while one was open for 0% of the time, Pallas kernels for 6%

profile of v6, /device:TPU:0, one launch (start us, length us, event | category | flops | bytes accessed | tf_op | source)
XLA Modules:
  0.0 68.6 jit_solution(14460990730605458447)
XLA Ops:
  0.6 0.0 copy-start
  0.6 0.0 copy-start.1
  0.7 0.0 copy-start.2
  0.7 1.0 %shard_map.96 = (f32[64,256]{1,0:T(8,128)S(1)}, f32[64,256]{1,0:T(8,128)S(1)}, f32[64,256]{1,0:T(8,128)S(1)}, f32[64,256]{1,0:T(8,128)S(1)}) custom-call(s32[1]{0:T(128)} %bitcast.refs_0_.device, f32[4,64,256]{2,1,0:T(8,128)} %outer.1), custom_call_target="tpu_custom_call" | custom-call | tf_op jit(solution)/shard_map/pallas_call | solution.py:125
  1.7 0.6 collective-permute-start
  2.3 2.6 %collective-permute-start.1 = (f32[64,256]{1,0:T(8,128)S(1)}, f32[64,256]{1,0:T(8,128)S(1)}, u32[]{:S(2)}, u32[]{:S(2)}) collective-permute-start(f32[64,256]{1,0:T(8,128)S(1)} %get-tuple-element.22), channel_id=1, source_target_pairs={{0,2},{1,3},{2,0},{3,1},{4,6},{5,7},{6,4},{7,5},{8,10},{9,11},{10,... | collective-permute-start | bytes 196616 | tf_op jit(solution)/shard_map/ppermute | solution.py:530
  4.8 0.0 collective-permute-start.2
  4.9 3.9 %shard_map.95 = f32[32,1,1152]{2,1,0:T(1,128)S(1)} custom-call(s32[1]{0:T(128)} %bitcast.refs_0_.device, s32[3,32]{1,0:T(4,128)} %bitcast.11, s32[1,6]{1,0:T(1,128)} %refs_2_.3, s32[1,16]{1,0:T(1,128)} %refs_3_.2, bf16[1,16,110592]{2,1,0:T(8,128)(2,1)} %refs_4_.2), custom_call_target="tpu_custom_call" | custom-call | flops 40000000 | bytes 4000000 | tf_op jit(solution)/shard_map/pallas_call | solution.py:241
  8.7 0.0 collective-permute-done.refs_5_
  8.7 0.0 collective-permute-done.1.refs_6_
  8.8 0.1 collective-permute-done.2.refs_7_
  8.9 14.2 %all_to_all.20.refs_1_ = f32[32,1,1152]{2,1,0:T(1,128)S(1)} all-to-all(f32[32,1,1152]{2,1,0:T(1,128)S(1)} %shard_map.95), channel_id=1, replica_groups=mesh['slab'=8,'sub'=4] {'slab','sub'}, dimensions={0} | all-to-all | bytes 294912 | tf_op jit(solution)/shard_map/all_to_all | solution.py:493
  23.1 0.0 copy-done
  23.1 1.2 %shard_map.97 = (f32[256,256]{1,0:T(8,128)S(1)}, f32[256,256]{1,0:T(8,128)S(1)}) custom-call(s32[1]{0:T(128)} %bitcast.refs_0_.device, f32[32,1,1152]{2,1,0:T(1,128)S(1)} %all_to_all.20.refs_1_, bf16[2,256,256]{2,1,0:T(8,128)(2,1)S(1)} %copy-done, bf16[2,256,256]{2,1,0:T(8,128)(2,1)S(1)} %copy-done, f32[64,256]{1,0:T(8,128)S(1)} %get-tuple-element.25.refs_4_, ...), custom_call_target="tpu_custom_call" | custom-call | tf_op jit(solution)/shard_map/pallas_call | solution.py:306
  24.3 12.5 %all_to_all.21 = f32[32,8,256]{2,1,0:T(8,128)S(1)} all-to-all(f32[32,8,256]{2,1,0:T(8,128)S(1)} %bitcast.10), channel_id=1, replica_groups=mesh['slab'=8,'sub'=4] {'slab','sub'}, dimensions={0} | all-to-all | bytes 524288 | tf_op jit(solution)/shard_map/all_to_all | solution.py:541
  36.8 0.0 copy-done.1
  36.8 0.9 %shard_map.98 = f32[256,256]{1,0:T(8,128)S(1)} custom-call(s32[1]{0:T(128)} %bitcast.refs_0_.device, f32[256,256]{1,0:T(8,128)S(1)} %bitcast.8, bf16[2,256,256]{2,1,0:T(8,128)(2,1)S(1)} %copy-done.1), custom_call_target="tpu_custom_call" | custom-call | tf_op jit(solution)/shard_map/pallas_call | solution.py:343
  37.7 12.8 %all_to_all.22 = f32[32,8,256]{2,1,0:T(8,128)S(1)} all-to-all(f32[32,8,256]{2,1,0:T(8,128)S(1)} %bitcast.9), channel_id=1, replica_groups=mesh['slab'=8,'sub'=4] {'slab','sub'}, dimensions={0} | all-to-all | bytes 524288 | tf_op jit(solution)/shard_map/all_to_all | solution.py:545
  50.5 0.0 copy-done.2
  50.5 2.7 %shard_map.99 = (f32[64,256]{1,0:T(8,128)S(1)}, f32[64,256]{1,0:T(8,128)S(1)}, f32[64,256]{1,0:T(8,128)S(1)}, f32[64,256]{1,0:T(8,128)S(1)}, f32[32,1,2304]{2,1,0:T(1,128)}) custom-call(s32[1]{0:T(128)} %bitcast.refs_0_.device, s32[3,32]{1,0:T(4,128)S(1)} %bitcast.12, f32[256,256]{1,0:T(8,128)S(1)} %bitcast.7, f32[256,256]{1,0:T(8,128)S(1)} %get-tuple-element.30.refs_3_, ...), custom_call_target="tpu_custom_call" | custom-call | tf_op jit(solution)/shard_map/pallas_call | solution.py:414
  53.2 2.6 %all-to-all-start.3 = ((f32[32,1,2304]{2,1,0:T(1,128)}), f32[32,1,2304]{2,1,0:T(1,128)S(1)}, u32[]{:S(2)}, u32[]{:S(2)}) async-start(f32[32,1,2304]{2,1,0:T(1,128)} %get-tuple-element.31), calls=%async_computation.3 | async-start | bytes 589824 | tf_op jit(solution)/shard_map/all_to_all | solution.py:493
  55.9 0.2 collective-permute-start.3
  56.0 1.6 %collective-permute-start.4 = (f32[64,256]{1,0:T(8,128)S(1)}, f32[64,256]{1,0:T(8,128)S(1)}, u32[]{:S(2)}, u32[]{:S(2)}) collective-permute-start(f32[64,256]{1,0:T(8,128)S(1)} %get-tuple-element.34), channel_id=1, source_target_pairs={{0,2},{1,3},{2,0},{3,1},{4,6},{5,7},{6,4},{7,5},{8,10},{9,11},{10,... | collective-permute-start | bytes 196616 | tf_op jit(solution)/shard_map/ppermute | solution.py:530
  57.7 0.1 collective-permute-start.5
  57.8 0.0 collective-permute-done.3.refs_4_
  57.8 5.1 %collective-permute-done.4.refs_5_ = f32[64,256]{1,0:T(8,128)S(1)} collective-permute-done((f32[64,256]{1,0:T(8,128)S(1)}, f32[64,256]{1,0:T(8,128)S(1)}, u32[]{:S(2)}, u32[]{:S(2)}) %collective-permute-start.4) | collective-permute-done | bytes 65568 | tf_op jit(solution)/shard_map/ppermute | solution.py:530
  62.9 0.4 collective-permute-done.5.refs_6_
  63.3 3.9 %all-to-all-done.3.refs_2_ = f32[32,1,2304]{2,1,0:T(1,128)S(1)} async-done(((f32[32,1,2304]{2,1,0:T(1,128)}), f32[32,1,2304]{2,1,0:T(1,128)S(1)}, u32[]{:S(2)}, u32[]{:S(2)}) %all-to-all-start.3) | async-done | bytes 294944 | tf_op jit(solution)/shard_map/all_to_all | solution.py:493
  67.2 1.4 %shard_map.100 = (f32[48,1,2304]{2,1,0:T(1,128)}, f32[4,64,256]{2,1,0:T(8,128)}) custom-call(s32[1]{0:T(128)} %bitcast.refs_0_.device, s32[3,32]{1,0:T(4,128)S(1)} %bitcast.13, f32[32,1,2304]{2,1,0:T(1,128)S(1)} %all-to-all-done.3.refs_2_, f32[64,256]{1,0:T(8,128)S(1)} %get-tuple-element.32.refs_3_, f32[64,256]{1,0:T(8,128)S(1)} %collective-permute-done.3.refs_4_, ...), custom_call_target="tpu_custom_call" | custom-call | tf_op jit(solution)/shard_map/pallas_call | solution.py:453
Async XLA Ops:
  0.6 22.5 %copy-start = (bf16[2,256,256]{2,1,0:T(8,128)(2,1)S(1)}, bf16[2,256,256]{2,1,0:T(8,128)(2,1)}, u32[]{:S(2)}) copy-start(bf16[2,256,256]{2,1,0:T(8,128)(2,1)} %constant.15.clone.refs_2_.refs_3_.refs_4_.refs_5_) | copy-start | bytes 786436
  0.6 36.1 %copy-start.1 = (bf16[2,256,256]{2,1,0:T(8,128)(2,1)S(1)}, bf16[2,256,256]{2,1,0:T(8,128)(2,1)}, u32[]{:S(2)}) copy-start(bf16[2,256,256]{2,1,0:T(8,128)(2,1)} %constant.16.clone.refs_2_) | copy-start | bytes 786436
  0.7 49.8 %copy-start.2 = (s32[32,3]{0,1:T(4,128)S(1)}, s32[32,3]{0,1:T(4,128)}, u32[]{:S(2)}) copy-start(s32[32,3]{0,1:T(4,128)} %param.11) | copy-start | bytes 1156
  1.7 7.0 %collective-permute-start = (f32[64,256]{1,0:T(8,128)S(1)}, f32[64,256]{1,0:T(8,128)S(1)}, u32[]{:S(2)}, u32[]{:S(2)}) collective-permute-start(f32[64,256]{1,0:T(8,128)S(1)} %get-tuple-element.21), channel_id=1, source_target_pairs={{0,1},{1,0},{2,3},{3,2},{4,5},{5,4},{6,7},{7,6},{8,9},{9,8},{10,11... | collective-permute-start | bytes 196616 | tf_op jit(solution)/shard_map/ppermute | solution.py:530
  2.3 6.5 %collective-permute-start.1 = (f32[64,256]{1,0:T(8,128)S(1)}, f32[64,256]{1,0:T(8,128)S(1)}, u32[]{:S(2)}, u32[]{:S(2)}) collective-permute-start(f32[64,256]{1,0:T(8,128)S(1)} %get-tuple-element.22), channel_id=1, source_target_pairs={{0,2},{1,3},{2,0},{3,1},{4,6},{5,7},{6,4},{7,5},{8,10},{9,11},{10,... | collective-permute-start | bytes 196616 | tf_op jit(solution)/shard_map/ppermute | solution.py:530
  4.8 4.1 %collective-permute-start.2 = (f32[64,256]{1,0:T(8,128)S(1)}, f32[64,256]{1,0:T(8,128)S(1)}, u32[]{:S(2)}, u32[]{:S(2)}) collective-permute-start(f32[64,256]{1,0:T(8,128)S(1)} %get-tuple-element.23), channel_id=1, source_target_pairs={{0,3},{1,2},{2,1},{3,0},{4,7},{5,6},{6,5},{7,4},{8,11},{9,10},{10,... | collective-permute-start | bytes 196616 | tf_op jit(solution)/shard_map/ppermute | solution.py:530
  53.2 14.0 %all-to-all-start.3 = ((f32[32,1,2304]{2,1,0:T(1,128)}), f32[32,1,2304]{2,1,0:T(1,128)S(1)}, u32[]{:S(2)}, u32[]{:S(2)}) async-start(f32[32,1,2304]{2,1,0:T(1,128)} %get-tuple-element.31), calls=%async_computation.3 | async-start | bytes 589824 | tf_op jit(solution)/shard_map/all_to_all | solution.py:493
  55.9 1.9 %collective-permute-start.3 = (f32[64,256]{1,0:T(8,128)S(1)}, f32[64,256]{1,0:T(8,128)S(1)}, u32[]{:S(2)}, u32[]{:S(2)}) collective-permute-start(f32[64,256]{1,0:T(8,128)S(1)} %get-tuple-element.33), channel_id=1, source_target_pairs={{0,1},{1,0},{2,3},{3,2},{4,5},{5,4},{6,7},{7,6},{8,9},{9,8},{10,11... | collective-permute-start | bytes 196616 | tf_op jit(solution)/shard_map/ppermute | solution.py:530
  56.0 6.9 %collective-permute-start.4 = (f32[64,256]{1,0:T(8,128)S(1)}, f32[64,256]{1,0:T(8,128)S(1)}, u32[]{:S(2)}, u32[]{:S(2)}) collective-permute-start(f32[64,256]{1,0:T(8,128)S(1)} %get-tuple-element.34), channel_id=1, source_target_pairs={{0,2},{1,3},{2,0},{3,1},{4,6},{5,7},{6,4},{7,5},{8,10},{9,11},{10,... | collective-permute-start | bytes 196616 | tf_op jit(solution)/shard_map/ppermute | solution.py:530
  57.7 5.6 %collective-permute-start.5 = (f32[64,256]{1,0:T(8,128)S(1)}, f32[64,256]{1,0:T(8,128)S(1)}, u32[]{:S(2)}, u32[]{:S(2)}) collective-permute-start(f32[64,256]{1,0:T(8,128)S(1)} %get-tuple-element.35), channel_id=1, source_target_pairs={{0,3},{1,2},{2,1},{3,0},{4,7},{5,6},{6,5},{7,4},{8,11},{9,10},{10,... | collective-permute-start | bytes 196616 | tf_op jit(solution)/shard_map/ppermute | solution.py:530

commit v7 on v5

--- a/solution.py
+++ b/solution.py
@@ -80,6 +80,15 @@
 
 def anywhere(count):
     return [pl.BlockSpec(memory_space=pl.ANY)] * count
+
+
+def at_once(slots):
+    return next(n for n in (8, 4, 2, 1) if slots % n == 0)
+
+
+def repeated(steps, step):
+    together = next(n for n in (4, 3, 2, 1) if steps % n == 0)
+    lax.fori_loop(0, steps, step, 0, unroll=together)
 
 
 def kept(shape):
@@ -133,7 +142,6 @@
 
 
 CHUNK = 8
-UNROLL = 4
 
 
 def core_kernel(
@@ -191,10 +199,11 @@
                 sums[pl.ds(at, 8), q * LANES : (q + 1) * LANES] = row_sums(cells)
             return carry
 
-        lax.fori_loop(0, groups, add_rows, 0, unroll=2)
-    count = CORE * GROUPS
-    for r in range(8):
-        rows[pl.ds(r, count, stride=8), 0:BOX] = sums[:, r * BOX : (r + 1) * BOX]
+        lax.fori_loop(0, groups, add_rows, 0, unroll=True)
+        count = 8 * groups
+        for r in range(8):
+            line = sums[c * count : (c + 1) * count, r * BOX : (r + 1) * BOX]
+            rows[pl.ds(8 * c * count + r, count, stride=8), 0:BOX] = line
 
     start_z = lax.rem(corners[0, own] + first_z, depth) - base(own)
     start_x = lax.rem(corners[1, own] + first_x, count_x)
@@ -203,17 +212,19 @@
     lane = lax.broadcasted_iota(jnp.int32, (8, LANES), 1)
     first = jnp.where(lane[0:1] == 0, start_x, start_y).astype(jnp.float32)
 
+    many = at_once(slots)
+
     def pack(step, carry):
         turned = []
-        for h in range(UNROLL):
-            p = lax.rem(UNROLL * step + h - start_z + depth, depth)
+        for h in range(many):
+            p = lax.rem(many * step + h - start_z + depth, depth)
             local = jnp.minimum(p + first_z - begin, CORE - 1)
             cells = rows[pl.ds(local * BOX + first_x, CORE), :]
             for q in range(4):
                 turn = lax.rem(32 * q - first_y + LANES, LANES)
                 turned.append(pltpu.roll(cells[8 * q : 8 * q + 8], turn, 1))
-        for h in range(UNROLL):
-            k = UNROLL * step + h
+        for h in range(many):
+            k = many * step + h
             held = lax.rem(k - start_z + depth, depth) < len_z
             packed = jnp.zeros((8, LANES), jnp.float32)
             for q in range(4):
@@ -224,7 +235,7 @@
             out[k, :, PACK:PIECE] = first
         return carry
 
-    lax.fori_loop(0, slots // UNROLL, pack, 0)
+    repeated(slots // many, pack)
 
 
 def core_pieces(device, corners, span, occupations, orbitals, slots, base, counts):
@@ -361,10 +372,12 @@
     lane = lax.broadcasted_iota(jnp.int32, (BOX, LANES), 1)
     scalars.wait()
 
+    many = at_once(slots)
+
     def cut_windows(step, carry):
         turned = []
-        for h in range(UNROLL):
-            f = fragment(UNROLL * step + h, device[0])
+        for h in range(many):
+            f = fragment(many * step + h, device[0])
             x, y = corners[1, f], corners[2, f]
             tile = y // LANES
             over = y - tile * LANES
@@ -372,12 +385,12 @@
             far = wide[pl.ds(lax.rem(tile + 1, tiles) * tall + x, BOX), :]
             turn = lax.rem(LANES - over, LANES)
             turned.append(pltpu.roll(jnp.where(lane < over, far, near), turn, 1))
-        for h in range(UNROLL):
-            at = pl.multiple_of((UNROLL * step + h) * BOX, 8)
+        for h in range(many):
+            at = pl.multiple_of((many * step + h) * BOX, 8)
             cut[pl.ds(at, BOX), :] = turned[h]
         return carry
 
-    lax.fori_loop(0, slots // UNROLL, cut_windows, 0)
+    repeated(slots // many, cut_windows)
     count = slots * GROUPS
     flat = jnp.concatenate(
         [cut[pl.ds(r, count, stride=8), :][:, 0:BOX] for r in range(8)], axis=1
@@ -418,9 +431,16 @@
         pltpu.make_async_copy(block, potential.at[sub ^ d], copied.at[BOX + d])
         for d, block in enumerate(blocks)
     ]
-    for i in range(BOX):
-        z = lax.rem(first + i, depth)
-        copies.append(pltpu.make_async_copy(windows.at[z], box.at[i], copied.at[i]))
+    tall = len(blocks)
+    over = lax.rem(first, tall)
+    for t in range(1, BOX // tall):
+        z = pl.ds(lax.rem(first - over + t * tall, depth), tall)
+        i = pl.ds(t * tall - over, tall)
+        copies.append(pltpu.make_async_copy(windows.at[z], box.at[i], copied.at[t]))
+    for q in range(tall):
+        z = jnp.where(q < over, lax.rem(first - over + BOX, depth), first - over) + q
+        i = jnp.where(q < over, BOX, 0) + q - over
+        copies.append(pltpu.make_async_copy(windows.at[z], box.at[i], copied.at[BOX + tall + q]))
     for copy in copies:
         copy.start()
     for copy in copies:
@@ -438,7 +458,7 @@
         ),
         in_specs=in_smem(1) + in_vmem(1) + anywhere(1 + count),
         out_specs=tuple(anywhere(2)),
-        scratch_shapes=[pltpu.SemaphoreType.DMA((BOX + count,))],
+        scratch_shapes=[pltpu.SemaphoreType.DMA((BOX + 2 * count,))],
     )(device, corners, windows, *blocks)
 
 

time: 68.5 us -> 67.8 us (0.990)
  Pallas kernels: 10.7 us -> 9.55 us
  waiting for transfers between devices: 9.78 us -> 10.5 us
    ppermute x6, waiting for transfers between devices: 5.84 us -> 6.55 us  [swapped(): lax.ppermute(block, 'sub', [(i, i ^ d) for i in range(sub_count)])]
    pallas_call x1, Pallas kernels: 3.68 us -> 2.97 us  [core_pieces(): small_call(lambda *refs: core_kernel(base, *counts, *refs), 8, out_shape=...]
  transfers between devices with their start and end apart: 7 -> 7, of which waited for: 4 -> 4; matrix products, arithmetic and copies ran while one was open for 0% -> 0% of each run, Pallas kernels for 5% -> 4%
where the time goes in v7:
time: 67.8 us; the launch traced here: 67.5 us
  blocking collectives  39.1 us (58%)
  waiting for transfers between devices  10.5 us (15%)
  Pallas kernels  9.55 us (14%)
  starting transfers between devices  7.68 us (11%)
  between operations  0.73 us (1%)
    all_to_all x2, blocking collectives, body(): spectrum = lax.all_to_all(spectrum.reshape(chunk), AXES, 0, 0, tiled=True)  25.3 us
    all_to_all x1, blocking collectives, spread(): return lax.all_to_all(pieces, AXES, 0, 0, tiled=True)  13.8 us
    ppermute x6, waiting for transfers between devices, swapped(): lax.ppermute(block, 'sub', [(i, i ^ d) for i in range(sub_count)])  6.55 us
    ppermute x6, starting transfers between devices, swapped(): lax.ppermute(block, 'sub', [(i, i ^ d) for i in range(sub_count)])  5.08 us
    all_to_all x1, waiting for transfers between devices, spread(): return lax.all_to_all(pieces, AXES, 0, 0, tiled=True)  3.95 us
    pallas_call x1, Pallas kernels, core_pieces(): small_call(lambda *refs: core_kernel(base, *counts, *refs), 8, out_shape=...  2.97 us
    all_to_all x1, starting transfers between devices, spread(): return lax.all_to_all(pieces, AXES, 0, 0, tiled=True)  2.61 us
    pallas_call x1, Pallas kernels, plane_windows(): small_call(lambda *refs: window_kernel(fragment, *refs), 12, out_shape=[b...  2.06 us
  transfers between devices with their start and end apart: 7, of which 4 were waited for; matrix products, arithmetic and copies ran while one was open for 0% of the time, Pallas kernels for 4%

profile of v7, /device:TPU:0, one launch (start us, length us, event | category | flops | bytes accessed | tf_op | source)
XLA Modules:
  0.0 67.5 jit_solution(15787420553106735201)
XLA Ops:
  0.6 0.0 copy-start
  0.6 0.0 copy-start.1
  0.7 0.0 copy-start.2
  0.7 1.0 %shard_map.96 = (f32[64,256]{1,0:T(8,128)S(1)}, f32[64,256]{1,0:T(8,128)S(1)}, f32[64,256]{1,0:T(8,128)S(1)}, f32[64,256]{1,0:T(8,128)S(1)}) custom-call(s32[1]{0:T(128)} %bitcast.refs_0_.device, f32[4,64,256]{2,1,0:T(8,128)} %outer.1), custom_call_target="tpu_custom_call" | custom-call | tf_op jit(solution)/shard_map/pallas_call | solution.py:134
  1.7 0.6 collective-permute-start
  2.3 2.6 %collective-permute-start.1 = (f32[64,256]{1,0:T(8,128)S(1)}, f32[64,256]{1,0:T(8,128)S(1)}, u32[]{:S(2)}, u32[]{:S(2)}) collective-permute-start(f32[64,256]{1,0:T(8,128)S(1)} %get-tuple-element.22), channel_id=1, source_target_pairs={{0,2},{1,3},{2,0},{3,1},{4,6},{5,7},{6,4},{7,5},{8,10},{9,11},{10,... | collective-permute-start | bytes 196616 | tf_op jit(solution)/shard_map/ppermute | solution.py:529
  4.8 0.0 collective-permute-start.2
  4.9 3.0 %shard_map.95 = f32[32,1,1152]{2,1,0:T(1,128)S(1)} custom-call(s32[1]{0:T(128)} %bitcast.refs_0_.device, s32[3,32]{1,0:T(4,128)} %bitcast.11, s32[1,6]{1,0:T(1,128)} %refs_2_.3, s32[1,16]{1,0:T(1,128)} %refs_3_.2, bf16[1,16,110592]{2,1,0:T(8,128)(2,1)} %refs_4_.2), custom_call_target="tpu_custom_call" | custom-call | flops 40000000 | bytes 4000000 | tf_op jit(solution)/shard_map/pallas_call | solution.py:243
  7.8 0.0 collective-permute-done.refs_5_
  7.8 0.0 collective-permute-done.1.refs_6_
  7.9 1.0 %collective-permute-done.2.refs_7_ = f32[64,256]{1,0:T(8,128)S(1)} collective-permute-done((f32[64,256]{1,0:T(8,128)S(1)}, f32[64,256]{1,0:T(8,128)S(1)}, u32[]{:S(2)}, u32[]{:S(2)}) %collective-permute-start.2) | collective-permute-done | bytes 65568 | tf_op jit(solution)/shard_map/ppermute | solution.py:529
  8.9 13.8 %all_to_all.20.refs_1_ = f32[32,1,1152]{2,1,0:T(1,128)S(1)} all-to-all(f32[32,1,1152]{2,1,0:T(1,128)S(1)} %shard_map.95), channel_id=1, replica_groups=mesh['slab'=8,'sub'=4] {'slab','sub'}, dimensions={0} | all-to-all | bytes 294912 | tf_op jit(solution)/shard_map/all_to_all | solution.py:492
  22.7 0.0 copy-done
  22.7 1.2 %shard_map.97 = (f32[256,256]{1,0:T(8,128)S(1)}, f32[256,256]{1,0:T(8,128)S(1)}) custom-call(s32[1]{0:T(128)} %bitcast.refs_0_.device, f32[32,1,1152]{2,1,0:T(1,128)S(1)} %all_to_all.20.refs_1_, bf16[2,256,256]{2,1,0:T(8,128)(2,1)S(1)} %copy-done, bf16[2,256,256]{2,1,0:T(8,128)(2,1)S(1)} %copy-done, f32[64,256]{1,0:T(8,128)S(1)} %get-tuple-element.25.refs_4_, ...), custom_call_target="tpu_custom_call" | custom-call | tf_op jit(solution)/shard_map/pallas_call | solution.py:307
  23.9 12.5 %all_to_all.21 = f32[32,8,256]{2,1,0:T(8,128)S(1)} all-to-all(f32[32,8,256]{2,1,0:T(8,128)S(1)} %bitcast.10), channel_id=1, replica_groups=mesh['slab'=8,'sub'=4] {'slab','sub'}, dimensions={0} | all-to-all | bytes 524288 | tf_op jit(solution)/shard_map/all_to_all | solution.py:540
  36.3 0.0 copy-done.1
  36.3 0.9 %shard_map.98 = f32[256,256]{1,0:T(8,128)S(1)} custom-call(s32[1]{0:T(128)} %bitcast.refs_0_.device, f32[256,256]{1,0:T(8,128)S(1)} %bitcast.8, bf16[2,256,256]{2,1,0:T(8,128)(2,1)S(1)} %copy-done.1), custom_call_target="tpu_custom_call" | custom-call | tf_op jit(solution)/shard_map/pallas_call | solution.py:344
  37.3 12.8 %all_to_all.22 = f32[32,8,256]{2,1,0:T(8,128)S(1)} all-to-all(f32[32,8,256]{2,1,0:T(8,128)S(1)} %bitcast.9), channel_id=1, replica_groups=mesh['slab'=8,'sub'=4] {'slab','sub'}, dimensions={0} | all-to-all | bytes 524288 | tf_op jit(solution)/shard_map/all_to_all | solution.py:544
  50.1 0.0 copy-done.2
  50.1 2.1 %shard_map.99 = (f32[64,256]{1,0:T(8,128)S(1)}, f32[64,256]{1,0:T(8,128)S(1)}, f32[64,256]{1,0:T(8,128)S(1)}, f32[64,256]{1,0:T(8,128)S(1)}, f32[32,1,2304]{2,1,0:T(1,128)}) custom-call(s32[1]{0:T(128)} %bitcast.refs_0_.device, s32[3,32]{1,0:T(4,128)S(1)} %bitcast.12, f32[256,256]{1,0:T(8,128)S(1)} %bitcast.7, f32[256,256]{1,0:T(8,128)S(1)} %get-tuple-element.30.refs_3_, ...), custom_call_target="tpu_custom_call" | custom-call | tf_op jit(solution)/shard_map/pallas_call | solution.py:408
  52.1 2.6 %all-to-all-start.3 = ((f32[32,1,2304]{2,1,0:T(1,128)}), f32[32,1,2304]{2,1,0:T(1,128)S(1)}, u32[]{:S(2)}, u32[]{:S(2)}) async-start(f32[32,1,2304]{2,1,0:T(1,128)} %get-tuple-element.31), calls=%async_computation.3 | async-start | bytes 589824 | tf_op jit(solution)/shard_map/all_to_all | solution.py:492
  54.8 0.2 collective-permute-start.3
  54.9 1.6 %collective-permute-start.4 = (f32[64,256]{1,0:T(8,128)S(1)}, f32[64,256]{1,0:T(8,128)S(1)}, u32[]{:S(2)}, u32[]{:S(2)}) collective-permute-start(f32[64,256]{1,0:T(8,128)S(1)} %get-tuple-element.34), channel_id=1, source_target_pairs={{0,2},{1,3},{2,0},{3,1},{4,6},{5,7},{6,4},{7,5},{8,10},{9,11},{10,... | collective-permute-start | bytes 196616 | tf_op jit(solution)/shard_map/ppermute | solution.py:529
  56.6 0.1 collective-permute-start.5
  56.7 0.0 collective-permute-done.3.refs_4_
  56.7 5.1 %collective-permute-done.4.refs_5_ = f32[64,256]{1,0:T(8,128)S(1)} collective-permute-done((f32[64,256]{1,0:T(8,128)S(1)}, f32[64,256]{1,0:T(8,128)S(1)}, u32[]{:S(2)}, u32[]{:S(2)}) %collective-permute-start.4) | collective-permute-done | bytes 65568 | tf_op jit(solution)/shard_map/ppermute | solution.py:529
  61.8 0.4 collective-permute-done.5.refs_6_
  62.2 3.9 %all-to-all-done.3.refs_2_ = f32[32,1,2304]{2,1,0:T(1,128)S(1)} async-done(((f32[32,1,2304]{2,1,0:T(1,128)}), f32[32,1,2304]{2,1,0:T(1,128)S(1)}, u32[]{:S(2)}, u32[]{:S(2)}) %all-to-all-start.3) | async-done | bytes 294944 | tf_op jit(solution)/shard_map/all_to_all | solution.py:492
  66.2 1.4 %shard_map.100 = (f32[48,1,2304]{2,1,0:T(1,128)}, f32[4,64,256]{2,1,0:T(8,128)}) custom-call(s32[1]{0:T(128)} %bitcast.refs_0_.device, s32[3,32]{1,0:T(4,128)S(1)} %bitcast.13, f32[32,1,2304]{2,1,0:T(1,128)S(1)} %all-to-all-done.3.refs_2_, f32[64,256]{1,0:T(8,128)S(1)} %get-tuple-element.32.refs_3_, f32[64,256]{1,0:T(8,128)S(1)} %collective-permute-done.3.refs_4_, ...), custom_call_target="tpu_custom_call" | custom-call | tf_op jit(solution)/shard_map/pallas_call | solution.py:452
Async XLA Ops:
  0.6 22.0 %copy-start = (bf16[2,256,256]{2,1,0:T(8,128)(2,1)S(1)}, bf16[2,256,256]{2,1,0:T(8,128)(2,1)}, u32[]{:S(2)}) copy-start(bf16[2,256,256]{2,1,0:T(8,128)(2,1)} %constant.15.clone.refs_2_.refs_3_.refs_4_.refs_5_) | copy-start | bytes 786436
  0.6 35.7 %copy-start.1 = (bf16[2,256,256]{2,1,0:T(8,128)(2,1)S(1)}, bf16[2,256,256]{2,1,0:T(8,128)(2,1)}, u32[]{:S(2)}) copy-start(bf16[2,256,256]{2,1,0:T(8,128)(2,1)} %constant.16.clone.refs_2_) | copy-start | bytes 786436
  0.7 49.4 %copy-start.2 = (s32[32,3]{0,1:T(4,128)S(1)}, s32[32,3]{0,1:T(4,128)}, u32[]{:S(2)}) copy-start(s32[32,3]{0,1:T(4,128)} %param.11) | copy-start | bytes 1156
  1.7 6.1 %collective-permute-start = (f32[64,256]{1,0:T(8,128)S(1)}, f32[64,256]{1,0:T(8,128)S(1)}, u32[]{:S(2)}, u32[]{:S(2)}) collective-permute-start(f32[64,256]{1,0:T(8,128)S(1)} %get-tuple-element.21), channel_id=1, source_target_pairs={{0,1},{1,0},{2,3},{3,2},{4,5},{5,4},{6,7},{7,6},{8,9},{9,8},{10,11... | collective-permute-start | bytes 196616 | tf_op jit(solution)/shard_map/ppermute | solution.py:529
  2.3 5.6 %collective-permute-start.1 = (f32[64,256]{1,0:T(8,128)S(1)}, f32[64,256]{1,0:T(8,128)S(1)}, u32[]{:S(2)}, u32[]{:S(2)}) collective-permute-start(f32[64,256]{1,0:T(8,128)S(1)} %get-tuple-element.22), channel_id=1, source_target_pairs={{0,2},{1,3},{2,0},{3,1},{4,6},{5,7},{6,4},{7,5},{8,10},{9,11},{10,... | collective-permute-start | bytes 196616 | tf_op jit(solution)/shard_map/ppermute | solution.py:529
  4.8 4.1 %collective-permute-start.2 = (f32[64,256]{1,0:T(8,128)S(1)}, f32[64,256]{1,0:T(8,128)S(1)}, u32[]{:S(2)}, u32[]{:S(2)}) collective-permute-start(f32[64,256]{1,0:T(8,128)S(1)} %get-tuple-element.23), channel_id=1, source_target_pairs={{0,3},{1,2},{2,1},{3,0},{4,7},{5,6},{6,5},{7,4},{8,11},{9,10},{10,... | collective-permute-start | bytes 196616 | tf_op jit(solution)/shard_map/ppermute | solution.py:529
  52.1 14.0 %all-to-all-start.3 = ((f32[32,1,2304]{2,1,0:T(1,128)}), f32[32,1,2304]{2,1,0:T(1,128)S(1)}, u32[]{:S(2)}, u32[]{:S(2)}) async-start(f32[32,1,2304]{2,1,0:T(1,128)} %get-tuple-element.31), calls=%async_computation.3 | async-start | bytes 589824 | tf_op jit(solution)/shard_map/all_to_all | solution.py:492
  54.8 1.9 %collective-permute-start.3 = (f32[64,256]{1,0:T(8,128)S(1)}, f32[64,256]{1,0:T(8,128)S(1)}, u32[]{:S(2)}, u32[]{:S(2)}) collective-permute-start(f32[64,256]{1,0:T(8,128)S(1)} %get-tuple-element.33), channel_id=1, source_target_pairs={{0,1},{1,0},{2,3},{3,2},{4,5},{5,4},{6,7},{7,6},{8,9},{9,8},{10,11... | collective-permute-start | bytes 196616 | tf_op jit(solution)/shard_map/ppermute | solution.py:529
  54.9 6.9 %collective-permute-start.4 = (f32[64,256]{1,0:T(8,128)S(1)}, f32[64,256]{1,0:T(8,128)S(1)}, u32[]{:S(2)}, u32[]{:S(2)}) collective-permute-start(f32[64,256]{1,0:T(8,128)S(1)} %get-tuple-element.34), channel_id=1, source_target_pairs={{0,2},{1,3},{2,0},{3,1},{4,6},{5,7},{6,4},{7,5},{8,10},{9,11},{10,... | collective-permute-start | bytes 196616 | tf_op jit(solution)/shard_map/ppermute | solution.py:529
  56.6 5.6 %collective-permute-start.5 = (f32[64,256]{1,0:T(8,128)S(1)}, f32[64,256]{1,0:T(8,128)S(1)}, u32[]{:S(2)}, u32[]{:S(2)}) collective-permute-start(f32[64,256]{1,0:T(8,128)S(1)} %get-tuple-element.35), channel_id=1, source_target_pairs={{0,3},{1,2},{2,1},{3,0},{4,7},{5,6},{6,5},{7,4},{8,11},{9,10},{10,... | collective-permute-start | bytes 196616 | tf_op jit(solution)/shard_map/ppermute | solution.py:529

commit v8 on v7

--- a/solution.py
+++ b/solution.py
@@ -260,15 +260,9 @@
     )(device, corners, span, occupations, orbitals)
 
 
-def plane_kernel(group, device, pieces, table_x, table_y, *refs):
-    *blocks, spectrum, exchange, density, packed = refs
-    slots = pieces.shape[0]
-    count_x, count_y = density.shape
-    sub = lax.rem(device[0], len(blocks))
-    x_dev = count_x // len(blocks)
-    for d, block in enumerate(blocks):
-        density[pl.ds(pl.multiple_of((sub ^ d) * x_dev, 8), x_dev), :] = block[...]
-    groups = slots // group
+def place_kernel(group, pieces, placed, packed):
+    count_x, count_y = placed.shape
+    groups = pieces.shape[0] // group
     column = lax.broadcasted_iota(jnp.int32, (count_x, CORE), 1)
     cell_x = lax.broadcasted_iota(jnp.int32, (count_x, CORE), 0)
     row = lax.broadcasted_iota(jnp.int32, (CORE, count_y), 0)
@@ -295,26 +289,43 @@
         lefts.append(jnp.where(left, 1.0, 0.0).astype(jnp.bfloat16))
         rights.append([product(part, right).astype(jnp.bfloat16) for part in (high, middle, low)])
     left = jnp.concatenate(lefts, axis=1)
-    placed = density[...]
-    for part in range(2, -1, -1):
-        placed = placed + product(left, jnp.concatenate([r[part] for r in rights], axis=0))
-    exchange[...] = exchange_correlation(placed)
-    spectrum[...] = times_table(table_times(table_x, placed), table_y)
-
-
-def plane_spectrum(device, pieces, group, table_x, table_y, blocks):
-    shape = (blocks[0].shape[0] * len(blocks), blocks[0].shape[1])
-    return small_call(
-        lambda *refs: plane_kernel(group, *refs),
+    total = product(left, jnp.concatenate([r[2] for r in rights], axis=0))
+    for part in (1, 0):
+        total = total + product(left, jnp.concatenate([r[part] for r in rights], axis=0))
+    placed[...] = total
+
+
+def placed_cores(pieces, group, count_x, count_y):
+    return small_call(
+        lambda *refs: place_kernel(group, *refs),
         12,
-        out_shape=(kept(shape), kept(shape)),
+        out_shape=kept((count_x, count_y)),
+        in_specs=in_vmem(1),
+        out_specs=in_vmem(1)[0],
+        scratch_shapes=[pltpu.VMEM((8 * (pieces.shape[0] // group), LANES), jnp.float32)],
+    )(pieces)
+
+
+def plane_kernel(device, placed, table_x, table_y, *refs):
+    *blocks, spectrum, exchange, outer = refs
+    sub = lax.rem(device[0], len(blocks))
+    x_dev = placed.shape[0] // len(blocks)
+    for d, block in enumerate(blocks):
+        outer[pl.ds(pl.multiple_of((sub ^ d) * x_dev, 8), x_dev), :] = block[...]
+    density = outer[...] + placed[...]
+    exchange[...] = exchange_correlation(density)
+    spectrum[...] = times_table(table_times(table_x, density), table_y)
+
+
+def plane_spectrum(device, placed, table_x, table_y, blocks):
+    return small_call(
+        plane_kernel,
+        12,
+        out_shape=(kept(placed.shape), kept(placed.shape)),
         in_specs=in_smem(1) + in_vmem(3 + len(blocks)),
         out_specs=in_vmem(2),
-        scratch_shapes=[
-            pltpu.VMEM(shape, jnp.float32),
-            pltpu.VMEM((8 * (pieces.shape[0] // group), LANES), jnp.float32),
-        ],
-    )(device, pieces, table_x, table_y, *blocks)
+        scratch_shapes=[pltpu.VMEM(placed.shape, jnp.float32)],
+    )(device, placed, table_x, table_y, *blocks)
 
 
 def wave_squares(index, count):
@@ -327,14 +338,13 @@
     rows, lanes = values.shape
     deep = rows // count_z
     transformed = table_times(table, values[...])
-    row = lax.broadcasted_iota(jnp.int32, (rows, lanes), 0)
-    lane = lax.broadcasted_iota(jnp.int32, (rows, lanes), 1)
-    cell = (device[0] * deep + row % deep) * lanes + lane
+    row = lax.broadcasted_iota(jnp.int32, (rows, 1), 0)
+    lane = lax.broadcasted_iota(jnp.int32, (1, lanes), 1)
+    assert deep == 1 or lanes == count_y
+    cell = (device[0] * deep + row % deep) * lanes
     square = (
-        wave_squares(row // deep, count_z)
-        + wave_squares(cell // count_y, count_x)
-        + wave_squares(cell % count_y, count_y)
-    )
+        wave_squares(row // deep, count_z) + wave_squares(cell // count_y, count_x)
+    ) + wave_squares(device[0] * deep * lanes % count_y + lane, count_y)
     scale = 4.0 * math.pi / float(count_z * count_x * count_y)
     kernel = jnp.where(square > 0, scale / jnp.where(square > 0, square, 1.0), 0.0)
     out[...] = table_times(table, transformed * kernel)
@@ -532,10 +542,9 @@
 
     blocks = outer_blocks(device, arguments.pop())
     blocks = swapped(blocks)
-    pieces = core_pieces(device, *arguments, slots, base, counts)
-    pieces, blocks = lax.optimization_barrier((pieces, blocks))
-    pieces = spread(pieces)
-    spectrum, exchange = plane_spectrum(device, pieces, group, table_x, table_y, blocks)
+    pieces = spread(core_pieces(device, *arguments, slots, base, counts))
+    placed = placed_cores(pieces, group, count_x, count_y)
+    spectrum, exchange = plane_spectrum(device, placed, table_x, table_y, blocks)
     chunk = (devices, deep, per_device // deep)
     spectrum = lax.all_to_all(spectrum.reshape(chunk), AXES, 0, 0, tiled=True)
     spectrum = column_hartree(

time: 67.8 us -> 66.6 us (0.982)
  blocking collectives: 39.1 us -> 26.5 us
  starting transfers between devices: 7.68 us -> 13.8 us
  waiting for transfers between devices: 10.5 us -> 15.1 us
    all_to_all x1 -> x0, blocking collectives: 13.8 us -> none  [spread(): return lax.all_to_all(pieces, AXES, 0, 0, tiled=True)]
    all_to_all x1 -> x2, starting transfers between devices: 2.61 us -> 9.94 us  [spread(): return lax.all_to_all(pieces, AXES, 0, 0, tiled=True)]
    all_to_all x1 -> x2, waiting for transfers between devices: 3.95 us -> 9.52 us  [spread(): return lax.all_to_all(pieces, AXES, 0, 0, tiled=True)]
    all_to_all x2, blocking collectives: 25.3 us -> 26.5 us  [body(): spectrum = lax.all_to_all(spectrum.reshape(chunk), AXES, 0, 0, tiled=True)]
    ppermute x6, starting transfers between devices: 5.08 us -> 3.88 us  [swapped(): lax.ppermute(block, 'sub', [(i, i ^ d) for i in range(sub_count)])]
    ppermute x6, waiting for transfers between devices: 6.55 us -> 5.53 us  [swapped(): lax.ppermute(block, 'sub', [(i, i ^ d) for i in range(sub_count)])]
    pallas_call x1, Pallas kernels: 2.97 us -> 3.68 us  [core_pieces(): small_call(lambda *refs: core_kernel(base, *counts, *refs), 8, out_shape=...]
  transfers between devices with their start and end apart: 7 -> 8, of which waited for: 4 -> 4; matrix products, arithmetic and copies ran while one was open for 0% -> 0% of each run, Pallas kernels for 4% -> 2%
where the time goes in v8:
time: 66.6 us; the launch traced here: 66.2 us
  blocking collectives  26.5 us (40%)
  waiting for transfers between devices  15.1 us (23%)
  starting transfers between devices  13.8 us (21%)
  Pallas kernels  10.1 us (15%)
  between operations  0.76 us (1%)
    all_to_all x2, blocking collectives, body(): spectrum = lax.all_to_all(spectrum.reshape(chunk), AXES, 0, 0, tiled=True)  26.5 us
    all_to_all x2, starting transfers between devices, spread(): return lax.all_to_all(pieces, AXES, 0, 0, tiled=True)  9.94 us
    all_to_all x2, waiting for transfers between devices, spread(): return lax.all_to_all(pieces, AXES, 0, 0, tiled=True)  9.52 us
    ppermute x6, waiting for transfers between devices, swapped(): lax.ppermute(block, 'sub', [(i, i ^ d) for i in range(sub_count)])  5.53 us
    ppermute x6, starting transfers between devices, swapped(): lax.ppermute(block, 'sub', [(i, i ^ d) for i in range(sub_count)])  3.88 us
    pallas_call x1, Pallas kernels, core_pieces(): small_call(lambda *refs: core_kernel(base, *counts, *refs), 8, out_shape=...  3.68 us
    pallas_call x1, Pallas kernels, plane_windows(): small_call(lambda *refs: window_kernel(fragment, *refs), 12, out_shape=[b...  2.06 us
    pallas_call x1, Pallas kernels, outputs(): small_call(lambda *refs: output_kernel(base, *refs), 4, out_shape=(jax.Sh...  1.38 us
  transfers between devices with their start and end apart: 8, of which 4 were waited for; matrix products, arithmetic and copies ran while one was open for 0% of the time, Pallas kernels for 2%

profile of v8, /device:TPU:0, one launch (start us, length us, event | category | flops | bytes accessed | tf_op | source)
XLA Modules:
  0.0 66.2 jit_solution(6310511543812066200)
XLA Ops:
  0.6 0.0 copy-start
  0.6 0.0 copy-start.1
  0.7 0.0 copy-start.2
  0.7 3.7 %shard_map.95 = f32[32,1,1152]{2,1,0:T(1,128)} custom-call(s32[1]{0:T(128)} %bitcast.refs_0_.device, s32[3,32]{1,0:T(4,128)} %bitcast.11, s32[1,6]{1,0:T(1,128)} %refs_2_.2, s32[1,16]{1,0:T(1,128)} %refs_3_.1, bf16[1,16,110592]{2,1,0:T(8,128)(2,1)} %refs_4_.2), custom_call_target="tpu_custom_call" | custom-call | flops 40000000 | bytes 4000000 | tf_op jit(solution)/shard_map/pallas_call | solution.py:243
  4.4 7.3 %all-to-all-start = ((f32[32,1,1152]{2,1,0:T(1,128)}), f32[32,1,1152]{2,1,0:T(1,128)S(1)}, u32[]{:S(2)}, u32[]{:S(2)}) async-start(f32[32,1,1152]{2,1,0:T(1,128)} %shard_map.95), calls=%async_computation | async-start | bytes 294912 | tf_op jit(solution)/shard_map/all_to_all | solution.py:502
  11.7 1.0 %shard_map.97 = (f32[64,256]{1,0:T(8,128)S(1)}, f32[64,256]{1,0:T(8,128)S(1)}, f32[64,256]{1,0:T(8,128)S(1)}, f32[64,256]{1,0:T(8,128)S(1)}) custom-call(s32[1]{0:T(128)} %bitcast.refs_0_.device, f32[4,64,256]{2,1,0:T(8,128)} %outer.1), custom_call_target="tpu_custom_call" | custom-call | tf_op jit(solution)/shard_map/pallas_call | solution.py:134
  12.7 0.3 collective-permute-start
  13.0 1.6 %collective-permute-start.1 = (f32[64,256]{1,0:T(8,128)S(1)}, f32[64,256]{1,0:T(8,128)S(1)}, u32[]{:S(2)}, u32[]{:S(2)}) collective-permute-start(f32[64,256]{1,0:T(8,128)S(1)} %get-tuple-element.17), channel_id=1, source_target_pairs={{0,2},{1,3},{2,0},{3,1},{4,6},{5,7},{6,4},{7,5},{8,10},{9,11},{10,... | collective-permute-start | bytes 196616 | tf_op jit(solution)/shard_map/ppermute | solution.py:539
  14.6 0.0 collective-permute-start.2
  14.6 5.6 %all-to-all-done.refs_0_ = f32[32,1,1152]{2,1,0:T(1,128)S(1)} async-done(((f32[32,1,1152]{2,1,0:T(1,128)}), f32[32,1,1152]{2,1,0:T(1,128)S(1)}, u32[]{:S(2)}, u32[]{:S(2)}) %all-to-all-start) | async-done | bytes 147488 | tf_op jit(solution)/shard_map/all_to_all | solution.py:502
  20.2 0.5 shard_map.96.placed
  20.7 0.0 collective-permute-done.refs_1_
  20.7 0.0 collective-permute-done.1.refs_2_
  20.8 0.0 collective-permute-done.2.refs_3_
  20.8 0.0 copy-done
  20.8 0.7 %shard_map.98 = (f32[256,256]{1,0:T(8,128)S(1)}, f32[256,256]{1,0:T(8,128)S(1)}) custom-call(s32[1]{0:T(128)} %bitcast.refs_0_.device, f32[256,256]{1,0:T(8,128)S(1)} %shard_map.96.placed, bf16[2,256,256]{2,1,0:T(8,128)(2,1)S(1)} %copy-done, bf16[2,256,256]{2,1,0:T(8,128)(2,1)S(1)} %copy-done, f32[64,256]{1,0:T(8,128)S(1)} %get-tuple-element.15.refs_0_, ...), custom_call_target="tpu_custom_call" | custom-call | tf_op jit(solution)/shard_map/pallas_call | solution.py:321
  21.5 13.8 %all_to_all.20 = f32[32,8,256]{2,1,0:T(8,128)S(1)} all-to-all(f32[32,8,256]{2,1,0:T(8,128)S(1)} %bitcast.10), channel_id=1, replica_groups=mesh['slab'=8,'sub'=4] {'slab','sub'}, dimensions={0} | all-to-all | bytes 524288 | tf_op jit(solution)/shard_map/all_to_all | solution.py:549
  35.3 0.0 copy-done.1
  35.3 0.7 %shard_map.99 = f32[256,256]{1,0:T(8,128)S(1)} custom-call(s32[1]{0:T(128)} %bitcast.refs_0_.device, f32[256,256]{1,0:T(8,128)S(1)} %bitcast.8, bf16[2,256,256]{2,1,0:T(8,128)(2,1)S(1)} %copy-done.1), custom_call_target="tpu_custom_call" | custom-call | tf_op jit(solution)/shard_map/pallas_call | solution.py:354
  36.0 12.8 %all_to_all.21 = f32[32,8,256]{2,1,0:T(8,128)S(1)} all-to-all(f32[32,8,256]{2,1,0:T(8,128)S(1)} %bitcast.9), channel_id=1, replica_groups=mesh['slab'=8,'sub'=4] {'slab','sub'}, dimensions={0} | all-to-all | bytes 524288 | tf_op jit(solution)/shard_map/all_to_all | solution.py:553
  48.8 0.0 copy-done.2
  48.8 2.1 %shard_map.100 = (f32[64,256]{1,0:T(8,128)S(1)}, f32[64,256]{1,0:T(8,128)S(1)}, f32[64,256]{1,0:T(8,128)S(1)}, f32[64,256]{1,0:T(8,128)S(1)}, f32[32,1,2304]{2,1,0:T(1,128)}) custom-call(s32[1]{0:T(128)} %bitcast.refs_0_.device, s32[3,32]{1,0:T(4,128)S(1)} %bitcast.12, f32[256,256]{1,0:T(8,128)S(1)} %bitcast.7, f32[256,256]{1,0:T(8,128)S(1)} %get-tuple-element.20.refs_3_, ...), custom_call_target="tpu_custom_call" | custom-call | tf_op jit(solution)/shard_map/pallas_call | solution.py:418
  50.9 2.6 %all-to-all-start.3 = ((f32[32,1,2304]{2,1,0:T(1,128)}), f32[32,1,2304]{2,1,0:T(1,128)S(1)}, u32[]{:S(2)}, u32[]{:S(2)}) async-start(f32[32,1,2304]{2,1,0:T(1,128)} %get-tuple-element.21), calls=%async_computation.3 | async-start | bytes 589824 | tf_op jit(solution)/shard_map/all_to_all | solution.py:502
  53.5 0.2 collective-permute-start.3
  53.7 1.6 %collective-permute-start.4 = (f32[64,256]{1,0:T(8,128)S(1)}, f32[64,256]{1,0:T(8,128)S(1)}, u32[]{:S(2)}, u32[]{:S(2)}) collective-permute-start(f32[64,256]{1,0:T(8,128)S(1)} %get-tuple-element.24), channel_id=1, source_target_pairs={{0,2},{1,3},{2,0},{3,1},{4,6},{5,7},{6,4},{7,5},{8,10},{9,11},{10,... | collective-permute-start | bytes 196616 | tf_op jit(solution)/shard_map/ppermute | solution.py:539
  55.3 0.1 collective-permute-start.5
  55.4 0.0 collective-permute-done.3.refs_4_
  55.4 5.1 %collective-permute-done.4.refs_5_ = f32[64,256]{1,0:T(8,128)S(1)} collective-permute-done((f32[64,256]{1,0:T(8,128)S(1)}, f32[64,256]{1,0:T(8,128)S(1)}, u32[]{:S(2)}, u32[]{:S(2)}) %collective-permute-start.4) | collective-permute-done | bytes 65568 | tf_op jit(solution)/shard_map/ppermute | solution.py:539
  60.5 0.4 collective-permute-done.5.refs_6_
  60.9 3.9 %all-to-all-done.3.refs_2_ = f32[32,1,2304]{2,1,0:T(1,128)S(1)} async-done(((f32[32,1,2304]{2,1,0:T(1,128)}), f32[32,1,2304]{2,1,0:T(1,128)S(1)}, u32[]{:S(2)}, u32[]{:S(2)}) %all-to-all-start.3) | async-done | bytes 294944 | tf_op jit(solution)/shard_map/all_to_all | solution.py:502
  64.9 1.4 %shard_map.101 = (f32[48,1,2304]{2,1,0:T(1,128)}, f32[4,64,256]{2,1,0:T(8,128)}) custom-call(s32[1]{0:T(128)} %bitcast.refs_0_.device, s32[3,32]{1,0:T(4,128)S(1)} %bitcast.13, f32[32,1,2304]{2,1,0:T(1,128)S(1)} %all-to-all-done.3.refs_2_, f32[64,256]{1,0:T(8,128)S(1)} %get-tuple-element.22.refs_3_, f32[64,256]{1,0:T(8,128)S(1)} %collective-permute-done.3.refs_4_, ...), custom_call_target="tpu_custom_call" | custom-call | tf_op jit(solution)/shard_map/pallas_call | solution.py:462
Async XLA Ops:
  0.6 20.1 %copy-start = (bf16[2,256,256]{2,1,0:T(8,128)(2,1)S(1)}, bf16[2,256,256]{2,1,0:T(8,128)(2,1)}, u32[]{:S(2)}) copy-start(bf16[2,256,256]{2,1,0:T(8,128)(2,1)} %constant.15.clone.table_x.table_y.refs_4_.refs_5_) | copy-start | bytes 786436
  0.6 34.6 %copy-start.1 = (bf16[2,256,256]{2,1,0:T(8,128)(2,1)S(1)}, bf16[2,256,256]{2,1,0:T(8,128)(2,1)}, u32[]{:S(2)}) copy-start(bf16[2,256,256]{2,1,0:T(8,128)(2,1)} %constant.16.clone.refs_2_) | copy-start | bytes 786436
  0.7 48.1 %copy-start.2 = (s32[32,3]{0,1:T(4,128)S(1)}, s32[32,3]{0,1:T(4,128)}, u32[]{:S(2)}) copy-start(s32[32,3]{0,1:T(4,128)} %param.11) | copy-start | bytes 1156
  4.4 15.9 %all-to-all-start = ((f32[32,1,1152]{2,1,0:T(1,128)}), f32[32,1,1152]{2,1,0:T(1,128)S(1)}, u32[]{:S(2)}, u32[]{:S(2)}) async-start(f32[32,1,1152]{2,1,0:T(1,128)} %shard_map.95), calls=%async_computation | async-start | bytes 294912 | tf_op jit(solution)/shard_map/all_to_all | solution.py:502
  12.7 8.0 %collective-permute-start = (f32[64,256]{1,0:T(8,128)S(1)}, f32[64,256]{1,0:T(8,128)S(1)}, u32[]{:S(2)}, u32[]{:S(2)}) collective-permute-start(f32[64,256]{1,0:T(8,128)S(1)} %get-tuple-element.16), channel_id=1, source_target_pairs={{0,1},{1,0},{2,3},{3,2},{4,5},{5,4},{6,7},{7,6},{8,9},{9,8},{10,11... | collective-permute-start | bytes 196616 | tf_op jit(solution)/shard_map/ppermute | solution.py:539
  13.0 7.7 %collective-permute-start.1 = (f32[64,256]{1,0:T(8,128)S(1)}, f32[64,256]{1,0:T(8,128)S(1)}, u32[]{:S(2)}, u32[]{:S(2)}) collective-permute-start(f32[64,256]{1,0:T(8,128)S(1)} %get-tuple-element.17), channel_id=1, source_target_pairs={{0,2},{1,3},{2,0},{3,1},{4,6},{5,7},{6,4},{7,5},{8,10},{9,11},{10,... | collective-permute-start | bytes 196616 | tf_op jit(solution)/shard_map/ppermute | solution.py:539
  14.6 6.1 %collective-permute-start.2 = (f32[64,256]{1,0:T(8,128)S(1)}, f32[64,256]{1,0:T(8,128)S(1)}, u32[]{:S(2)}, u32[]{:S(2)}) collective-permute-start(f32[64,256]{1,0:T(8,128)S(1)} %get-tuple-element.18), channel_id=1, source_target_pairs={{0,3},{1,2},{2,1},{3,0},{4,7},{5,6},{6,5},{7,4},{8,11},{9,10},{10,... | collective-permute-start | bytes 196616 | tf_op jit(solution)/shard_map/ppermute | solution.py:539
  50.9 14.0 %all-to-all-start.3 = ((f32[32,1,2304]{2,1,0:T(1,128)}), f32[32,1,2304]{2,1,0:T(1,128)S(1)}, u32[]{:S(2)}, u32[]{:S(2)}) async-start(f32[32,1,2304]{2,1,0:T(1,128)} %get-tuple-element.21), calls=%async_computation.3 | async-start | bytes 589824 | tf_op jit(solution)/shard_map/all_to_all | solution.py:502
  53.5 1.9 %collective-permute-start.3 = (f32[64,256]{1,0:T(8,128)S(1)}, f32[64,256]{1,0:T(8,128)S(1)}, u32[]{:S(2)}, u32[]{:S(2)}) collective-permute-start(f32[64,256]{1,0:T(8,128)S(1)} %get-tuple-element.23), channel_id=1, source_target_pairs={{0,1},{1,0},{2,3},{3,2},{4,5},{5,4},{6,7},{7,6},{8,9},{9,8},{10,11... | collective-permute-start | bytes 196616 | tf_op jit(solution)/shard_map/ppermute | solution.py:539
  53.7 6.9 %collective-permute-start.4 = (f32[64,256]{1,0:T(8,128)S(1)}, f32[64,256]{1,0:T(8,128)S(1)}, u32[]{:S(2)}, u32[]{:S(2)}) collective-permute-start(f32[64,256]{1,0:T(8,128)S(1)} %get-tuple-element.24), channel_id=1, source_target_pairs={{0,2},{1,3},{2,0},{3,1},{4,6},{5,7},{6,4},{7,5},{8,10},{9,11},{10,... | collective-permute-start | bytes 196616 | tf_op jit(solution)/shard_map/ppermute | solution.py:539
  55.3 5.6 %collective-permute-start.5 = (f32[64,256]{1,0:T(8,128)S(1)}, f32[64,256]{1,0:T(8,128)S(1)}, u32[]{:S(2)}, u32[]{:S(2)}) collective-permute-start(f32[64,256]{1,0:T(8,128)S(1)} %get-tuple-element.25), channel_id=1, source_target_pairs={{0,3},{1,2},{2,1},{3,0},{4,7},{5,6},{6,5},{7,4},{8,11},{9,10},{10,... | collective-permute-start | bytes 196616 | tf_op jit(solution)/shard_map/ppermute | solution.py:539

commit v9 on v8

--- a/solution.py
+++ b/solution.py
@@ -116,38 +116,14 @@
     return fours[0]
 
 
-def block_kernel(device, outer, *refs):
-    *blocks, filled = refs
-    sub = lax.rem(device[0], len(blocks))
-    fills = [
-        pltpu.make_async_copy(outer.at[sub ^ d], block, filled.at[d])
-        for d, block in enumerate(blocks)
-    ]
-    for fill in fills:
-        fill.start()
-    for fill in fills:
-        fill.wait()
-
-
-def outer_blocks(device, outer):
-    count = outer.shape[0]
-    return small_call(
-        block_kernel,
-        4,
-        out_shape=[kept(outer.shape[1:])] * count,
-        in_specs=in_smem(1) + anywhere(1),
-        out_specs=in_vmem(count),
-        scratch_shapes=[pltpu.SemaphoreType.DMA((count,))],
-    )(device, outer)
-
-
 CHUNK = 8
 
 
 def core_kernel(
     base, depth, count_x, count_y, device, corner_table, span_row, occupation_row, orbitals,
-    out, buffer, sums, rows, corners, span, occupations, arrived, staged,
+    outer, out, *refs,
 ):
+    *blocks, buffer, sums, rows, corners, span, occupations, arrived, staged, filled = refs
     own, slots, orbital_count = device[0], out.shape[0], orbitals.shape[1]
     scalars = [
         pltpu.make_async_copy(source, target, staged.at[n])
@@ -165,6 +141,13 @@
             pltpu.make_async_copy(orbitals.at[0, :, part], buffer.at[:, part], arrived.at[c])
         )
         copies[c].start()
+    sub = lax.rem(own, len(blocks))
+    fills = [
+        pltpu.make_async_copy(outer.at[sub ^ d], block, filled.at[d])
+        for d, block in enumerate(blocks)
+    ]
+    for fill in fills:
+        fill.start()
     for copy in scalars:
         copy.wait()
     first_z, first_x, first_y = span[0, 0], span[0, 1], span[0, 2]
@@ -236,16 +219,18 @@
         return carry
 
     repeated(slots // many, pack)
-
-
-def core_pieces(device, corners, span, occupations, orbitals, slots, base, counts):
+    for fill in fills:
+        fill.wait()
+
+
+def core_pieces(device, corners, span, occupations, orbitals, outer, slots, base, counts):
     orbital_count = orbitals.shape[1]
     return small_call(
         lambda *refs: core_kernel(base, *counts, *refs),
         8,
-        out_shape=kept((slots, 1, PIECE)),
-        in_specs=in_smem(1) + anywhere(4),
-        out_specs=in_vmem(1)[0],
+        out_shape=[kept((slots, 1, PIECE))] + [kept(outer.shape[1:])] * outer.shape[0],
+        in_specs=in_smem(1) + anywhere(5),
+        out_specs=in_vmem(1 + outer.shape[0]),
         scratch_shapes=[
             pltpu.VMEM((orbital_count, BOX * PLANE), orbitals.dtype),
             pltpu.VMEM((CORE * GROUPS, WIDE), jnp.float32),
@@ -255,9 +240,10 @@
             pltpu.SMEM(occupations.shape, jnp.int32),
             pltpu.SemaphoreType.DMA((BOX // CHUNK,)),
             pltpu.SemaphoreType.DMA((3,)),
+            pltpu.SemaphoreType.DMA((outer.shape[0],)),
         ],
         cost_estimate=pl.CostEstimate(flops=40_000_000, bytes_accessed=4_000_000, transcendentals=0),
-    )(device, corners, span, occupations, orbitals)
+    )(device, corners, span, occupations, orbitals, outer)
 
 
 def place_kernel(group, pieces, placed, packed):
@@ -540,9 +526,9 @@
             for d, block in enumerate(blocks)
         ]
 
-    blocks = outer_blocks(device, arguments.pop())
+    pieces, *blocks = core_pieces(device, *arguments, slots, base, counts)
     blocks = swapped(blocks)
-    pieces = spread(core_pieces(device, *arguments, slots, base, counts))
+    pieces = spread(pieces)
     placed = placed_cores(pieces, group, count_x, count_y)
     spectrum, exchange = plane_spectrum(device, placed, table_x, table_y, blocks)
     chunk = (devices, deep, per_device // deep)

time: 66.6 us -> 65.9 us (0.989)
  Pallas kernels: 10.1 us -> 9.13 us
  waiting for transfers between devices: 15.1 us -> 16 us
    pallas_call x1 -> x0, Pallas kernels: 0.98 us -> none  [outer_blocks(): small_call(block_kernel, 4, out_shape=[kept(outer.shape[1:])] * count, in...]
    all_to_all x2, waiting for transfers between devices: 9.52 us -> 10.4 us  [spread(): return lax.all_to_all(pieces, AXES, 0, 0, tiled=True)]
    all_to_all x2, blocking collectives: 26.5 us -> 25.9 us  [body(): spectrum = lax.all_to_all(spectrum.reshape(chunk), AXES, 0, 0, tiled=True)]
  transfers between devices with their start and end apart: 8 -> 8, of which waited for: 4 -> 4; matrix products, arithmetic and copies ran while one was open for 0% -> 0% of each run, Pallas kernels for 2% -> 1%
where the time goes in v9:
time: 65.9 us; the launch traced here: 65.6 us
  blocking collectives  25.9 us (39%)
  waiting for transfers between devices  16 us (24%)
  starting transfers between devices  13.8 us (21%)
  Pallas kernels  9.13 us (14%)
  between operations  0.75 us (1%)
    all_to_all x2, blocking collectives, body(): spectrum = lax.all_to_all(spectrum.reshape(chunk), AXES, 0, 0, tiled=True)  25.9 us
    all_to_all x2, waiting for transfers between devices, spread(): return lax.all_to_all(pieces, AXES, 0, 0, tiled=True)  10.4 us
    all_to_all x2, starting transfers between devices, spread(): return lax.all_to_all(pieces, AXES, 0, 0, tiled=True)  9.94 us
    ppermute x6, waiting for transfers between devices, swapped(): lax.ppermute(block, 'sub', [(i, i ^ d) for i in range(sub_count)])  5.53 us
    ppermute x6, starting transfers between devices, swapped(): lax.ppermute(block, 'sub', [(i, i ^ d) for i in range(sub_count)])  3.88 us
    pallas_call x1, Pallas kernels, core_pieces(): small_call(lambda *refs: core_kernel(base, *counts, *refs), 8, out_shape=...  3.73 us
    pallas_call x1, Pallas kernels, plane_windows(): small_call(lambda *refs: window_kernel(fragment, *refs), 12, out_shape=[b...  2.06 us
    pallas_call x1, Pallas kernels, outputs(): small_call(lambda *refs: output_kernel(base, *refs), 4, out_shape=(jax.Sh...  1.38 us
  transfers between devices with their start and end apart: 8, of which 4 were waited for; matrix products, arithmetic and copies ran while one was open for 0% of the time, Pallas kernels for 1%

profile of v9, /device:TPU:0, one launch (start us, length us, event | category | flops | bytes accessed | tf_op | source)
XLA Modules:
  0.0 65.6 jit_solution(12910423064634583432)
XLA Ops:
  0.6 0.0 copy-start
  0.6 0.0 copy-start.1
  0.7 0.0 copy-start.2
  0.7 3.7 %shard_map.95 = (f32[32,1,1152]{2,1,0:T(1,128)}, f32[64,256]{1,0:T(8,128)S(1)}, f32[64,256]{1,0:T(8,128)S(1)}, f32[64,256]{1,0:T(8,128)S(1)}, f32[64,256]{1,0:T(8,128)S(1)}) custom-call(s32[1]{0:T(128)} %bitcast.refs_0_.device, s32[3,32]{1,0:T(4,128)} %bitcast.11, s32[1,6]{1,0:T(1,128)} %refs_2_.2, s32[1,16]{1,0:T(1,128)} %refs_3_.1, ...), custom_call_target="tpu_custom_call" | custom-call | flops 40000000 | bytes 4000000 | tf_op jit(solution)/shard_map/pallas_call | solution.py:228
  4.4 7.3 %all-to-all-start = ((f32[32,1,1152]{2,1,0:T(1,128)}), f32[32,1,1152]{2,1,0:T(1,128)S(1)}, u32[]{:S(2)}, u32[]{:S(2)}) async-start(f32[32,1,1152]{2,1,0:T(1,128)} %get-tuple-element.16), calls=%async_computation | async-start | bytes 294912 | tf_op jit(solution)/shard_map/all_to_all | solution.py:488
  11.8 0.3 collective-permute-start
  12.1 1.6 %collective-permute-start.1 = (f32[64,256]{1,0:T(8,128)S(1)}, f32[64,256]{1,0:T(8,128)S(1)}, u32[]{:S(2)}, u32[]{:S(2)}) collective-permute-start(f32[64,256]{1,0:T(8,128)S(1)} %get-tuple-element.19), channel_id=1, source_target_pairs={{0,2},{1,3},{2,0},{3,1},{4,6},{5,7},{6,4},{7,5},{8,10},{9,11},{10,... | collective-permute-start | bytes 196616 | tf_op jit(solution)/shard_map/ppermute | solution.py:525
  13.7 0.0 collective-permute-start.2
  13.7 6.5 %all-to-all-done.refs_0_ = f32[32,1,1152]{2,1,0:T(1,128)S(1)} async-done(((f32[32,1,1152]{2,1,0:T(1,128)}), f32[32,1,1152]{2,1,0:T(1,128)S(1)}, u32[]{:S(2)}, u32[]{:S(2)}) %all-to-all-start) | async-done | bytes 147488 | tf_op jit(solution)/shard_map/all_to_all | solution.py:488
  20.2 0.5 shard_map.96.placed
  20.7 0.0 collective-permute-done.refs_1_
  20.7 0.0 collective-permute-done.1.refs_2_
  20.7 0.0 collective-permute-done.2.refs_3_
  20.7 0.0 copy-done
  20.8 0.7 %shard_map.97 = (f32[256,256]{1,0:T(8,128)S(1)}, f32[256,256]{1,0:T(8,128)S(1)}) custom-call(s32[1]{0:T(128)} %bitcast.refs_0_.device, f32[256,256]{1,0:T(8,128)S(1)} %shard_map.96.placed, bf16[2,256,256]{2,1,0:T(8,128)(2,1)S(1)} %copy-done, bf16[2,256,256]{2,1,0:T(8,128)(2,1)S(1)} %copy-done, f32[64,256]{1,0:T(8,128)S(1)} %get-tuple-element.17.refs_0_, ...), custom_call_target="tpu_custom_call" | custom-call | tf_op jit(solution)/shard_map/pallas_call | solution.py:307
  21.5 13.1 %all_to_all.20 = f32[32,8,256]{2,1,0:T(8,128)S(1)} all-to-all(f32[32,8,256]{2,1,0:T(8,128)S(1)} %bitcast.10), channel_id=1, replica_groups=mesh['slab'=8,'sub'=4] {'slab','sub'}, dimensions={0} | all-to-all | bytes 524288 | tf_op jit(solution)/shard_map/all_to_all | solution.py:535
  34.6 0.0 copy-done.1
  34.6 0.7 %shard_map.98 = f32[256,256]{1,0:T(8,128)S(1)} custom-call(s32[1]{0:T(128)} %bitcast.refs_0_.device, f32[256,256]{1,0:T(8,128)S(1)} %bitcast.8, bf16[2,256,256]{2,1,0:T(8,128)(2,1)S(1)} %copy-done.1), custom_call_target="tpu_custom_call" | custom-call | tf_op jit(solution)/shard_map/pallas_call | solution.py:340
  35.3 12.8 %all_to_all.21 = f32[32,8,256]{2,1,0:T(8,128)S(1)} all-to-all(f32[32,8,256]{2,1,0:T(8,128)S(1)} %bitcast.9), channel_id=1, replica_groups=mesh['slab'=8,'sub'=4] {'slab','sub'}, dimensions={0} | all-to-all | bytes 524288 | tf_op jit(solution)/shard_map/all_to_all | solution.py:539
  48.1 0.0 copy-done.2
  48.1 2.1 %shard_map.99 = (f32[64,256]{1,0:T(8,128)S(1)}, f32[64,256]{1,0:T(8,128)S(1)}, f32[64,256]{1,0:T(8,128)S(1)}, f32[64,256]{1,0:T(8,128)S(1)}, f32[32,1,2304]{2,1,0:T(1,128)}) custom-call(s32[1]{0:T(128)} %bitcast.refs_0_.device, s32[3,32]{1,0:T(4,128)S(1)} %bitcast.12, f32[256,256]{1,0:T(8,128)S(1)} %bitcast.7, f32[256,256]{1,0:T(8,128)S(1)} %get-tuple-element.22.refs_3_, ...), custom_call_target="tpu_custom_call" | custom-call | tf_op jit(solution)/shard_map/pallas_call | solution.py:404
  50.2 2.6 %all-to-all-start.3 = ((f32[32,1,2304]{2,1,0:T(1,128)}), f32[32,1,2304]{2,1,0:T(1,128)S(1)}, u32[]{:S(2)}, u32[]{:S(2)}) async-start(f32[32,1,2304]{2,1,0:T(1,128)} %get-tuple-element.23), calls=%async_computation.3 | async-start | bytes 589824 | tf_op jit(solution)/shard_map/all_to_all | solution.py:488
  52.8 0.2 collective-permute-start.3
  53.0 1.6 %collective-permute-start.4 = (f32[64,256]{1,0:T(8,128)S(1)}, f32[64,256]{1,0:T(8,128)S(1)}, u32[]{:S(2)}, u32[]{:S(2)}) collective-permute-start(f32[64,256]{1,0:T(8,128)S(1)} %get-tuple-element.26), channel_id=1, source_target_pairs={{0,2},{1,3},{2,0},{3,1},{4,6},{5,7},{6,4},{7,5},{8,10},{9,11},{10,... | collective-permute-start | bytes 196616 | tf_op jit(solution)/shard_map/ppermute | solution.py:525
  54.6 0.1 collective-permute-start.5
  54.7 0.0 collective-permute-done.3.refs_4_
  54.7 5.1 %collective-permute-done.4.refs_5_ = f32[64,256]{1,0:T(8,128)S(1)} collective-permute-done((f32[64,256]{1,0:T(8,128)S(1)}, f32[64,256]{1,0:T(8,128)S(1)}, u32[]{:S(2)}, u32[]{:S(2)}) %collective-permute-start.4) | collective-permute-done | bytes 65568 | tf_op jit(solution)/shard_map/ppermute | solution.py:525
  59.8 0.4 collective-permute-done.5.refs_6_
  60.2 3.9 %all-to-all-done.3.refs_2_ = f32[32,1,2304]{2,1,0:T(1,128)S(1)} async-done(((f32[32,1,2304]{2,1,0:T(1,128)}), f32[32,1,2304]{2,1,0:T(1,128)S(1)}, u32[]{:S(2)}, u32[]{:S(2)}) %all-to-all-start.3) | async-done | bytes 294944 | tf_op jit(solution)/shard_map/all_to_all | solution.py:488
  64.2 1.4 %shard_map.100 = (f32[48,1,2304]{2,1,0:T(1,128)}, f32[4,64,256]{2,1,0:T(8,128)}) custom-call(s32[1]{0:T(128)} %bitcast.refs_0_.device, s32[3,32]{1,0:T(4,128)S(1)} %bitcast.13, f32[32,1,2304]{2,1,0:T(1,128)S(1)} %all-to-all-done.3.refs_2_, f32[64,256]{1,0:T(8,128)S(1)} %get-tuple-element.24.refs_3_, f32[64,256]{1,0:T(8,128)S(1)} %collective-permute-done.3.refs_4_, ...), custom_call_target="tpu_custom_call" | custom-call | tf_op jit(solution)/shard_map/pallas_call | solution.py:448
Async XLA Ops:
  0.6 20.1 %copy-start = (bf16[2,256,256]{2,1,0:T(8,128)(2,1)S(1)}, bf16[2,256,256]{2,1,0:T(8,128)(2,1)}, u32[]{:S(2)}) copy-start(bf16[2,256,256]{2,1,0:T(8,128)(2,1)} %constant.15.clone.table_x.table_y.refs_4_.refs_5_) | copy-start | bytes 786436
  0.6 33.9 %copy-start.1 = (bf16[2,256,256]{2,1,0:T(8,128)(2,1)S(1)}, bf16[2,256,256]{2,1,0:T(8,128)(2,1)}, u32[]{:S(2)}) copy-start(bf16[2,256,256]{2,1,0:T(8,128)(2,1)} %constant.16.clone.refs_2_) | copy-start | bytes 786436
  0.7 47.4 %copy-start.2 = (s32[32,3]{0,1:T(4,128)S(1)}, s32[32,3]{0,1:T(4,128)}, u32[]{:S(2)}) copy-start(s32[32,3]{0,1:T(4,128)} %param.11) | copy-start | bytes 1156
  4.4 15.8 %all-to-all-start = ((f32[32,1,1152]{2,1,0:T(1,128)}), f32[32,1,1152]{2,1,0:T(1,128)S(1)}, u32[]{:S(2)}, u32[]{:S(2)}) async-start(f32[32,1,1152]{2,1,0:T(1,128)} %get-tuple-element.16), calls=%async_computation | async-start | bytes 294912 | tf_op jit(solution)/shard_map/all_to_all | solution.py:488
  11.8 9.0 %collective-permute-start = (f32[64,256]{1,0:T(8,128)S(1)}, f32[64,256]{1,0:T(8,128)S(1)}, u32[]{:S(2)}, u32[]{:S(2)}) collective-permute-start(f32[64,256]{1,0:T(8,128)S(1)} %get-tuple-element.18), channel_id=1, source_target_pairs={{0,1},{1,0},{2,3},{3,2},{4,5},{5,4},{6,7},{7,6},{8,9},{9,8},{10,11... | collective-permute-start | bytes 196616 | tf_op jit(solution)/shard_map/ppermute | solution.py:525
  12.1 8.7 %collective-permute-start.1 = (f32[64,256]{1,0:T(8,128)S(1)}, f32[64,256]{1,0:T(8,128)S(1)}, u32[]{:S(2)}, u32[]{:S(2)}) collective-permute-start(f32[64,256]{1,0:T(8,128)S(1)} %get-tuple-element.19), channel_id=1, source_target_pairs={{0,2},{1,3},{2,0},{3,1},{4,6},{5,7},{6,4},{7,5},{8,10},{9,11},{10,... | collective-permute-start | bytes 196616 | tf_op jit(solution)/shard_map/ppermute | solution.py:525
  13.7 7.0 %collective-permute-start.2 = (f32[64,256]{1,0:T(8,128)S(1)}, f32[64,256]{1,0:T(8,128)S(1)}, u32[]{:S(2)}, u32[]{:S(2)}) collective-permute-start(f32[64,256]{1,0:T(8,128)S(1)} %get-tuple-element.20), channel_id=1, source_target_pairs={{0,3},{1,2},{2,1},{3,0},{4,7},{5,6},{6,5},{7,4},{8,11},{9,10},{10,... | collective-permute-start | bytes 196616 | tf_op jit(solution)/shard_map/ppermute | solution.py:525
  50.2 14.0 %all-to-all-start.3 = ((f32[32,1,2304]{2,1,0:T(1,128)}), f32[32,1,2304]{2,1,0:T(1,128)S(1)}, u32[]{:S(2)}, u32[]{:S(2)}) async-start(f32[32,1,2304]{2,1,0:T(1,128)} %get-tuple-element.23), calls=%async_computation.3 | async-start | bytes 589824 | tf_op jit(solution)/shard_map/all_to_all | solution.py:488
  52.8 1.9 %collective-permute-start.3 = (f32[64,256]{1,0:T(8,128)S(1)}, f32[64,256]{1,0:T(8,128)S(1)}, u32[]{:S(2)}, u32[]{:S(2)}) collective-permute-start(f32[64,256]{1,0:T(8,128)S(1)} %get-tuple-element.25), channel_id=1, source_target_pairs={{0,1},{1,0},{2,3},{3,2},{4,5},{5,4},{6,7},{7,6},{8,9},{9,8},{10,11... | collective-permute-start | bytes 196616 | tf_op jit(solution)/shard_map/ppermute | solution.py:525
  53.0 6.9 %collective-permute-start.4 = (f32[64,256]{1,0:T(8,128)S(1)}, f32[64,256]{1,0:T(8,128)S(1)}, u32[]{:S(2)}, u32[]{:S(2)}) collective-permute-start(f32[64,256]{1,0:T(8,128)S(1)} %get-tuple-element.26), channel_id=1, source_target_pairs={{0,2},{1,3},{2,0},{3,1},{4,6},{5,7},{6,4},{7,5},{8,10},{9,11},{10,... | collective-permute-start | bytes 196616 | tf_op jit(solution)/shard_map/ppermute | solution.py:525
  54.6 5.6 %collective-permute-start.5 = (f32[64,256]{1,0:T(8,128)S(1)}, f32[64,256]{1,0:T(8,128)S(1)}, u32[]{:S(2)}, u32[]{:S(2)}) collective-permute-start(f32[64,256]{1,0:T(8,128)S(1)} %get-tuple-element.27), channel_id=1, source_target_pairs={{0,3},{1,2},{2,1},{3,0},{4,7},{5,6},{6,5},{7,4},{8,11},{9,10},{10,... | collective-permute-start | bytes 196616 | tf_op jit(solution)/shard_map/ppermute | solution.py:525

commit v10 on v9

--- a/solution.py
+++ b/solution.py
@@ -10,6 +10,7 @@
 
 BOX = 48
 CORE = 32
+FIRST = 8
 PLANE = BOX * BOX
 GROUPS = 6
 WIDE = PLANE // GROUPS
@@ -80,6 +81,10 @@
 
 def anywhere(count):
     return [pl.BlockSpec(memory_space=pl.ANY)] * count
+
+
+def by_distance(blocks):
+    return [((len(blocks) - n) % len(blocks), block) for n, block in enumerate(blocks)]
 
 
 def at_once(slots):
@@ -133,18 +138,19 @@
     ]
     for copy in scalars:
         copy.start()
-    chunks = BOX // CHUNK
+    chunks = (BOX - FIRST) // CHUNK
     copies = []
     for c in range(chunks):
-        part = pl.ds(c * CHUNK * PLANE, CHUNK * PLANE)
+        part = pl.ds((FIRST + c * CHUNK) * PLANE, CHUNK * PLANE)
+        room = pl.ds(c * CHUNK * PLANE, CHUNK * PLANE)
         copies.append(
-            pltpu.make_async_copy(orbitals.at[0, :, part], buffer.at[:, part], arrived.at[c])
+            pltpu.make_async_copy(orbitals.at[0, :, part], buffer.at[:, room], arrived.at[c])
         )
         copies[c].start()
     sub = lax.rem(own, len(blocks))
     fills = [
         pltpu.make_async_copy(outer.at[sub ^ d], block, filled.at[d])
-        for d, block in enumerate(blocks)
+        for d, block in by_distance(blocks)
     ]
     for fill in fills:
         fill.start()
@@ -173,7 +179,7 @@
             for q in range(tiles):
                 cells = []
                 for s in range(8):
-                    line = begin * GROUPS + (c * groups + b) * 8 + s
+                    line = (begin - FIRST) * GROUPS + (c * groups + b) * 8 + s
                     lane = pl.multiple_of(line * WIDE + q * LANES, LANES)
                     values = buffer[:, pl.ds(lane, LANES)].astype(jnp.float32)
                     values = values * values * weight
@@ -232,13 +238,13 @@
         in_specs=in_smem(1) + anywhere(5),
         out_specs=in_vmem(1 + outer.shape[0]),
         scratch_shapes=[
-            pltpu.VMEM((orbital_count, BOX * PLANE), orbitals.dtype),
+            pltpu.VMEM((orbital_count, (BOX - FIRST) * PLANE), orbitals.dtype),
             pltpu.VMEM((CORE * GROUPS, WIDE), jnp.float32),
             pltpu.VMEM((CORE * BOX + CORE, LANES), jnp.float32),
             pltpu.SMEM(corners.shape, jnp.int32),
             pltpu.SMEM(span.shape, jnp.int32),
             pltpu.SMEM(occupations.shape, jnp.int32),
-            pltpu.SemaphoreType.DMA((BOX // CHUNK,)),
+            pltpu.SemaphoreType.DMA(((BOX - FIRST) // CHUNK,)),
             pltpu.SemaphoreType.DMA((3,)),
             pltpu.SemaphoreType.DMA((outer.shape[0],)),
         ],
@@ -296,7 +302,7 @@
     *blocks, spectrum, exchange, outer = refs
     sub = lax.rem(device[0], len(blocks))
     x_dev = placed.shape[0] // len(blocks)
-    for d, block in enumerate(blocks):
+    for d, block in by_distance(blocks):
         outer[pl.ds(pl.multiple_of((sub ^ d) * x_dev, 8), x_dev), :] = block[...]
     density = outer[...] + placed[...]
     exchange[...] = exchange_correlation(density)
@@ -361,7 +367,7 @@
         wide[t * tall : t * tall + count_x, :] = part
         wide[t * tall + count_x : (t + 1) * tall, :] = part[0:BOX]
     sub = lax.rem(device[0], len(blocks))
-    for d, block in enumerate(blocks):
+    for d, block in by_distance(blocks):
         for t in range(tiles):
             at = pl.multiple_of(t * tall + (sub ^ d) * x_dev, 8)
             block[:, t * LANES : (t + 1) * LANES] = wide[pl.ds(at, x_dev), :]
@@ -425,7 +431,7 @@
     sub = lax.rem(device[0], len(blocks))
     copies = [
         pltpu.make_async_copy(block, potential.at[sub ^ d], copied.at[BOX + d])
-        for d, block in enumerate(blocks)
+        for d, block in by_distance(blocks)
     ]
     tall = len(blocks)
     over = lax.rem(first, tall)
@@ -523,7 +529,7 @@
     def swapped(blocks):
         return [
             lax.ppermute(block, "sub", [(i, i ^ d) for i in range(sub_count)]) if d else block
-            for d, block in enumerate(blocks)
+            for d, block in by_distance(blocks)
         ]
 
     pieces, *blocks = core_pieces(device, *arguments, slots, base, counts)

time: 65.9 us -> 66 us (level)
  no operation moved by 1% of the time
where the time goes in v10:
time: 66 us; the launch traced here: 65.7 us
  blocking collectives  26.2 us (40%)
  waiting for transfers between devices  15.9 us (24%)
  starting transfers between devices  13.8 us (21%)
  Pallas kernels  8.95 us (14%)
  between operations  0.75 us (1%)
    all_to_all x2, blocking collectives, body(): spectrum = lax.all_to_all(spectrum.reshape(chunk), AXES, 0, 0, tiled=True)  26.2 us
    all_to_all x2, starting transfers between devices, spread(): return lax.all_to_all(pieces, AXES, 0, 0, tiled=True)  9.94 us
    all_to_all x2, waiting for transfers between devices, spread(): return lax.all_to_all(pieces, AXES, 0, 0, tiled=True)  9.84 us
    ppermute x6, waiting for transfers between devices, swapped(): lax.ppermute(block, 'sub', [(i, i ^ d) for i in range(sub_count)])  6.09 us
    ppermute x6, starting transfers between devices, swapped(): lax.ppermute(block, 'sub', [(i, i ^ d) for i in range(sub_count)])  3.88 us
    pallas_call x1, Pallas kernels, core_pieces(): small_call(lambda *refs: core_kernel(base, *counts, *refs), 8, out_shape=...  3.54 us
    pallas_call x1, Pallas kernels, plane_windows(): small_call(lambda *refs: window_kernel(fragment, *refs), 12, out_shape=[b...  2.06 us
    pallas_call x1, Pallas kernels, outputs(): small_call(lambda *refs: output_kernel(base, *refs), 4, out_shape=(jax.Sh...  1.38 us
  transfers between devices with their start and end apart: 8, of which 4 were waited for; matrix products, arithmetic and copies ran while one was open for 0% of the time, Pallas kernels for 1%

profile of v10, /device:TPU:0, one launch (start us, length us, event | category | flops | bytes accessed | tf_op | source)
XLA Modules:
  0.0 65.7 jit_solution(3270483702882479176)
XLA Ops:
  0.6 0.0 copy-start
  0.6 0.0 copy-start.1
  0.7 0.0 copy-start.2
  0.7 3.5 %shard_map.95 = (f32[32,1,1152]{2,1,0:T(1,128)}, f32[64,256]{1,0:T(8,128)S(1)}, f32[64,256]{1,0:T(8,128)S(1)}, f32[64,256]{1,0:T(8,128)S(1)}, f32[64,256]{1,0:T(8,128)S(1)}) custom-call(s32[1]{0:T(128)} %bitcast.refs_0_.device, s32[3,32]{1,0:T(4,128)} %bitcast.11, s32[1,6]{1,0:T(1,128)} %refs_2_.2, s32[1,16]{1,0:T(1,128)} %refs_3_.1, ...), custom_call_target="tpu_custom_call" | custom-call | flops 40000000 | bytes 4000000 | tf_op jit(solution)/shard_map/pallas_call | solution.py:234
  4.2 7.3 %all-to-all-start = ((f32[32,1,1152]{2,1,0:T(1,128)}), f32[32,1,1152]{2,1,0:T(1,128)S(1)}, u32[]{:S(2)}, u32[]{:S(2)}) async-start(f32[32,1,1152]{2,1,0:T(1,128)} %get-tuple-element.16), calls=%async_computation | async-start | bytes 294912 | tf_op jit(solution)/shard_map/all_to_all | solution.py:494
  11.6 1.6 %collective-permute-start = (f32[64,256]{1,0:T(8,128)S(1)}, f32[64,256]{1,0:T(8,128)S(1)}, u32[]{:S(2)}, u32[]{:S(2)}) collective-permute-start(f32[64,256]{1,0:T(8,128)S(1)} %get-tuple-element.18), channel_id=1, source_target_pairs={{0,3},{1,2},{2,1},{3,0},{4,7},{5,6},{6,5},{7,4},{8,11},{9,10},{10,... | collective-permute-start | bytes 196616 | tf_op jit(solution)/shard_map/ppermute | solution.py:531
  13.1 0.4 collective-permute-start.1
  13.5 0.0 collective-permute-start.2
  13.5 6.5 %all-to-all-done.refs_0_ = f32[32,1,1152]{2,1,0:T(1,128)S(1)} async-done(((f32[32,1,1152]{2,1,0:T(1,128)}), f32[32,1,1152]{2,1,0:T(1,128)S(1)}, u32[]{:S(2)}, u32[]{:S(2)}) %all-to-all-start) | async-done | bytes 147488 | tf_op jit(solution)/shard_map/all_to_all | solution.py:494
  20.0 0.5 shard_map.96.placed
  20.5 0.0 collective-permute-done.refs_1_
  20.5 0.0 collective-permute-done.1.refs_2_
  20.5 0.0 collective-permute-done.2.refs_3_
  20.5 0.0 copy-done
  20.5 0.7 %shard_map.97 = (f32[256,256]{1,0:T(8,128)S(1)}, f32[256,256]{1,0:T(8,128)S(1)}) custom-call(s32[1]{0:T(128)} %bitcast.refs_0_.device, f32[256,256]{1,0:T(8,128)S(1)} %shard_map.96.placed, bf16[2,256,256]{2,1,0:T(8,128)(2,1)S(1)} %copy-done, bf16[2,256,256]{2,1,0:T(8,128)(2,1)S(1)} %copy-done, f32[64,256]{1,0:T(8,128)S(1)} %get-tuple-element.17.refs_0_, ...), custom_call_target="tpu_custom_call" | custom-call | tf_op jit(solution)/shard_map/pallas_call | solution.py:313
  21.3 13.5 %all_to_all.20 = f32[32,8,256]{2,1,0:T(8,128)S(1)} all-to-all(f32[32,8,256]{2,1,0:T(8,128)S(1)} %bitcast.10), channel_id=1, replica_groups=mesh['slab'=8,'sub'=4] {'slab','sub'}, dimensions={0} | all-to-all | bytes 524288 | tf_op jit(solution)/shard_map/all_to_all | solution.py:541
  34.7 0.0 copy-done.1
  34.7 0.7 %shard_map.98 = f32[256,256]{1,0:T(8,128)S(1)} custom-call(s32[1]{0:T(128)} %bitcast.refs_0_.device, f32[256,256]{1,0:T(8,128)S(1)} %bitcast.8, bf16[2,256,256]{2,1,0:T(8,128)(2,1)S(1)} %copy-done.1), custom_call_target="tpu_custom_call" | custom-call | tf_op jit(solution)/shard_map/pallas_call | solution.py:346
  35.5 12.8 %all_to_all.21 = f32[32,8,256]{2,1,0:T(8,128)S(1)} all-to-all(f32[32,8,256]{2,1,0:T(8,128)S(1)} %bitcast.9), channel_id=1, replica_groups=mesh['slab'=8,'sub'=4] {'slab','sub'}, dimensions={0} | all-to-all | bytes 524288 | tf_op jit(solution)/shard_map/all_to_all | solution.py:545
  48.2 0.0 copy-done.2
  48.2 2.1 %shard_map.99 = (f32[64,256]{1,0:T(8,128)S(1)}, f32[64,256]{1,0:T(8,128)S(1)}, f32[64,256]{1,0:T(8,128)S(1)}, f32[64,256]{1,0:T(8,128)S(1)}, f32[32,1,2304]{2,1,0:T(1,128)}) custom-call(s32[1]{0:T(128)} %bitcast.refs_0_.device, s32[3,32]{1,0:T(4,128)S(1)} %bitcast.12, f32[256,256]{1,0:T(8,128)S(1)} %bitcast.7, f32[256,256]{1,0:T(8,128)S(1)} %get-tuple-element.22.refs_3_, ...), custom_call_target="tpu_custom_call" | custom-call | tf_op jit(solution)/shard_map/pallas_call | solution.py:410
  50.3 2.6 %all-to-all-start.3 = ((f32[32,1,2304]{2,1,0:T(1,128)}), f32[32,1,2304]{2,1,0:T(1,128)S(1)}, u32[]{:S(2)}, u32[]{:S(2)}) async-start(f32[32,1,2304]{2,1,0:T(1,128)} %get-tuple-element.23), calls=%async_computation.3 | async-start | bytes 589824 | tf_op jit(solution)/shard_map/all_to_all | solution.py:494
  52.9 1.4 %collective-permute-start.3 = (f32[64,256]{1,0:T(8,128)S(1)}, f32[64,256]{1,0:T(8,128)S(1)}, u32[]{:S(2)}, u32[]{:S(2)}) collective-permute-start(f32[64,256]{1,0:T(8,128)S(1)} %get-tuple-element.25), channel_id=1, source_target_pairs={{0,3},{1,2},{2,1},{3,0},{4,7},{5,6},{6,5},{7,4},{8,11},{9,10},{10,... | collective-permute-start | bytes 196616 | tf_op jit(solution)/shard_map/ppermute | solution.py:531
  54.4 0.4 collective-permute-start.4
  54.7 0.1 collective-permute-start.5
  54.9 3.0 %collective-permute-done.3.refs_4_ = f32[64,256]{1,0:T(8,128)S(1)} collective-permute-done((f32[64,256]{1,0:T(8,128)S(1)}, f32[64,256]{1,0:T(8,128)S(1)}, u32[]{:S(2)}, u32[]{:S(2)}) %collective-permute-start.3) | collective-permute-done | bytes 65568 | tf_op jit(solution)/shard_map/ppermute | solution.py:531
  57.8 3.1 %collective-permute-done.4.refs_5_ = f32[64,256]{1,0:T(8,128)S(1)} collective-permute-done((f32[64,256]{1,0:T(8,128)S(1)}, f32[64,256]{1,0:T(8,128)S(1)}, u32[]{:S(2)}, u32[]{:S(2)}) %collective-permute-start.4) | collective-permute-done | bytes 65568 | tf_op jit(solution)/shard_map/ppermute | solution.py:531
  60.9 0.0 collective-permute-done.5.refs_6_
  60.9 3.4 %all-to-all-done.3.refs_2_ = f32[32,1,2304]{2,1,0:T(1,128)S(1)} async-done(((f32[32,1,2304]{2,1,0:T(1,128)}), f32[32,1,2304]{2,1,0:T(1,128)S(1)}, u32[]{:S(2)}, u32[]{:S(2)}) %all-to-all-start.3) | async-done | bytes 294944 | tf_op jit(solution)/shard_map/all_to_all | solution.py:494
  64.3 1.4 %shard_map.100 = (f32[48,1,2304]{2,1,0:T(1,128)}, f32[4,64,256]{2,1,0:T(8,128)}) custom-call(s32[1]{0:T(128)} %bitcast.refs_0_.device, s32[3,32]{1,0:T(4,128)S(1)} %bitcast.13, f32[32,1,2304]{2,1,0:T(1,128)S(1)} %all-to-all-done.3.refs_2_, f32[64,256]{1,0:T(8,128)S(1)} %get-tuple-element.24.refs_3_, f32[64,256]{1,0:T(8,128)S(1)} %collective-permute-done.3.refs_4_, ...), custom_call_target="tpu_custom_call" | custom-call | tf_op jit(solution)/shard_map/pallas_call | solution.py:454
Async XLA Ops:
  0.6 19.9 %copy-start = (bf16[2,256,256]{2,1,0:T(8,128)(2,1)S(1)}, bf16[2,256,256]{2,1,0:T(8,128)(2,1)}, u32[]{:S(2)}) copy-start(bf16[2,256,256]{2,1,0:T(8,128)(2,1)} %constant.15.clone.table_x.table_y.refs_4_.refs_5_) | copy-start | bytes 786436
  0.6 34.1 %copy-start.1 = (bf16[2,256,256]{2,1,0:T(8,128)(2,1)S(1)}, bf16[2,256,256]{2,1,0:T(8,128)(2,1)}, u32[]{:S(2)}) copy-start(bf16[2,256,256]{2,1,0:T(8,128)(2,1)} %constant.16.clone.refs_2_) | copy-start | bytes 786436
  0.7 47.6 %copy-start.2 = (s32[32,3]{0,1:T(4,128)S(1)}, s32[32,3]{0,1:T(4,128)}, u32[]{:S(2)}) copy-start(s32[32,3]{0,1:T(4,128)} %param.11) | copy-start | bytes 1156
  4.2 15.8 %all-to-all-start = ((f32[32,1,1152]{2,1,0:T(1,128)}), f32[32,1,1152]{2,1,0:T(1,128)S(1)}, u32[]{:S(2)}, u32[]{:S(2)}) async-start(f32[32,1,1152]{2,1,0:T(1,128)} %get-tuple-element.16), calls=%async_computation | async-start | bytes 294912 | tf_op jit(solution)/shard_map/all_to_all | solution.py:494
  11.6 8.9 %collective-permute-start = (f32[64,256]{1,0:T(8,128)S(1)}, f32[64,256]{1,0:T(8,128)S(1)}, u32[]{:S(2)}, u32[]{:S(2)}) collective-permute-start(f32[64,256]{1,0:T(8,128)S(1)} %get-tuple-element.18), channel_id=1, source_target_pairs={{0,3},{1,2},{2,1},{3,0},{4,7},{5,6},{6,5},{7,4},{8,11},{9,10},{10,... | collective-permute-start | bytes 196616 | tf_op jit(solution)/shard_map/ppermute | solution.py:531
  13.1 7.4 %collective-permute-start.1 = (f32[64,256]{1,0:T(8,128)S(1)}, f32[64,256]{1,0:T(8,128)S(1)}, u32[]{:S(2)}, u32[]{:S(2)}) collective-permute-start(f32[64,256]{1,0:T(8,128)S(1)} %get-tuple-element.19), channel_id=1, source_target_pairs={{0,2},{1,3},{2,0},{3,1},{4,6},{5,7},{6,4},{7,5},{8,10},{9,11},{10,... | collective-permute-start | bytes 196616 | tf_op jit(solution)/shard_map/ppermute | solution.py:531
  13.5 7.0 %collective-permute-start.2 = (f32[64,256]{1,0:T(8,128)S(1)}, f32[64,256]{1,0:T(8,128)S(1)}, u32[]{:S(2)}, u32[]{:S(2)}) collective-permute-start(f32[64,256]{1,0:T(8,128)S(1)} %get-tuple-element.20), channel_id=1, source_target_pairs={{0,1},{1,0},{2,3},{3,2},{4,5},{5,4},{6,7},{7,6},{8,9},{9,8},{10,11... | collective-permute-start | bytes 196616 | tf_op jit(solution)/shard_map/ppermute | solution.py:531
  50.3 14.0 %all-to-all-start.3 = ((f32[32,1,2304]{2,1,0:T(1,128)}), f32[32,1,2304]{2,1,0:T(1,128)S(1)}, u32[]{:S(2)}, u32[]{:S(2)}) async-start(f32[32,1,2304]{2,1,0:T(1,128)} %get-tuple-element.23), calls=%async_computation.3 | async-start | bytes 589824 | tf_op jit(solution)/shard_map/all_to_all | solution.py:494
  52.9 4.9 %collective-permute-start.3 = (f32[64,256]{1,0:T(8,128)S(1)}, f32[64,256]{1,0:T(8,128)S(1)}, u32[]{:S(2)}, u32[]{:S(2)}) collective-permute-start(f32[64,256]{1,0:T(8,128)S(1)} %get-tuple-element.25), channel_id=1, source_target_pairs={{0,3},{1,2},{2,1},{3,0},{4,7},{5,6},{6,5},{7,4},{8,11},{9,10},{10,... | collective-permute-start | bytes 196616 | tf_op jit(solution)/shard_map/ppermute | solution.py:531
  54.4 6.6 %collective-permute-start.4 = (f32[64,256]{1,0:T(8,128)S(1)}, f32[64,256]{1,0:T(8,128)S(1)}, u32[]{:S(2)}, u32[]{:S(2)}) collective-permute-start(f32[64,256]{1,0:T(8,128)S(1)} %get-tuple-element.26), channel_id=1, source_target_pairs={{0,2},{1,3},{2,0},{3,1},{4,6},{5,7},{6,4},{7,5},{8,10},{9,11},{10,... | collective-permute-start | bytes 196616 | tf_op jit(solution)/shard_map/ppermute | solution.py:531
  54.7 6.2 %collective-permute-start.5 = (f32[64,256]{1,0:T(8,128)S(1)}, f32[64,256]{1,0:T(8,128)S(1)}, u32[]{:S(2)}, u32[]{:S(2)}) collective-permute-start(f32[64,256]{1,0:T(8,128)S(1)} %get-tuple-element.27), channel_id=1, source_target_pairs={{0,1},{1,0},{2,3},{3,2},{4,5},{5,4},{6,7},{7,6},{8,9},{9,8},{10,11... | collective-permute-start | bytes 196616 | tf_op jit(solution)/shard_map/ppermute | solution.py:531

commit v11 on v10

--- a/solution.py
+++ b/solution.py
@@ -81,10 +81,6 @@
 
 def anywhere(count):
     return [pl.BlockSpec(memory_space=pl.ANY)] * count
-
-
-def by_distance(blocks):
-    return [((len(blocks) - n) % len(blocks), block) for n, block in enumerate(blocks)]
 
 
 def at_once(slots):
@@ -150,7 +146,7 @@
     sub = lax.rem(own, len(blocks))
     fills = [
         pltpu.make_async_copy(outer.at[sub ^ d], block, filled.at[d])
-        for d, block in by_distance(blocks)
+        for d, block in enumerate(blocks)
     ]
     for fill in fills:
         fill.start()
@@ -302,7 +298,7 @@
     *blocks, spectrum, exchange, outer = refs
     sub = lax.rem(device[0], len(blocks))
     x_dev = placed.shape[0] // len(blocks)
-    for d, block in by_distance(blocks):
+    for d, block in enumerate(blocks):
         outer[pl.ds(pl.multiple_of((sub ^ d) * x_dev, 8), x_dev), :] = block[...]
     density = outer[...] + placed[...]
     exchange[...] = exchange_correlation(density)
@@ -367,7 +363,7 @@
         wide[t * tall : t * tall + count_x, :] = part
         wide[t * tall + count_x : (t + 1) * tall, :] = part[0:BOX]
     sub = lax.rem(device[0], len(blocks))
-    for d, block in by_distance(blocks):
+    for d, block in enumerate(blocks):
         for t in range(tiles):
             at = pl.multiple_of(t * tall + (sub ^ d) * x_dev, 8)
             block[:, t * LANES : (t + 1) * LANES] = wide[pl.ds(at, x_dev), :]
@@ -431,7 +427,7 @@
     sub = lax.rem(device[0], len(blocks))
     copies = [
         pltpu.make_async_copy(block, potential.at[sub ^ d], copied.at[BOX + d])
-        for d, block in by_distance(blocks)
+        for d, block in enumerate(blocks)
     ]
     tall = len(blocks)
     over = lax.rem(first, tall)
@@ -529,7 +525,7 @@
     def swapped(blocks):
         return [
             lax.ppermute(block, "sub", [(i, i ^ d) for i in range(sub_count)]) if d else block
-            for d, block in by_distance(blocks)
+            for d, block in enumerate(blocks)
         ]
 
     pieces, *blocks = core_pieces(device, *arguments, slots, base, counts)

time: 66 us -> 65.7 us (level)
  no operation moved by 1% of the time
where the time goes in v11:
time: 65.7 us; the launch traced here: 65.4 us
  blocking collectives  25.9 us (39%)
  waiting for transfers between devices  16 us (24%)
  starting transfers between devices  13.8 us (21%)
  Pallas kernels  8.95 us (14%)
  between operations  0.75 us (1%)
    all_to_all x2, blocking collectives, body(): spectrum = lax.all_to_all(spectrum.reshape(chunk), AXES, 0, 0, tiled=True)  25.9 us
    all_to_all x2, waiting for transfers between devices, spread(): return lax.all_to_all(pieces, AXES, 0, 0, tiled=True)  10.4 us
    all_to_all x2, starting transfers between devices, spread(): return lax.all_to_all(pieces, AXES, 0, 0, tiled=True)  9.94 us
    ppermute x6, waiting for transfers between devices, swapped(): lax.ppermute(block, 'sub', [(i, i ^ d) for i in range(sub_count)])  5.53 us
    ppermute x6, starting transfers between devices, swapped(): lax.ppermute(block, 'sub', [(i, i ^ d) for i in range(sub_count)])  3.88 us
    pallas_call x1, Pallas kernels, core_pieces(): small_call(lambda *refs: core_kernel(base, *counts, *refs), 8, out_shape=...  3.54 us
    pallas_call x1, Pallas kernels, plane_windows(): small_call(lambda *refs: window_kernel(fragment, *refs), 12, out_shape=[b...  2.06 us
    pallas_call x1, Pallas kernels, outputs(): small_call(lambda *refs: output_kernel(base, *refs), 4, out_shape=(jax.Sh...  1.38 us
  transfers between devices with their start and end apart: 8, of which 4 were waited for; matrix products, arithmetic and copies ran while one was open for 0% of the time, Pallas kernels for 1%

profile of v11, /device:TPU:0, one launch (start us, length us, event | category | flops | bytes accessed | tf_op | source)
XLA Modules:
  0.0 65.4 jit_solution(11036034757103559580)
XLA Ops:
  0.6 0.0 copy-start
  0.6 0.0 copy-start.1
  0.7 0.0 copy-start.2
  0.7 3.5 %shard_map.95 = (f32[32,1,1152]{2,1,0:T(1,128)}, f32[64,256]{1,0:T(8,128)S(1)}, f32[64,256]{1,0:T(8,128)S(1)}, f32[64,256]{1,0:T(8,128)S(1)}, f32[64,256]{1,0:T(8,128)S(1)}) custom-call(s32[1]{0:T(128)} %bitcast.refs_0_.device, s32[3,32]{1,0:T(4,128)} %bitcast.11, s32[1,6]{1,0:T(1,128)} %refs_2_.2, s32[1,16]{1,0:T(1,128)} %refs_3_.1, ...), custom_call_target="tpu_custom_call" | custom-call | flops 40000000 | bytes 4000000 | tf_op jit(solution)/shard_map/pallas_call | solution.py:230
  4.2 7.3 %all-to-all-start = ((f32[32,1,1152]{2,1,0:T(1,128)}), f32[32,1,1152]{2,1,0:T(1,128)S(1)}, u32[]{:S(2)}, u32[]{:S(2)}) async-start(f32[32,1,1152]{2,1,0:T(1,128)} %get-tuple-element.16), calls=%async_computation | async-start | bytes 294912 | tf_op jit(solution)/shard_map/all_to_all | solution.py:490
  11.6 0.3 collective-permute-start
  11.9 1.6 %collective-permute-start.1 = (f32[64,256]{1,0:T(8,128)S(1)}, f32[64,256]{1,0:T(8,128)S(1)}, u32[]{:S(2)}, u32[]{:S(2)}) collective-permute-start(f32[64,256]{1,0:T(8,128)S(1)} %get-tuple-element.19), channel_id=1, source_target_pairs={{0,2},{1,3},{2,0},{3,1},{4,6},{5,7},{6,4},{7,5},{8,10},{9,11},{10,... | collective-permute-start | bytes 196616 | tf_op jit(solution)/shard_map/ppermute | solution.py:527
  13.5 0.0 collective-permute-start.2
  13.5 6.5 %all-to-all-done.refs_0_ = f32[32,1,1152]{2,1,0:T(1,128)S(1)} async-done(((f32[32,1,1152]{2,1,0:T(1,128)}), f32[32,1,1152]{2,1,0:T(1,128)S(1)}, u32[]{:S(2)}, u32[]{:S(2)}) %all-to-all-start) | async-done | bytes 147488 | tf_op jit(solution)/shard_map/all_to_all | solution.py:490
  20.0 0.5 shard_map.96.placed
  20.5 0.0 collective-permute-done.refs_1_
  20.5 0.0 collective-permute-done.1.refs_2_
  20.5 0.0 collective-permute-done.2.refs_3_
  20.6 0.0 copy-done
  20.6 0.7 %shard_map.97 = (f32[256,256]{1,0:T(8,128)S(1)}, f32[256,256]{1,0:T(8,128)S(1)}) custom-call(s32[1]{0:T(128)} %bitcast.refs_0_.device, f32[256,256]{1,0:T(8,128)S(1)} %shard_map.96.placed, bf16[2,256,256]{2,1,0:T(8,128)(2,1)S(1)} %copy-done, bf16[2,256,256]{2,1,0:T(8,128)(2,1)S(1)} %copy-done, f32[64,256]{1,0:T(8,128)S(1)} %get-tuple-element.17.refs_0_, ...), custom_call_target="tpu_custom_call" | custom-call | tf_op jit(solution)/shard_map/pallas_call | solution.py:309
  21.3 13.1 %all_to_all.20 = f32[32,8,256]{2,1,0:T(8,128)S(1)} all-to-all(f32[32,8,256]{2,1,0:T(8,128)S(1)} %bitcast.10), channel_id=1, replica_groups=mesh['slab'=8,'sub'=4] {'slab','sub'}, dimensions={0} | all-to-all | bytes 524288 | tf_op jit(solution)/shard_map/all_to_all | solution.py:537
  34.4 0.0 copy-done.1
  34.4 0.7 %shard_map.98 = f32[256,256]{1,0:T(8,128)S(1)} custom-call(s32[1]{0:T(128)} %bitcast.refs_0_.device, f32[256,256]{1,0:T(8,128)S(1)} %bitcast.8, bf16[2,256,256]{2,1,0:T(8,128)(2,1)S(1)} %copy-done.1), custom_call_target="tpu_custom_call" | custom-call | tf_op jit(solution)/shard_map/pallas_call | solution.py:342
  35.1 12.8 %all_to_all.21 = f32[32,8,256]{2,1,0:T(8,128)S(1)} all-to-all(f32[32,8,256]{2,1,0:T(8,128)S(1)} %bitcast.9), channel_id=1, replica_groups=mesh['slab'=8,'sub'=4] {'slab','sub'}, dimensions={0} | all-to-all | bytes 524288 | tf_op jit(solution)/shard_map/all_to_all | solution.py:541
  47.9 0.0 copy-done.2
  47.9 2.1 %shard_map.99 = (f32[64,256]{1,0:T(8,128)S(1)}, f32[64,256]{1,0:T(8,128)S(1)}, f32[64,256]{1,0:T(8,128)S(1)}, f32[64,256]{1,0:T(8,128)S(1)}, f32[32,1,2304]{2,1,0:T(1,128)}) custom-call(s32[1]{0:T(128)} %bitcast.refs_0_.device, s32[3,32]{1,0:T(4,128)S(1)} %bitcast.12, f32[256,256]{1,0:T(8,128)S(1)} %bitcast.7, f32[256,256]{1,0:T(8,128)S(1)} %get-tuple-element.22.refs_3_, ...), custom_call_target="tpu_custom_call" | custom-call | tf_op jit(solution)/shard_map/pallas_call | solution.py:406
  50.0 2.6 %all-to-all-start.3 = ((f32[32,1,2304]{2,1,0:T(1,128)}), f32[32,1,2304]{2,1,0:T(1,128)S(1)}, u32[]{:S(2)}, u32[]{:S(2)}) async-start(f32[32,1,2304]{2,1,0:T(1,128)} %get-tuple-element.23), calls=%async_computation.3 | async-start | bytes 589824 | tf_op jit(solution)/shard_map/all_to_all | solution.py:490
  52.6 0.2 collective-permute-start.3
  52.8 1.6 %collective-permute-start.4 = (f32[64,256]{1,0:T(8,128)S(1)}, f32[64,256]{1,0:T(8,128)S(1)}, u32[]{:S(2)}, u32[]{:S(2)}) collective-permute-start(f32[64,256]{1,0:T(8,128)S(1)} %get-tuple-element.26), channel_id=1, source_target_pairs={{0,2},{1,3},{2,0},{3,1},{4,6},{5,7},{6,4},{7,5},{8,10},{9,11},{10,... | collective-permute-start | bytes 196616 | tf_op jit(solution)/shard_map/ppermute | solution.py:527
  54.4 0.1 collective-permute-start.5
  54.5 0.0 collective-permute-done.3.refs_4_
  54.5 5.1 %collective-permute-done.4.refs_5_ = f32[64,256]{1,0:T(8,128)S(1)} collective-permute-done((f32[64,256]{1,0:T(8,128)S(1)}, f32[64,256]{1,0:T(8,128)S(1)}, u32[]{:S(2)}, u32[]{:S(2)}) %collective-permute-start.4) | collective-permute-done | bytes 65568 | tf_op jit(solution)/shard_map/ppermute | solution.py:527
  59.6 0.4 collective-permute-done.5.refs_6_
  60.0 3.9 %all-to-all-done.3.refs_2_ = f32[32,1,2304]{2,1,0:T(1,128)S(1)} async-done(((f32[32,1,2304]{2,1,0:T(1,128)}), f32[32,1,2304]{2,1,0:T(1,128)S(1)}, u32[]{:S(2)}, u32[]{:S(2)}) %all-to-all-start.3) | async-done | bytes 294944 | tf_op jit(solution)/shard_map/all_to_all | solution.py:490
  64.0 1.4 %shard_map.100 = (f32[48,1,2304]{2,1,0:T(1,128)}, f32[4,64,256]{2,1,0:T(8,128)}) custom-call(s32[1]{0:T(128)} %bitcast.refs_0_.device, s32[3,32]{1,0:T(4,128)S(1)} %bitcast.13, f32[32,1,2304]{2,1,0:T(1,128)S(1)} %all-to-all-done.3.refs_2_, f32[64,256]{1,0:T(8,128)S(1)} %get-tuple-element.24.refs_3_, f32[64,256]{1,0:T(8,128)S(1)} %collective-permute-done.3.refs_4_, ...), custom_call_target="tpu_custom_call" | custom-call | tf_op jit(solution)/shard_map/pallas_call | solution.py:450
Async XLA Ops:
  0.6 19.9 %copy-start = (bf16[2,256,256]{2,1,0:T(8,128)(2,1)S(1)}, bf16[2,256,256]{2,1,0:T(8,128)(2,1)}, u32[]{:S(2)}) copy-start(bf16[2,256,256]{2,1,0:T(8,128)(2,1)} %constant.15.clone.table_x.table_y.refs_4_.refs_5_) | copy-start | bytes 786436
  0.6 33.7 %copy-start.1 = (bf16[2,256,256]{2,1,0:T(8,128)(2,1)S(1)}, bf16[2,256,256]{2,1,0:T(8,128)(2,1)}, u32[]{:S(2)}) copy-start(bf16[2,256,256]{2,1,0:T(8,128)(2,1)} %constant.16.clone.refs_2_) | copy-start | bytes 786436
  0.7 47.3 %copy-start.2 = (s32[32,3]{0,1:T(4,128)S(1)}, s32[32,3]{0,1:T(4,128)}, u32[]{:S(2)}) copy-start(s32[32,3]{0,1:T(4,128)} %param.11) | copy-start | bytes 1156
  4.2 15.8 %all-to-all-start = ((f32[32,1,1152]{2,1,0:T(1,128)}), f32[32,1,1152]{2,1,0:T(1,128)S(1)}, u32[]{:S(2)}, u32[]{:S(2)}) async-start(f32[32,1,1152]{2,1,0:T(1,128)} %get-tuple-element.16), calls=%async_computation | async-start | bytes 294912 | tf_op jit(solution)/shard_map/all_to_all | solution.py:490
  11.6 9.0 %collective-permute-start = (f32[64,256]{1,0:T(8,128)S(1)}, f32[64,256]{1,0:T(8,128)S(1)}, u32[]{:S(2)}, u32[]{:S(2)}) collective-permute-start(f32[64,256]{1,0:T(8,128)S(1)} %get-tuple-element.18), channel_id=1, source_target_pairs={{0,1},{1,0},{2,3},{3,2},{4,5},{5,4},{6,7},{7,6},{8,9},{9,8},{10,11... | collective-permute-start | bytes 196616 | tf_op jit(solution)/shard_map/ppermute | solution.py:527
  11.9 8.7 %collective-permute-start.1 = (f32[64,256]{1,0:T(8,128)S(1)}, f32[64,256]{1,0:T(8,128)S(1)}, u32[]{:S(2)}, u32[]{:S(2)}) collective-permute-start(f32[64,256]{1,0:T(8,128)S(1)} %get-tuple-element.19), channel_id=1, source_target_pairs={{0,2},{1,3},{2,0},{3,1},{4,6},{5,7},{6,4},{7,5},{8,10},{9,11},{10,... | collective-permute-start | bytes 196616 | tf_op jit(solution)/shard_map/ppermute | solution.py:527
  13.5 7.0 %collective-permute-start.2 = (f32[64,256]{1,0:T(8,128)S(1)}, f32[64,256]{1,0:T(8,128)S(1)}, u32[]{:S(2)}, u32[]{:S(2)}) collective-permute-start(f32[64,256]{1,0:T(8,128)S(1)} %get-tuple-element.20), channel_id=1, source_target_pairs={{0,3},{1,2},{2,1},{3,0},{4,7},{5,6},{6,5},{7,4},{8,11},{9,10},{10,... | collective-permute-start | bytes 196616 | tf_op jit(solution)/shard_map/ppermute | solution.py:527
  50.0 14.0 %all-to-all-start.3 = ((f32[32,1,2304]{2,1,0:T(1,128)}), f32[32,1,2304]{2,1,0:T(1,128)S(1)}, u32[]{:S(2)}, u32[]{:S(2)}) async-start(f32[32,1,2304]{2,1,0:T(1,128)} %get-tuple-element.23), calls=%async_computation.3 | async-start | bytes 589824 | tf_op jit(solution)/shard_map/all_to_all | solution.py:490
  52.6 1.9 %collective-permute-start.3 = (f32[64,256]{1,0:T(8,128)S(1)}, f32[64,256]{1,0:T(8,128)S(1)}, u32[]{:S(2)}, u32[]{:S(2)}) collective-permute-start(f32[64,256]{1,0:T(8,128)S(1)} %get-tuple-element.25), channel_id=1, source_target_pairs={{0,1},{1,0},{2,3},{3,2},{4,5},{5,4},{6,7},{7,6},{8,9},{9,8},{10,11... | collective-permute-start | bytes 196616 | tf_op jit(solution)/shard_map/ppermute | solution.py:527
  52.8 6.9 %collective-permute-start.4 = (f32[64,256]{1,0:T(8,128)S(1)}, f32[64,256]{1,0:T(8,128)S(1)}, u32[]{:S(2)}, u32[]{:S(2)}) collective-permute-start(f32[64,256]{1,0:T(8,128)S(1)} %get-tuple-element.26), channel_id=1, source_target_pairs={{0,2},{1,3},{2,0},{3,1},{4,6},{5,7},{6,4},{7,5},{8,10},{9,11},{10,... | collective-permute-start | bytes 196616 | tf_op jit(solution)/shard_map/ppermute | solution.py:527
  54.4 5.6 %collective-permute-start.5 = (f32[64,256]{1,0:T(8,128)S(1)}, f32[64,256]{1,0:T(8,128)S(1)}, u32[]{:S(2)}, u32[]{:S(2)}) collective-permute-start(f32[64,256]{1,0:T(8,128)S(1)} %get-tuple-element.27), channel_id=1, source_target_pairs={{0,3},{1,2},{2,1},{3,0},{4,7},{5,6},{6,5},{7,4},{8,11},{9,10},{10,... | collective-permute-start | bytes 196616 | tf_op jit(solution)/shard_map/ppermute | solution.py:527

commit v12 on v11

--- a/solution.py
+++ b/solution.py
@@ -251,11 +251,11 @@
 def place_kernel(group, pieces, placed, packed):
     count_x, count_y = placed.shape
     groups = pieces.shape[0] // group
-    column = lax.broadcasted_iota(jnp.int32, (count_x, CORE), 1)
-    cell_x = lax.broadcasted_iota(jnp.int32, (count_x, CORE), 0)
     row = lax.broadcasted_iota(jnp.int32, (CORE, count_y), 0)
     cell_y = lax.broadcasted_iota(jnp.int32, (CORE, count_y), 1)
-    lefts, rights = [], []
+    lane = lax.broadcasted_iota(jnp.int32, (1, groups * CORE), 1)
+    first_x = jnp.zeros((1, groups * CORE), jnp.int32)
+    highs, lows = [], []
     for j in range(groups):
         total = pieces[j * group, :, 0:PACK]
         for m in range(1, group):
@@ -265,21 +265,18 @@
         tile = packed[8 * j : 8 * j + 8, :]
         square = jnp.concatenate([tile[:, 32 * q : 32 * q + 32] for q in range(4)], axis=0)
         first = pieces[j * group, :, PACK : PACK + LANES].astype(jnp.int32)
-        away_x = cell_x - first[:, 0:1]
-        away_y = cell_y - first[:, 1:2]
-        left = jnp.where(away_x < 0, away_x + count_x, away_x) == column
-        right = jnp.where(away_y < 0, away_y + count_y, away_y) == row
+        first_x = jnp.where(lane // CORE == j, first[:, 0:1], first_x)
+        away = cell_y - first[:, 1:2]
+        right = jnp.where(away < 0, away + count_y, away) == row
         right = jnp.where(right, 1.0, 0.0).astype(jnp.bfloat16)
-        high = square.astype(jnp.bfloat16)
-        rest = square - high.astype(jnp.float32)
-        middle = rest.astype(jnp.bfloat16)
-        low = (rest - middle.astype(jnp.float32)).astype(jnp.bfloat16)
-        lefts.append(jnp.where(left, 1.0, 0.0).astype(jnp.bfloat16))
-        rights.append([product(part, right).astype(jnp.bfloat16) for part in (high, middle, low)])
-    left = jnp.concatenate(lefts, axis=1)
-    total = product(left, jnp.concatenate([r[2] for r in rights], axis=0))
-    for part in (1, 0):
-        total = total + product(left, jnp.concatenate([r[part] for r in rights], axis=0))
+        high, low = parts(square)
+        highs.append(product(high, right).astype(jnp.bfloat16))
+        lows.append(product(low, right).astype(jnp.bfloat16))
+    away = lax.broadcasted_iota(jnp.int32, (count_x, groups * CORE), 0) - first_x
+    left = jnp.where(away < 0, away + count_x, away) == lane % CORE
+    left = jnp.where(left, 1.0, 0.0).astype(jnp.bfloat16)
+    total = product(left, jnp.concatenate(lows, axis=0))
+    total = total + product(left, jnp.concatenate(highs, axis=0))
     placed[...] = total
 
 
@@ -421,14 +418,17 @@
 def output_kernel(base, device, corners, windows, *refs):
     *blocks, box, potential, copied = refs
     depth = windows.shape[0]
+    sub = lax.rem(device[0], len(blocks))
+    first_copies = [
+        pltpu.make_async_copy(block, potential.at[sub ^ d], copied.at[BOX + d])
+        for d, block in enumerate(blocks)
+    ]
+    for copy in first_copies:
+        copy.start()
     row = corners[0:1, :]
     own = lax.broadcasted_iota(jnp.int32, row.shape, 1) == device[0]
     first = jnp.sum(jnp.where(own, row, 0)) - base(device[0])
-    sub = lax.rem(device[0], len(blocks))
-    copies = [
-        pltpu.make_async_copy(block, potential.at[sub ^ d], copied.at[BOX + d])
-        for d, block in enumerate(blocks)
-    ]
+    copies = []
     tall = len(blocks)
     over = lax.rem(first, tall)
     for t in range(1, BOX // tall):
@@ -441,7 +441,7 @@
         copies.append(pltpu.make_async_copy(windows.at[z], box.at[i], copied.at[BOX + tall + q]))
     for copy in copies:
         copy.start()
-    for copy in copies:
+    for copy in first_copies + copies:
         copy.wait()
 
 

time: 65.7 us -> 65.7 us (level)
  no operation moved by 1% of the time
where the time goes in v12:
time: 65.7 us; the launch traced here: 65.4 us
  blocking collectives  25.9 us (39%)
  waiting for transfers between devices  16 us (24%)
  starting transfers between devices  13.8 us (21%)
  Pallas kernels  8.88 us (14%)
  between operations  0.75 us (1%)
    all_to_all x2, blocking collectives, body(): spectrum = lax.all_to_all(spectrum.reshape(chunk), AXES, 0, 0, tiled=True)  25.9 us
    all_to_all x2, waiting for transfers between devices, spread(): return lax.all_to_all(pieces, AXES, 0, 0, tiled=True)  10.4 us
    all_to_all x2, starting transfers between devices, spread(): return lax.all_to_all(pieces, AXES, 0, 0, tiled=True)  9.94 us
    ppermute x6, waiting for transfers between devices, swapped(): lax.ppermute(block, 'sub', [(i, i ^ d) for i in range(sub_count)])  5.53 us
    ppermute x6, starting transfers between devices, swapped(): lax.ppermute(block, 'sub', [(i, i ^ d) for i in range(sub_count)])  3.88 us
    pallas_call x1, Pallas kernels, core_pieces(): small_call(lambda *refs: core_kernel(base, *counts, *refs), 8, out_shape=...  3.54 us
    pallas_call x1, Pallas kernels, plane_windows(): small_call(lambda *refs: window_kernel(fragment, *refs), 12, out_shape=[b...  2.06 us
    pallas_call x1, Pallas kernels, outputs(): small_call(lambda *refs: output_kernel(base, *refs), 4, out_shape=(jax.Sh...  1.38 us
  transfers between devices with their start and end apart: 8, of which 4 were waited for; matrix products, arithmetic and copies ran while one was open for 0% of the time, Pallas kernels for 1%

profile of v12, /device:TPU:0, one launch (start us, length us, event | category | flops | bytes accessed | tf_op | source)
XLA Modules:
  0.0 65.4 jit_solution(16317129399194046757)
XLA Ops:
  0.6 0.0 copy-start
  0.6 0.0 copy-start.1
  0.7 0.0 copy-start.2
  0.7 3.5 %shard_map.95 = (f32[32,1,1152]{2,1,0:T(1,128)}, f32[64,256]{1,0:T(8,128)S(1)}, f32[64,256]{1,0:T(8,128)S(1)}, f32[64,256]{1,0:T(8,128)S(1)}, f32[64,256]{1,0:T(8,128)S(1)}) custom-call(s32[1]{0:T(128)} %bitcast.refs_0_.device, s32[3,32]{1,0:T(4,128)} %bitcast.11, s32[1,6]{1,0:T(1,128)} %refs_2_.2, s32[1,16]{1,0:T(1,128)} %refs_3_.1, ...), custom_call_target="tpu_custom_call" | custom-call | flops 40000000 | bytes 4000000 | tf_op jit(solution)/shard_map/pallas_call | solution.py:230
  4.2 7.3 %all-to-all-start = ((f32[32,1,1152]{2,1,0:T(1,128)}), f32[32,1,1152]{2,1,0:T(1,128)S(1)}, u32[]{:S(2)}, u32[]{:S(2)}) async-start(f32[32,1,1152]{2,1,0:T(1,128)} %get-tuple-element.16), calls=%async_computation | async-start | bytes 294912 | tf_op jit(solution)/shard_map/all_to_all | solution.py:490
  11.6 0.3 collective-permute-start
  11.9 1.6 %collective-permute-start.1 = (f32[64,256]{1,0:T(8,128)S(1)}, f32[64,256]{1,0:T(8,128)S(1)}, u32[]{:S(2)}, u32[]{:S(2)}) collective-permute-start(f32[64,256]{1,0:T(8,128)S(1)} %get-tuple-element.19), channel_id=1, source_target_pairs={{0,2},{1,3},{2,0},{3,1},{4,6},{5,7},{6,4},{7,5},{8,10},{9,11},{10,... | collective-permute-start | bytes 196616 | tf_op jit(solution)/shard_map/ppermute | solution.py:527
  13.5 0.0 collective-permute-start.2
  13.5 6.5 %all-to-all-done.refs_0_ = f32[32,1,1152]{2,1,0:T(1,128)S(1)} async-done(((f32[32,1,1152]{2,1,0:T(1,128)}), f32[32,1,1152]{2,1,0:T(1,128)S(1)}, u32[]{:S(2)}, u32[]{:S(2)}) %all-to-all-start) | async-done | bytes 147488 | tf_op jit(solution)/shard_map/all_to_all | solution.py:490
  20.0 0.4 shard_map.96.placed
  20.5 0.0 collective-permute-done.refs_1_
  20.5 0.0 collective-permute-done.1.refs_2_
  20.5 0.0 collective-permute-done.2.refs_3_
  20.5 0.0 copy-done
  20.5 0.7 %shard_map.97 = (f32[256,256]{1,0:T(8,128)S(1)}, f32[256,256]{1,0:T(8,128)S(1)}) custom-call(s32[1]{0:T(128)} %bitcast.refs_0_.device, f32[256,256]{1,0:T(8,128)S(1)} %shard_map.96.placed, bf16[2,256,256]{2,1,0:T(8,128)(2,1)S(1)} %copy-done, bf16[2,256,256]{2,1,0:T(8,128)(2,1)S(1)} %copy-done, f32[64,256]{1,0:T(8,128)S(1)} %get-tuple-element.17.refs_0_, ...), custom_call_target="tpu_custom_call" | custom-call | tf_op jit(solution)/shard_map/pallas_call | solution.py:306
  21.2 13.2 %all_to_all.20 = f32[32,8,256]{2,1,0:T(8,128)S(1)} all-to-all(f32[32,8,256]{2,1,0:T(8,128)S(1)} %bitcast.10), channel_id=1, replica_groups=mesh['slab'=8,'sub'=4] {'slab','sub'}, dimensions={0} | all-to-all | bytes 524288 | tf_op jit(solution)/shard_map/all_to_all | solution.py:537
  34.4 0.0 copy-done.1
  34.4 0.7 %shard_map.98 = f32[256,256]{1,0:T(8,128)S(1)} custom-call(s32[1]{0:T(128)} %bitcast.refs_0_.device, f32[256,256]{1,0:T(8,128)S(1)} %bitcast.8, bf16[2,256,256]{2,1,0:T(8,128)(2,1)S(1)} %copy-done.1), custom_call_target="tpu_custom_call" | custom-call | tf_op jit(solution)/shard_map/pallas_call | solution.py:339
  35.1 12.8 %all_to_all.21 = f32[32,8,256]{2,1,0:T(8,128)S(1)} all-to-all(f32[32,8,256]{2,1,0:T(8,128)S(1)} %bitcast.9), channel_id=1, replica_groups=mesh['slab'=8,'sub'=4] {'slab','sub'}, dimensions={0} | all-to-all | bytes 524288 | tf_op jit(solution)/shard_map/all_to_all | solution.py:541
  47.9 0.0 copy-done.2
  47.9 2.1 %shard_map.99 = (f32[64,256]{1,0:T(8,128)S(1)}, f32[64,256]{1,0:T(8,128)S(1)}, f32[64,256]{1,0:T(8,128)S(1)}, f32[64,256]{1,0:T(8,128)S(1)}, f32[32,1,2304]{2,1,0:T(1,128)}) custom-call(s32[1]{0:T(128)} %bitcast.refs_0_.device, s32[3,32]{1,0:T(4,128)S(1)} %bitcast.12, f32[256,256]{1,0:T(8,128)S(1)} %bitcast.7, f32[256,256]{1,0:T(8,128)S(1)} %get-tuple-element.22.refs_3_, ...), custom_call_target="tpu_custom_call" | custom-call | tf_op jit(solution)/shard_map/pallas_call | solution.py:403
  50.0 2.6 %all-to-all-start.3 = ((f32[32,1,2304]{2,1,0:T(1,128)}), f32[32,1,2304]{2,1,0:T(1,128)S(1)}, u32[]{:S(2)}, u32[]{:S(2)}) async-start(f32[32,1,2304]{2,1,0:T(1,128)} %get-tuple-element.23), calls=%async_computation.3 | async-start | bytes 589824 | tf_op jit(solution)/shard_map/all_to_all | solution.py:490
  52.6 0.2 collective-permute-start.3
  52.8 1.6 %collective-permute-start.4 = (f32[64,256]{1,0:T(8,128)S(1)}, f32[64,256]{1,0:T(8,128)S(1)}, u32[]{:S(2)}, u32[]{:S(2)}) collective-permute-start(f32[64,256]{1,0:T(8,128)S(1)} %get-tuple-element.26), channel_id=1, source_target_pairs={{0,2},{1,3},{2,0},{3,1},{4,6},{5,7},{6,4},{7,5},{8,10},{9,11},{10,... | collective-permute-start | bytes 196616 | tf_op jit(solution)/shard_map/ppermute | solution.py:527
  54.4 0.1 collective-permute-start.5
  54.5 0.0 collective-permute-done.3.refs_4_
  54.5 5.1 %collective-permute-done.4.refs_5_ = f32[64,256]{1,0:T(8,128)S(1)} collective-permute-done((f32[64,256]{1,0:T(8,128)S(1)}, f32[64,256]{1,0:T(8,128)S(1)}, u32[]{:S(2)}, u32[]{:S(2)}) %collective-permute-start.4) | collective-permute-done | bytes 65568 | tf_op jit(solution)/shard_map/ppermute | solution.py:527
  59.6 0.4 collective-permute-done.5.refs_6_
  60.0 3.9 %all-to-all-done.3.refs_2_ = f32[32,1,2304]{2,1,0:T(1,128)S(1)} async-done(((f32[32,1,2304]{2,1,0:T(1,128)}), f32[32,1,2304]{2,1,0:T(1,128)S(1)}, u32[]{:S(2)}, u32[]{:S(2)}) %all-to-all-start.3) | async-done | bytes 294944 | tf_op jit(solution)/shard_map/all_to_all | solution.py:490
  64.0 1.4 %shard_map.100 = (f32[48,1,2304]{2,1,0:T(1,128)}, f32[4,64,256]{2,1,0:T(8,128)}) custom-call(s32[1]{0:T(128)} %bitcast.refs_0_.device, s32[3,32]{1,0:T(4,128)S(1)} %bitcast.13, f32[32,1,2304]{2,1,0:T(1,128)S(1)} %all-to-all-done.3.refs_2_, f32[64,256]{1,0:T(8,128)S(1)} %get-tuple-element.24.refs_3_, f32[64,256]{1,0:T(8,128)S(1)} %collective-permute-done.3.refs_4_, ...), custom_call_target="tpu_custom_call" | custom-call | tf_op jit(solution)/shard_map/pallas_call | solution.py:450
Async XLA Ops:
  0.6 19.9 %copy-start = (bf16[2,256,256]{2,1,0:T(8,128)(2,1)S(1)}, bf16[2,256,256]{2,1,0:T(8,128)(2,1)}, u32[]{:S(2)}) copy-start(bf16[2,256,256]{2,1,0:T(8,128)(2,1)} %constant.15.clone.table_x.table_y.refs_4_.refs_5_) | copy-start | bytes 786436
  0.6 33.7 %copy-start.1 = (bf16[2,256,256]{2,1,0:T(8,128)(2,1)S(1)}, bf16[2,256,256]{2,1,0:T(8,128)(2,1)}, u32[]{:S(2)}) copy-start(bf16[2,256,256]{2,1,0:T(8,128)(2,1)} %constant.16.clone.refs_2_) | copy-start | bytes 786436
  0.7 47.3 %copy-start.2 = (s32[32,3]{0,1:T(4,128)S(1)}, s32[32,3]{0,1:T(4,128)}, u32[]{:S(2)}) copy-start(s32[32,3]{0,1:T(4,128)} %param.11) | copy-start | bytes 1156
  4.2 15.8 %all-to-all-start = ((f32[32,1,1152]{2,1,0:T(1,128)}), f32[32,1,1152]{2,1,0:T(1,128)S(1)}, u32[]{:S(2)}, u32[]{:S(2)}) async-start(f32[32,1,1152]{2,1,0:T(1,128)} %get-tuple-element.16), calls=%async_computation | async-start | bytes 294912 | tf_op jit(solution)/shard_map/all_to_all | solution.py:490
  11.6 8.9 %collective-permute-start = (f32[64,256]{1,0:T(8,128)S(1)}, f32[64,256]{1,0:T(8,128)S(1)}, u32[]{:S(2)}, u32[]{:S(2)}) collective-permute-start(f32[64,256]{1,0:T(8,128)S(1)} %get-tuple-element.18), channel_id=1, source_target_pairs={{0,1},{1,0},{2,3},{3,2},{4,5},{5,4},{6,7},{7,6},{8,9},{9,8},{10,11... | collective-permute-start | bytes 196616 | tf_op jit(solution)/shard_map/ppermute | solution.py:527
  11.9 8.6 %collective-permute-start.1 = (f32[64,256]{1,0:T(8,128)S(1)}, f32[64,256]{1,0:T(8,128)S(1)}, u32[]{:S(2)}, u32[]{:S(2)}) collective-permute-start(f32[64,256]{1,0:T(8,128)S(1)} %get-tuple-element.19), channel_id=1, source_target_pairs={{0,2},{1,3},{2,0},{3,1},{4,6},{5,7},{6,4},{7,5},{8,10},{9,11},{10,... | collective-permute-start | bytes 196616 | tf_op jit(solution)/shard_map/ppermute | solution.py:527
  13.5 7.0 %collective-permute-start.2 = (f32[64,256]{1,0:T(8,128)S(1)}, f32[64,256]{1,0:T(8,128)S(1)}, u32[]{:S(2)}, u32[]{:S(2)}) collective-permute-start(f32[64,256]{1,0:T(8,128)S(1)} %get-tuple-element.20), channel_id=1, source_target_pairs={{0,3},{1,2},{2,1},{3,0},{4,7},{5,6},{6,5},{7,4},{8,11},{9,10},{10,... | collective-permute-start | bytes 196616 | tf_op jit(solution)/shard_map/ppermute | solution.py:527
  50.0 14.0 %all-to-all-start.3 = ((f32[32,1,2304]{2,1,0:T(1,128)}), f32[32,1,2304]{2,1,0:T(1,128)S(1)}, u32[]{:S(2)}, u32[]{:S(2)}) async-start(f32[32,1,2304]{2,1,0:T(1,128)} %get-tuple-element.23), calls=%async_computation.3 | async-start | bytes 589824 | tf_op jit(solution)/shard_map/all_to_all | solution.py:490
  52.6 1.9 %collective-permute-start.3 = (f32[64,256]{1,0:T(8,128)S(1)}, f32[64,256]{1,0:T(8,128)S(1)}, u32[]{:S(2)}, u32[]{:S(2)}) collective-permute-start(f32[64,256]{1,0:T(8,128)S(1)} %get-tuple-element.25), channel_id=1, source_target_pairs={{0,1},{1,0},{2,3},{3,2},{4,5},{5,4},{6,7},{7,6},{8,9},{9,8},{10,11... | collective-permute-start | bytes 196616 | tf_op jit(solution)/shard_map/ppermute | solution.py:527
  52.8 6.9 %collective-permute-start.4 = (f32[64,256]{1,0:T(8,128)S(1)}, f32[64,256]{1,0:T(8,128)S(1)}, u32[]{:S(2)}, u32[]{:S(2)}) collective-permute-start(f32[64,256]{1,0:T(8,128)S(1)} %get-tuple-element.26), channel_id=1, source_target_pairs={{0,2},{1,3},{2,0},{3,1},{4,6},{5,7},{6,4},{7,5},{8,10},{9,11},{10,... | collective-permute-start | bytes 196616 | tf_op jit(solution)/shard_map/ppermute | solution.py:527
  54.4 5.6 %collective-permute-start.5 = (f32[64,256]{1,0:T(8,128)S(1)}, f32[64,256]{1,0:T(8,128)S(1)}, u32[]{:S(2)}, u32[]{:S(2)}) collective-permute-start(f32[64,256]{1,0:T(8,128)S(1)} %get-tuple-element.27), channel_id=1, source_target_pairs={{0,3},{1,2},{2,1},{3,0},{4,7},{5,6},{6,5},{7,4},{8,11},{9,10},{10,... | collective-permute-start | bytes 196616 | tf_op jit(solution)/shard_map/ppermute | solution.py:527

commit v13 on v11

--- a/solution.py
+++ b/solution.py
@@ -418,18 +418,37 @@
     )(device, corners, spectrum, exchange, table_x, table_y)
 
 
-def output_kernel(base, device, corners, windows, *refs):
-    *blocks, box, potential, copied = refs
+def block_kernel(device, *refs):
+    *blocks, potential, copied = refs
+    sub = lax.rem(device[0], len(blocks))
+    copies = [
+        pltpu.make_async_copy(block, potential.at[sub ^ d], copied.at[d])
+        for d, block in enumerate(blocks)
+    ]
+    for copy in copies:
+        copy.start()
+    for copy in copies:
+        copy.wait()
+
+
+def grid_block(device, blocks):
+    count = len(blocks)
+    return small_call(
+        block_kernel,
+        4,
+        out_shape=jax.ShapeDtypeStruct((count,) + blocks[0].shape, jnp.float32),
+        in_specs=in_smem(1) + anywhere(count),
+        out_specs=anywhere(1)[0],
+        scratch_shapes=[pltpu.SemaphoreType.DMA((count,))],
+    )(device, *blocks)
+
+
+def output_kernel(base, tall, device, corners, windows, box, copied):
     depth = windows.shape[0]
     row = corners[0:1, :]
     own = lax.broadcasted_iota(jnp.int32, row.shape, 1) == device[0]
     first = jnp.sum(jnp.where(own, row, 0)) - base(device[0])
-    sub = lax.rem(device[0], len(blocks))
-    copies = [
-        pltpu.make_async_copy(block, potential.at[sub ^ d], copied.at[BOX + d])
-        for d, block in enumerate(blocks)
-    ]
-    tall = len(blocks)
+    copies = []
     over = lax.rem(first, tall)
     for t in range(1, BOX // tall):
         z = pl.ds(lax.rem(first - over + t * tall, depth), tall)
@@ -445,19 +464,15 @@
         copy.wait()
 
 
-def outputs(device, corners, windows, blocks, base):
-    count = len(blocks)
-    return small_call(
-        lambda *refs: output_kernel(base, *refs),
+def box_planes(device, corners, windows, tall, base):
+    return small_call(
+        lambda *refs: output_kernel(base, tall, *refs),
         4,
-        out_shape=(
-            jax.ShapeDtypeStruct((BOX, 1, PLANE), jnp.float32),
-            jax.ShapeDtypeStruct((count,) + blocks[0].shape, jnp.float32),
-        ),
-        in_specs=in_smem(1) + in_vmem(1) + anywhere(1 + count),
-        out_specs=tuple(anywhere(2)),
-        scratch_shapes=[pltpu.SemaphoreType.DMA((BOX + 2 * count,))],
-    )(device, corners, windows, *blocks)
+        out_shape=jax.ShapeDtypeStruct((BOX, 1, PLANE), jnp.float32),
+        in_specs=in_smem(1) + in_vmem(1) + anywhere(1),
+        out_specs=anywhere(1)[0],
+        scratch_shapes=[pltpu.SemaphoreType.DMA((BOX + 2 * tall,))],
+    )(device, corners, windows)
 
 
 def body(orbitals, occupations, patch_sign, corners, core_span, outer_density):
@@ -552,7 +567,8 @@
     )
     blocks = swapped(blocks)
     windows = collect(windows)
-    box, potential = outputs(device, corners, windows, blocks, base)
+    potential = grid_block(device, blocks)
+    box = box_planes(device, corners, windows, z_dev, base)
     return (box.reshape(1, BOX * PLANE), potential)
 
 

time: 65.7 us -> 65.7 us (level)
  waiting for transfers between devices: 16 us -> 15.2 us
  Pallas kernels: 8.95 us -> 9.67 us
    all_to_all x2, waiting for transfers between devices: 10.4 us -> 9.71 us  [spread(): return lax.all_to_all(pieces, AXES, 0, 0, tiled=True)]
    pallas_call x1 -> x2, Pallas kernels: 1.38 us -> 2.1 us  [the longest x1 1.38 us: box_planes(): small_call(lambda *refs: output_kernel(base, tall, *refs), 4, out_shape=j...]
  transfers between devices with their start and end apart: 8 -> 8, of which waited for: 4 -> 4; matrix products, arithmetic and copies ran while one was open for 0% -> 0% of each run, Pallas kernels for 1% -> 2%
where the time goes in v13:
time: 65.7 us; the launch traced here: 65.4 us
  blocking collectives  25.9 us (39%)
  waiting for transfers between devices  15.2 us (23%)
  starting transfers between devices  13.8 us (21%)
  Pallas kernels  9.67 us (15%)
  between operations  0.76 us (1%)
    all_to_all x2, blocking collectives, body(): spectrum = lax.all_to_all(spectrum.reshape(chunk), AXES, 0, 0, tiled=True)  25.9 us
    all_to_all x2, starting transfers between devices, spread(): return lax.all_to_all(pieces, AXES, 0, 0, tiled=True)  9.94 us
    all_to_all x2, waiting for transfers between devices, spread(): return lax.all_to_all(pieces, AXES, 0, 0, tiled=True)  9.71 us
    ppermute x6, waiting for transfers between devices, swapped(): lax.ppermute(block, 'sub', [(i, i ^ d) for i in range(sub_count)])  5.53 us
    ppermute x6, starting transfers between devices, swapped(): lax.ppermute(block, 'sub', [(i, i ^ d) for i in range(sub_count)])  3.88 us
    pallas_call x1, Pallas kernels, core_pieces(): small_call(lambda *refs: core_kernel(base, *counts, *refs), 8, out_shape=...  3.54 us
    pallas_call x1, Pallas kernels, plane_windows(): small_call(lambda *refs: window_kernel(fragment, *refs), 12, out_shape=[b...  2.06 us
    pallas_call x1, Pallas kernels, box_planes(): small_call(lambda *refs: output_kernel(base, tall, *refs), 4, out_shape=j...  1.38 us
  transfers between devices with their start and end apart: 8, of which 4 were waited for; matrix products, arithmetic and copies ran while one was open for 0% of the time, Pallas kernels for 2%

profile of v13, /device:TPU:0, one launch (start us, length us, event | category | flops | bytes accessed | tf_op | source)
XLA Modules:
  0.0 65.4 jit_solution(8409752710714223143)
XLA Ops:
  0.6 0.0 copy-start
  0.6 0.0 copy-start.1
  0.7 0.0 copy-start.2
  0.7 3.5 %shard_map.95 = (f32[32,1,1152]{2,1,0:T(1,128)}, f32[64,256]{1,0:T(8,128)S(1)}, f32[64,256]{1,0:T(8,128)S(1)}, f32[64,256]{1,0:T(8,128)S(1)}, f32[64,256]{1,0:T(8,128)S(1)}) custom-call(s32[1]{0:T(128)} %bitcast.refs_0_.device, s32[3,32]{1,0:T(4,128)} %bitcast.11, s32[1,6]{1,0:T(1,128)} %refs_2_.2, s32[1,16]{1,0:T(1,128)} %refs_3_.1, ...), custom_call_target="tpu_custom_call" | custom-call | flops 40000000 | bytes 4000000 | tf_op jit(solution)/shard_map/pallas_call | solution.py:230
  4.2 7.3 %all-to-all-start = ((f32[32,1,1152]{2,1,0:T(1,128)}), f32[32,1,1152]{2,1,0:T(1,128)S(1)}, u32[]{:S(2)}, u32[]{:S(2)}) async-start(f32[32,1,1152]{2,1,0:T(1,128)} %get-tuple-element.14), calls=%async_computation | async-start | bytes 294912 | tf_op jit(solution)/shard_map/all_to_all | solution.py:505
  11.6 0.3 collective-permute-start
  11.9 1.6 %collective-permute-start.1 = (f32[64,256]{1,0:T(8,128)S(1)}, f32[64,256]{1,0:T(8,128)S(1)}, u32[]{:S(2)}, u32[]{:S(2)}) collective-permute-start(f32[64,256]{1,0:T(8,128)S(1)} %get-tuple-element.17), channel_id=1, source_target_pairs={{0,2},{1,3},{2,0},{3,1},{4,6},{5,7},{6,4},{7,5},{8,10},{9,11},{10,... | collective-permute-start | bytes 196616 | tf_op jit(solution)/shard_map/ppermute | solution.py:542
  13.5 0.0 collective-permute-start.2
  13.5 6.5 %all-to-all-done.refs_0_ = f32[32,1,1152]{2,1,0:T(1,128)S(1)} async-done(((f32[32,1,1152]{2,1,0:T(1,128)}), f32[32,1,1152]{2,1,0:T(1,128)S(1)}, u32[]{:S(2)}, u32[]{:S(2)}) %all-to-all-start) | async-done | bytes 147488 | tf_op jit(solution)/shard_map/all_to_all | solution.py:505
  20.0 0.5 shard_map.96.placed
  20.5 0.0 collective-permute-done.refs_1_
  20.5 0.0 collective-permute-done.1.refs_2_
  20.5 0.0 collective-permute-done.2.refs_3_
  20.6 0.0 copy-done
  20.6 0.7 %shard_map.97 = (f32[256,256]{1,0:T(8,128)S(1)}, f32[256,256]{1,0:T(8,128)S(1)}) custom-call(s32[1]{0:T(128)} %bitcast.refs_0_.device, f32[256,256]{1,0:T(8,128)S(1)} %shard_map.96.placed, bf16[2,256,256]{2,1,0:T(8,128)(2,1)S(1)} %copy-done, bf16[2,256,256]{2,1,0:T(8,128)(2,1)S(1)} %copy-done, f32[64,256]{1,0:T(8,128)S(1)} %get-tuple-element.15.refs_0_, ...), custom_call_target="tpu_custom_call" | custom-call | tf_op jit(solution)/shard_map/pallas_call | solution.py:309
  21.3 13.1 %all_to_all.20 = f32[32,8,256]{2,1,0:T(8,128)S(1)} all-to-all(f32[32,8,256]{2,1,0:T(8,128)S(1)} %bitcast.10), channel_id=1, replica_groups=mesh['slab'=8,'sub'=4] {'slab','sub'}, dimensions={0} | all-to-all | bytes 524288 | tf_op jit(solution)/shard_map/all_to_all | solution.py:552
  34.4 0.0 copy-done.1
  34.4 0.7 %shard_map.98 = f32[256,256]{1,0:T(8,128)S(1)} custom-call(s32[1]{0:T(128)} %bitcast.refs_0_.device, f32[256,256]{1,0:T(8,128)S(1)} %bitcast.8, bf16[2,256,256]{2,1,0:T(8,128)(2,1)S(1)} %copy-done.1), custom_call_target="tpu_custom_call" | custom-call | tf_op jit(solution)/shard_map/pallas_call | solution.py:342
  35.1 12.8 %all_to_all.21 = f32[32,8,256]{2,1,0:T(8,128)S(1)} all-to-all(f32[32,8,256]{2,1,0:T(8,128)S(1)} %bitcast.9), channel_id=1, replica_groups=mesh['slab'=8,'sub'=4] {'slab','sub'}, dimensions={0} | all-to-all | bytes 524288 | tf_op jit(solution)/shard_map/all_to_all | solution.py:556
  47.9 0.0 copy-done.2
  47.9 2.1 %shard_map.99 = (f32[64,256]{1,0:T(8,128)S(1)}, f32[64,256]{1,0:T(8,128)S(1)}, f32[64,256]{1,0:T(8,128)S(1)}, f32[64,256]{1,0:T(8,128)S(1)}, f32[32,1,2304]{2,1,0:T(1,128)}) custom-call(s32[1]{0:T(128)} %bitcast.refs_0_.device, s32[3,32]{1,0:T(4,128)S(1)} %bitcast.12, f32[256,256]{1,0:T(8,128)S(1)} %bitcast.7, f32[256,256]{1,0:T(8,128)S(1)} %get-tuple-element.20.refs_3_, ...), custom_call_target="tpu_custom_call" | custom-call | tf_op jit(solution)/shard_map/pallas_call | solution.py:406
  50.0 2.6 %all-to-all-start.3 = ((f32[32,1,2304]{2,1,0:T(1,128)}), f32[32,1,2304]{2,1,0:T(1,128)S(1)}, u32[]{:S(2)}, u32[]{:S(2)}) async-start(f32[32,1,2304]{2,1,0:T(1,128)} %get-tuple-element.21), calls=%async_computation.3 | async-start | bytes 589824 | tf_op jit(solution)/shard_map/all_to_all | solution.py:505
  52.6 0.2 collective-permute-start.3
  52.8 1.6 %collective-permute-start.4 = (f32[64,256]{1,0:T(8,128)S(1)}, f32[64,256]{1,0:T(8,128)S(1)}, u32[]{:S(2)}, u32[]{:S(2)}) collective-permute-start(f32[64,256]{1,0:T(8,128)S(1)} %get-tuple-element.24), channel_id=1, source_target_pairs={{0,2},{1,3},{2,0},{3,1},{4,6},{5,7},{6,4},{7,5},{8,10},{9,11},{10,... | collective-permute-start | bytes 196616 | tf_op jit(solution)/shard_map/ppermute | solution.py:542
  54.4 0.1 collective-permute-start.5
  54.5 0.0 collective-permute-done.3.refs_1_
  54.5 5.1 %collective-permute-done.4.refs_2_ = f32[64,256]{1,0:T(8,128)S(1)} collective-permute-done((f32[64,256]{1,0:T(8,128)S(1)}, f32[64,256]{1,0:T(8,128)S(1)}, u32[]{:S(2)}, u32[]{:S(2)}) %collective-permute-start.4) | collective-permute-done | bytes 65568 | tf_op jit(solution)/shard_map/ppermute | solution.py:542
  59.6 0.4 collective-permute-done.5.refs_3_
  60.0 0.7 %shard_map.101 = f32[4,64,256]{2,1,0:T(8,128)} custom-call(s32[1]{0:T(128)} %bitcast.refs_0_.device, f32[64,256]{1,0:T(8,128)S(1)} %get-tuple-element.22.refs_0_, f32[64,256]{1,0:T(8,128)S(1)} %collective-permute-done.3.refs_1_, f32[64,256]{1,0:T(8,128)S(1)} %collective-permute-done.4.refs_2_, f32[64,256]{1,0:T(8,128)S(1)} %collective-permute-done.5.refs_3_), custom_call_target="tpu_custom_call" | custom-call | tf_op jit(solution)/shard_map/pallas_call | solution.py:436
  60.8 3.2 %all-to-all-done.3.refs_2_ = f32[32,1,2304]{2,1,0:T(1,128)S(1)} async-done(((f32[32,1,2304]{2,1,0:T(1,128)}), f32[32,1,2304]{2,1,0:T(1,128)S(1)}, u32[]{:S(2)}, u32[]{:S(2)}) %all-to-all-start.3) | async-done | bytes 294944 | tf_op jit(solution)/shard_map/all_to_all | solution.py:505
  64.0 1.4 %shard_map.100 = f32[48,1,2304]{2,1,0:T(1,128)} custom-call(s32[1]{0:T(128)} %bitcast.refs_0_.device, s32[3,32]{1,0:T(4,128)S(1)} %bitcast.13, f32[32,1,2304]{2,1,0:T(1,128)S(1)} %all-to-all-done.3.refs_2_), custom_call_target="tpu_custom_call" | custom-call | tf_op jit(solution)/shard_map/pallas_call | solution.py:468
Async XLA Ops:
  0.6 19.9 %copy-start = (bf16[2,256,256]{2,1,0:T(8,128)(2,1)S(1)}, bf16[2,256,256]{2,1,0:T(8,128)(2,1)}, u32[]{:S(2)}) copy-start(bf16[2,256,256]{2,1,0:T(8,128)(2,1)} %constant.15.clone.table_x.table_y.refs_4_.refs_5_) | copy-start | bytes 786436
  0.6 33.7 %copy-start.1 = (bf16[2,256,256]{2,1,0:T(8,128)(2,1)S(1)}, bf16[2,256,256]{2,1,0:T(8,128)(2,1)}, u32[]{:S(2)}) copy-start(bf16[2,256,256]{2,1,0:T(8,128)(2,1)} %constant.16.clone.refs_2_) | copy-start | bytes 786436
  0.7 47.3 %copy-start.2 = (s32[32,3]{0,1:T(4,128)S(1)}, s32[32,3]{0,1:T(4,128)}, u32[]{:S(2)}) copy-start(s32[32,3]{0,1:T(4,128)} %param.11) | copy-start | bytes 1156
  4.2 15.8 %all-to-all-start = ((f32[32,1,1152]{2,1,0:T(1,128)}), f32[32,1,1152]{2,1,0:T(1,128)S(1)}, u32[]{:S(2)}, u32[]{:S(2)}) async-start(f32[32,1,1152]{2,1,0:T(1,128)} %get-tuple-element.14), calls=%async_computation | async-start | bytes 294912 | tf_op jit(solution)/shard_map/all_to_all | solution.py:505
  11.6 9.0 %collective-permute-start = (f32[64,256]{1,0:T(8,128)S(1)}, f32[64,256]{1,0:T(8,128)S(1)}, u32[]{:S(2)}, u32[]{:S(2)}) collective-permute-start(f32[64,256]{1,0:T(8,128)S(1)} %get-tuple-element.16), channel_id=1, source_target_pairs={{0,1},{1,0},{2,3},{3,2},{4,5},{5,4},{6,7},{7,6},{8,9},{9,8},{10,11... | collective-permute-start | bytes 196616 | tf_op jit(solution)/shard_map/ppermute | solution.py:542
  11.9 8.7 %collective-permute-start.1 = (f32[64,256]{1,0:T(8,128)S(1)}, f32[64,256]{1,0:T(8,128)S(1)}, u32[]{:S(2)}, u32[]{:S(2)}) collective-permute-start(f32[64,256]{1,0:T(8,128)S(1)} %get-tuple-element.17), channel_id=1, source_target_pairs={{0,2},{1,3},{2,0},{3,1},{4,6},{5,7},{6,4},{7,5},{8,10},{9,11},{10,... | collective-permute-start | bytes 196616 | tf_op jit(solution)/shard_map/ppermute | solution.py:542
  13.5 7.0 %collective-permute-start.2 = (f32[64,256]{1,0:T(8,128)S(1)}, f32[64,256]{1,0:T(8,128)S(1)}, u32[]{:S(2)}, u32[]{:S(2)}) collective-permute-start(f32[64,256]{1,0:T(8,128)S(1)} %get-tuple-element.18), channel_id=1, source_target_pairs={{0,3},{1,2},{2,1},{3,0},{4,7},{5,6},{6,5},{7,4},{8,11},{9,10},{10,... | collective-permute-start | bytes 196616 | tf_op jit(solution)/shard_map/ppermute | solution.py:542
  50.0 14.0 %all-to-all-start.3 = ((f32[32,1,2304]{2,1,0:T(1,128)}), f32[32,1,2304]{2,1,0:T(1,128)S(1)}, u32[]{:S(2)}, u32[]{:S(2)}) async-start(f32[32,1,2304]{2,1,0:T(1,128)} %get-tuple-element.21), calls=%async_computation.3 | async-start | bytes 589824 | tf_op jit(solution)/shard_map/all_to_all | solution.py:505
  52.6 1.9 %collective-permute-start.3 = (f32[64,256]{1,0:T(8,128)S(1)}, f32[64,256]{1,0:T(8,128)S(1)}, u32[]{:S(2)}, u32[]{:S(2)}) collective-permute-start(f32[64,256]{1,0:T(8,128)S(1)} %get-tuple-element.23), channel_id=1, source_target_pairs={{0,1},{1,0},{2,3},{3,2},{4,5},{5,4},{6,7},{7,6},{8,9},{9,8},{10,11... | collective-permute-start | bytes 196616 | tf_op jit(solution)/shard_map/ppermute | solution.py:542
  52.8 6.9 %collective-permute-start.4 = (f32[64,256]{1,0:T(8,128)S(1)}, f32[64,256]{1,0:T(8,128)S(1)}, u32[]{:S(2)}, u32[]{:S(2)}) collective-permute-start(f32[64,256]{1,0:T(8,128)S(1)} %get-tuple-element.24), channel_id=1, source_target_pairs={{0,2},{1,3},{2,0},{3,1},{4,6},{5,7},{6,4},{7,5},{8,10},{9,11},{10,... | collective-permute-start | bytes 196616 | tf_op jit(solution)/shard_map/ppermute | solution.py:542
  54.4 5.6 %collective-permute-start.5 = (f32[64,256]{1,0:T(8,128)S(1)}, f32[64,256]{1,0:T(8,128)S(1)}, u32[]{:S(2)}, u32[]{:S(2)}) collective-permute-start(f32[64,256]{1,0:T(8,128)S(1)} %get-tuple-element.25), channel_id=1, source_target_pairs={{0,3},{1,2},{2,1},{3,0},{4,7},{5,6},{6,5},{7,4},{8,11},{9,10},{10,... | collective-permute-start | bytes 196616 | tf_op jit(solution)/shard_map/ppermute | solution.py:542
